TPU v7x, 256 devices: a whole 4x4x8 slice. The times are simulated.
256 devices in a mesh: section: 2 (over x_hi), row: 8 (over y, x_lo), col: 16 (over z, core).
Axes of the slice: x: 4 (x_hi: 2, x_lo: 2; x = x_hi * 2 + x_lo), y: 4, z: 8, core: 2. Of those that a mesh axis runs over, the one named last changes fastest.
Arguments:
- images: bfloat16 [2, 8, 48, 128, 256], P('section', None, None, 'row', 'col'), may hold values from -6 to 6
- stem_first: bfloat16 [48, 256], replicated, may hold values from -0.875 to 0.875
- stem_conv: bfloat16 [3, 3, 256, 256], replicated, may hold values from -0.125 to 0.125
- patch_weight: bfloat16 [4096, 1024], P('col'), may hold values from -0.09375 to 0.09375
- position: bfloat16 [64, 32, 1024], P('col', 'row'), may hold values from -6 to 6
- gain_attn: float32 [1024], replicated, may hold values from 0.1 to 1.9
- w_qkv: bfloat16 [3, 1024, 1024], P(None, None, 'col'), may hold values from -0.5 to 0.5
- w_out: bfloat16 [1024, 1024], P('col'), may hold values from -0.1875 to 0.1875
- gain_mlp: float32 [1024], replicated, may hold values from 0.1 to 1.9
- w_up: bfloat16 [1024, 4096], P(None, 'col'), may hold values from -0.1875 to 0.1875
- w_down: bfloat16 [4096, 1024], P('col'), may hold values from -0.09375 to 0.09375
Outputs:
- encoded: bfloat16 [2, 8, 64, 32, 1024], P('section', 'row', 'col')
All inputs are finite; a program needn't handle non-finite values.
Results may differ from a plain program's by a relative error of at most 0.024.
The roundings to bfloat16 on the way count: a program that leaves them out, or rounds other values in their place, can miss the bound.
Values may be sent and summed in bfloat16 or wider, within the bound.
No kernel may reach another device: no remote copies, remote signals or barrier semaphores. Data moves between devices by JAX's collectives and lax.ppermute only.
A program may use at most 64 MiB of HBM per device.

v0:
```python
import functools

import jax
import jax.numpy as jnp
from jax import lax
from jax.experimental import pallas as pl
from jax.experimental.pallas import tpu as pltpu
from jax.sharding import PartitionSpec as P

HD = 64
TEAM = 4
PAIR = 2


def cost(flops):
    return pl.CostEstimate(flops=flops, bytes_accessed=flops // 256, transcendentals=0)


VMEM = pl.BlockSpec(memory_space=pltpu.VMEM)
HBM = pl.BlockSpec(memory_space=pltpu.HBM)


def layer_norm(vectors, gain_vec):
    row_mean = jnp.mean(vectors, axis=-1, keepdims=True)
    center = vectors - row_mean
    spread = jnp.mean(center * center, axis=-1, keepdims=True)
    return center * lax.rsqrt(spread + 1e-06) * gain_vec


def image_strips(images, position):
    sections = lax.axis_size("section")
    rows = lax.axis_size("row")
    pixels = images[0]
    img_count, colours, height, width = pixels.shape
    tile = height * width
    cols_here, rows_here, model_width = position.shape
    pixels = pixels.reshape(img_count // PAIR, 1, PAIR * colours, tile)
    pixels = jnp.broadcast_to(pixels, (img_count // PAIR, PAIR, PAIR * colours, tile))
    pixels = pixels.reshape(img_count, PAIR * colours, tile)
    place = position.reshape(cols_here * rows_here, model_width // tile, tile)
    place = place.transpose(1, 0, 2).reshape(-1, tile)
    place_rows = place.shape[0]
    slot_rows = PAIR * colours
    place = jnp.pad(place, ((0, slot_rows - place_rows), (0, 0)))
    here = lax.axis_index("section")
    slots = lax.broadcasted_iota(jnp.int32, (sections, 1, 1, 1), 0)
    outgoing = jnp.where(slots == here, place[None, None], pixels[None])
    outgoing = outgoing.reshape(sections * rows, slot_rows, tile)
    incoming = lax.all_to_all(outgoing, ("section", "row"), 0, 0, tiled=True)
    other = (here + 1) % sections
    strips = lax.dynamic_slice_in_dim(incoming, other * rows, rows, 0)
    strips = strips.reshape(rows, PAIR, colours, tile).transpose(1, 0, 2, 3)
    place = lax.dynamic_slice_in_dim(incoming, here * rows, rows, 0)
    half_rows = place_rows // PAIR
    member = lax.axis_index("row") % PAIR
    place = lax.dynamic_slice_in_dim(place, member * half_rows, half_rows, 1)
    place = place.reshape(rows, -1, cols_here, rows_here, tile).transpose(2, 0, 3, 1, 4)
    return strips, place.reshape(cols_here, rows * rows_here, -1)


def moved(value, step):
    count = lax.axis_size("col")
    return lax.ppermute(value, "col", [(i, (i + step) % count) for i in range(count)])


def core_swapped(value):
    return lax.ppermute(value, "col", [(i, i ^ 1) for i in range(lax.axis_size("col"))])


def ring(shard, early_work):
    chips = lax.axis_size("col") // 2
    steps = chips // 2
    pieces = [(True, 0, shard), (False, 0, core_swapped(shard))]
    below, above = shard, shard
    for step in range(1, steps):
        if step > 2:
            held = [rows for _, _, rows in pieces[-6:-4]]
            below, above, held = lax.optimization_barrier((below, above, held))
            for i, rows in zip((-6, -5), held, strict=True):
                pieces[i] = (*pieces[i][:2], rows)
        below, above = moved(below, 2), moved(above, -2)
        pieces += [
            (False, chips - step, core_swapped(below)),
            (False, step, core_swapped(above)),
            (True, chips - step, below),
            (True, step, above),
        ]
    done = early_work(pieces[:-4])
    below, above, done = lax.optimization_barrier((below, above, done))
    pieces[-1] = (True, steps - 1, above)
    last = moved(below, 2)
    pieces += [(True, steps, last), (False, steps, core_swapped(last))]
    return pieces, done, above


def stem_body(parts, *refs):
    first_refs, low_refs, high_refs = (refs[i * parts : (i + 1) * parts] for i in range(3))
    weight_ref, out_ref, planes_ref = refs[3 * parts :]
    images, pixels, lanes = first_refs[0].shape
    width = 16
    count = pixels // (4 * width)
    row = lax.broadcasted_iota(jnp.int32, (count, parts * lanes), 0)
    group = images * count

    def put(a, b, slot, image, values):
        at = pl.multiple_of(slot * group + image * count, count)
        planes_ref[a + 1, b, pl.ds(at, count), :] = values.astype(jnp.bfloat16)
        if a == 3:
            moved_down = jnp.where(row == 0, 0.0, pltpu.roll(values, 1, 0))
            planes_ref[0, b, pl.ds(at, count), :] = moved_down.astype(jnp.bfloat16)
        if a == 0:
            moved_up = jnp.where(row == count - 1, 0.0, pltpu.roll(values, count - 1, 0))
            planes_ref[5, b, pl.ds(at, count), :] = moved_up.astype(jnp.bfloat16)

    def strided(part_refs, image, start, stride):
        return jnp.concatenate(
            [ref[image, pl.ds(start, count, stride=stride), :] for ref in part_refs], axis=1
        )

    def build(column, carry):
        j, b = column // 4, column % 4
        for image in range(images):
            for a in range(4):
                put(a, b, j + 1, image, strided(first_refs, image, width * a + column, 4 * width))
        return carry

    lax.fori_loop(0, width, build, 0)
    for image in range(images):
        for a in range(4):
            put(a, 3, 0, image, strided(low_refs, image, a, 4))
            put(a, 0, width // 4 + 1, image, strided(high_refs, image, a, 4))

    rows = width // 4 * group
    channels = out_ref.shape[1] // 16

    def convolve(phase, carry):
        a, b = phase // 4, phase % 4
        summed = planes_ref[a + 1, b, group : group + rows, :].astype(jnp.float32)
        for tap_a in range(3):
            for tap_b in range(3):
                column = b + tap_b + 3
                at = pl.multiple_of((column // 4) * group, group)
                window = planes_ref[a + tap_a, column % 4, pl.ds(at, rows), :]
                summed = summed + jnp.dot(
                    window, weight_ref[tap_a, tap_b], preferred_element_type=jnp.float32
                )
        at = pl.multiple_of(phase * channels, channels)
        out_ref[:, pl.ds(at, channels)] = jnp.maximum(summed, 0.0).astype(jnp.bfloat16)
        return carry

    lax.fori_loop(0, 16, convolve, 0)


def stem_features(strips, height, width, stem_first, stem_conv):
    images, parts, colours, _ = strips.shape
    total = parts * height
    channels = stem_first.shape[1]
    by_column = strips.reshape(images, parts, colours, height, width)

    def column(at):
        return by_column[:, :, :, :, at].transpose(2, 0, 1, 3).reshape(colours, images * total)

    count = lax.axis_size("col")
    forward = [(i, i + 1) for i in range(count - 1)]
    backward = [(target, source) for source, target in forward]
    low = lax.ppermute(column(width - 1), "col", forward)
    high = lax.ppermute(column(0), "col", backward)

    lanes = 128
    starts = range(0, channels, lanes)

    def first_of(values, spec, start):
        result = jnp.einsum(
            spec, values, stem_first[:, start : start + lanes], preferred_element_type=jnp.float32
        )
        result = lax.reduce_precision(jnp.maximum(result, 0.0), 8, 7)
        return result.reshape(images, -1, lanes)

    firsts = [first_of(strips, "mrkp,kc->mrpc", start) for start in starts]
    lows, highs = ([first_of(side, "kh,kc->hc", start) for start in starts] for side in (low, high))
    tokens = images * total * width // 16
    return pl.pallas_call(
        functools.partial(stem_body, len(starts)),
        out_shape=jax.ShapeDtypeStruct((tokens, 16 * channels), jnp.bfloat16),
        in_specs=[VMEM] * (3 * len(starts) + 1),
        out_specs=VMEM,
        scratch_shapes=[
            pltpu.VMEM((6, 4, (width // 4 + 2) * images * total // 4, channels), jnp.bfloat16)
        ],
        compiler_params=pltpu.CompilerParams(vmem_limit_bytes=28 << 20),
        cost_estimate=cost(18 * images * total * width * channels**2),
    )(*firsts, *lows, *highs, stem_conv)


def team_pairs(step):
    return [(i, i ^ step) for i in range(lax.axis_size("row"))]


def matmul_nt(left, right):
    return lax.dot_general(
        left, right, (((1,), (1,)), ((), ())), preferred_element_type=jnp.float32
    )


def project(rows, weight_ref):
    pair = jnp.concatenate([weight_ref[0], weight_ref[2]], axis=0)
    query_value = matmul_nt(rows, pair).astype(jnp.bfloat16)
    keys = matmul_nt(weight_ref[1], rows).astype(jnp.bfloat16)
    return query_value, keys


def project_body(weight_ref, *refs):
    *piece_refs, query_value_ref, key_ref = refs
    start = 0
    for piece_ref in piece_refs:
        count = piece_ref.shape[0]
        query_value, keys = project(piece_ref[...], weight_ref)
        query_value_ref[start : start + count] = query_value
        key_ref[:, start : start + count] = keys
        start += count


def attention_body(chips, tokens, early, late, place_ref, weight_ref, qv_ref, early_key_ref, *refs):
    *piece_refs, out_ref, all_ref, key_ref = refs
    place = place_ref[0]
    chip, core = place // 2, place % 2
    key_ref[HD:, :] = jnp.zeros((HD, key_ref.shape[1]), key_ref.dtype)

    def store(same, offset, query_value, keys):
        at = 2 * lax.rem(chip + offset, chips) + (core if same else 1 - core)
        at = pl.multiple_of(at * tokens, tokens)
        all_ref[pl.ds(at, tokens), :] = query_value
        key_ref[:HD, pl.ds(at, tokens)] = keys

    start = 0
    for same, offset in early:
        part = slice(start, start + tokens)
        store(same, offset, qv_ref[part, :], early_key_ref[:, part])
        start += tokens
    for (same, offset), piece_ref in zip(late, piece_refs, strict=True):
        store(same, offset, *project(piece_ref[...], weight_ref))

    block = 2 * tokens
    scale = HD ** (-0.5)

    def attend(step, carry):
        for i in range(2):
            at = pl.multiple_of((2 * step + i) * block, block)
            scores = jnp.dot(
                all_ref[pl.ds(at, block), :], key_ref[...], preferred_element_type=jnp.float32
            )
            peak = jnp.max(scores, axis=-1, keepdims=True)
            expo = jnp.exp((scores - peak) * scale)
            total = jnp.sum(expo, axis=-1, keepdims=True)
            probs = (expo * (1.0 / total)).astype(jnp.bfloat16)
            mixed = jnp.dot(probs, all_ref[...], preferred_element_type=jnp.float32)
            for j in range(2):
                out = mixed[j * tokens : (j + 1) * tokens, :].T[HD:, :]
                out_ref[2 * (2 * step + i) + j] = out.astype(jnp.bfloat16)
        return carry

    lax.fori_loop(0, all_ref.shape[0] // (2 * block), attend, 0)


def early_projection(weight, pieces):
    rows = sum(piece.shape[0] for _, _, piece in pieces)
    return pl.pallas_call(
        project_body,
        out_shape=(
            jax.ShapeDtypeStruct((rows, 2 * HD), jnp.bfloat16),
            jax.ShapeDtypeStruct((HD, rows), jnp.bfloat16),
        ),
        in_specs=[VMEM] * (1 + len(pieces)),
        out_specs=(VMEM, VMEM),
        compiler_params=pltpu.CompilerParams(vmem_limit_bytes=16 << 20),
        cost_estimate=cost(6 * rows * HD * weight.shape[2]),
    )(weight, *(piece for _, _, piece in pieces))


def attended_heads(normed, w_qkv):
    cols = lax.axis_size("col")
    weight = w_qkv.transpose(0, 2, 1)
    tokens = normed.shape[0]
    pieces, (query_value, keys), mark = ring(normed, functools.partial(early_projection, weight))
    count = cols - 6
    early, late = pieces[:count], pieces[count:]
    body = functools.partial(
        attention_body,
        cols // 2,
        tokens,
        [(same, offset) for same, offset, _ in early],
        [(same, offset) for same, offset, _ in late],
    )
    heads = pl.pallas_call(
        body,
        out_shape=jax.ShapeDtypeStruct((cols, HD, tokens), jnp.bfloat16),
        in_specs=[pl.BlockSpec(memory_space=pltpu.SMEM)] + [VMEM] * (3 + len(late)),
        out_specs=VMEM,
        scratch_shapes=[
            pltpu.VMEM((cols * tokens, 2 * HD), jnp.bfloat16),
            pltpu.VMEM((2 * HD, cols * tokens), jnp.bfloat16),
        ],
        compiler_params=pltpu.CompilerParams(vmem_limit_bytes=24 << 20),
        cost_estimate=cost(16 * HD * (cols * tokens) ** 2),
    )
    return heads(
        lax.axis_index("col").reshape(1), weight, query_value, keys, *(piece for _, _, piece in late)
    ), mark


def embed_body(
    half_ref, features_ref, gathered_ref, place_ref, own_ref, other_ref, left_ref, weight_ref, sems
):
    groups, per_group, channels, width = weight_ref.shape
    span = per_group * channels
    copies = [
        (
            pltpu.make_async_copy(
                features_ref.at[:, pl.ds(i * span, span)], left_ref.at[i], sems.at[0, i]
            ),
            pltpu.make_async_copy(
                gathered_ref.at[pl.ds(i * per_group, per_group), pl.ds(0, channels), :],
                weight_ref.at[i],
                sems.at[1, i],
            ),
        )
        for i in range(groups)
    ]
    for pair in copies:
        for copy in pair:
            copy.start()
    summed = jnp.zeros((features_ref.shape[0], width), jnp.float32)
    for i, pair in enumerate(copies):
        for copy in pair:
            copy.wait()
        summed = summed + jnp.dot(
            left_ref[i],
            weight_ref[i].reshape(span, width),
            preferred_element_type=jnp.float32,
        )
    columns, count, _ = place_ref.shape
    first_half = half_ref[0] == 0
    for column in range(columns):
        place = place_ref[column].astype(jnp.float32)
        first, second = (
            summed[(PAIR * column + image) * count :][:count] + place for image in range(PAIR)
        )
        part = slice(column * count, (column + 1) * count)
        own_ref[part, :] = jnp.where(first_half, first, second).astype(jnp.bfloat16)
        other_ref[part, :] = jnp.where(first_half, second, first).astype(jnp.bfloat16)


def embed(half, features, gathered, place):
    cols, _, width = gathered.shape
    groups = 4
    channels = features.shape[1] // cols
    out = jax.ShapeDtypeStruct((features.shape[0] // PAIR, width), jnp.bfloat16)
    return pl.pallas_call(
        embed_body,
        out_shape=(out, out),
        in_specs=[pl.BlockSpec(memory_space=pltpu.SMEM), HBM, HBM, VMEM],
        out_specs=(VMEM, VMEM),
        scratch_shapes=[
            pltpu.VMEM((groups, features.shape[0], features.shape[1] // groups), jnp.bfloat16),
            pltpu.VMEM((groups, cols // groups, channels, width), jnp.bfloat16),
            pltpu.SemaphoreType.DMA((2, groups)),
        ],
        compiler_params=pltpu.CompilerParams(vmem_limit_bytes=20 << 20),
        cost_estimate=cost(2 * features.size * width),
    )(half.reshape(1), features, gathered, place)


def out_body(heads_ref, gathered_ref, tokens_ref, gain_ref, after_ref, normed_ref, weight_ref, sems):
    first = gathered_ref.shape[1] - PAIR * HD
    copies = [
        pltpu.make_async_copy(
            gathered_ref.at[:, pl.ds(first + i * HD, HD), :], weight_ref.at[i], sems.at[i]
        )
        for i in range(PAIR)
    ]
    for copy in copies:
        copy.start()
    heads = heads_ref[...].astype(jnp.float32).T.astype(jnp.bfloat16)
    sides = []
    for i, copy in enumerate(copies):
        copy.wait()
        weight = weight_ref[i].reshape(heads.shape[1], weight_ref.shape[-1])
        sides.append(jnp.dot(heads, weight, preferred_element_type=jnp.float32))
    after = tokens_ref[...].astype(jnp.float32) + jnp.concatenate(sides, axis=1)
    after_ref[...] = after
    normed_ref[...] = layer_norm(after, gain_ref[...]).astype(jnp.bfloat16)


def out_projection(heads, gathered, tokens_in, gain):
    cols, _, half_width = gathered.shape
    width = tokens_in.shape[1]
    return pl.pallas_call(
        out_body,
        out_shape=(
            jax.ShapeDtypeStruct(tokens_in.shape, jnp.float32),
            jax.ShapeDtypeStruct(tokens_in.shape, jnp.bfloat16),
        ),
        in_specs=[VMEM, HBM, VMEM, VMEM],
        out_specs=(VMEM, VMEM),
        scratch_shapes=[
            pltpu.VMEM((PAIR, cols, HD, half_width), jnp.bfloat16),
            pltpu.SemaphoreType.DMA((PAIR,)),
        ],
        compiler_params=pltpu.CompilerParams(vmem_limit_bytes=16 << 20),
        cost_estimate=cost(2 * tokens_in.shape[0] * width * width),
    )(heads, gathered, tokens_in, gain.reshape(1, width))


def mlp_body(first_ref, second_ref, gathered_ref, out_first_ref, out_second_ref, weight_ref, sems):
    groups, per_group, units, width = weight_ref.shape
    copies = [
        pltpu.make_async_copy(
            gathered_ref.at[pl.ds(i * per_group, per_group)], weight_ref.at[i], sems.at[i]
        )
        for i in range(groups)
    ]
    for copy in copies:
        copy.start()
    tokens = first_ref.shape[0]
    rows = jnp.concatenate([first_ref[...], second_ref[...]], axis=0)
    summed = jnp.zeros(rows.shape, jnp.float32)
    for i, copy in enumerate(copies):
        copy.wait()
        up = weight_ref[i, :, : units // 2, :].reshape(-1, width)
        down = weight_ref[i, :, units // 2 :, :].reshape(-1, width)
        hidden = jax.nn.gelu(matmul_nt(rows, up), approximate=True).astype(jnp.bfloat16)
        summed = summed + jnp.dot(hidden, down, preferred_element_type=jnp.float32)
    out_first_ref[...] = summed[:tokens].astype(out_first_ref.dtype)
    out_second_ref[...] = summed[tokens:].astype(out_second_ref.dtype)


def mlp_terms(first, second, gathered, first_type):
    cols, rows, width = gathered.shape
    groups = 4
    return pl.pallas_call(
        mlp_body,
        out_shape=(
            jax.ShapeDtypeStruct(first.shape, first_type),
            jax.ShapeDtypeStruct(first.shape, jnp.bfloat16),
        ),
        in_specs=[VMEM, VMEM, HBM],
        out_specs=(VMEM, VMEM),
        scratch_shapes=[
            pltpu.VMEM((groups, cols // groups, rows, width), jnp.bfloat16),
            pltpu.SemaphoreType.DMA((groups,)),
        ],
        compiler_params=pltpu.CompilerParams(vmem_limit_bytes=20 << 20),
        cost_estimate=cost(4 * first.shape[0] * width * cols * rows),
    )(first, second, gathered)


def on_device(
    images,
    stem_first,
    stem_conv,
    patch_weight,
    position,
    gain_attn,
    w_qkv,
    w_out,
    gain_mlp,
    w_up,
    w_down,
):
    member = lax.axis_index("row") % TEAM
    model_width = patch_weight.shape[1]
    hidden_here = w_down.shape[0] // TEAM
    half = lax.axis_index("row") % PAIR
    half_width = model_width // PAIR
    half_patch = lax.dynamic_slice_in_dim(patch_weight, half * half_width, half_width, 1)
    first_shard = jnp.concatenate(
        [half_patch, w_out[:, :half_width], w_out[:, half_width:]], axis=0
    )
    first_weights = lax.all_gather(first_shard, "col", axis=0, tiled=False)
    first_weights = pltpu.with_memory_space_constraint(first_weights, pltpu.HBM)
    strips, place = image_strips(images, position)
    packed = jnp.concatenate(
        [
            lax.dynamic_slice_in_dim(w_up.T, member * hidden_here, hidden_here, 0),
            lax.dynamic_slice_in_dim(w_down, member * hidden_here, hidden_here, 0),
        ],
        axis=0,
    )
    packed, strips = lax.optimization_barrier((packed, strips))
    cols_here = position.shape[0]
    features = stem_features(strips, images.shape[3], images.shape[4], stem_first, stem_conv)
    features = pltpu.with_memory_space_constraint(features, pltpu.HBM)
    even = half == 0
    own, others = embed(half, features, first_weights, place)
    others = lax.ppermute(others, "row", team_pairs(1))
    tokens_in = jnp.concatenate(
        [jnp.where(even, own, others), jnp.where(even, others, own)], axis=1
    )
    token_rows = tokens_in.shape[0]
    normed = layer_norm(tokens_in.astype(jnp.float32), gain_attn).astype(jnp.bfloat16)
    heads, mark = attended_heads(normed, w_qkv)
    packed, mark = lax.optimization_barrier((packed, mark))
    gathered = lax.all_gather(packed, "col", axis=0, tiled=False)
    gathered = pltpu.with_memory_space_constraint(gathered, pltpu.HBM)
    heads_back = lax.all_to_all(heads, "col", 0, 0, tiled=True)
    after, normed_mlp = out_projection(
        heads_back.reshape(-1, token_rows), first_weights, tokens_in, gain_mlp
    )
    near, far, farthest = (lax.ppermute(normed_mlp, "row", team_pairs(i)) for i in (1, 2, 3))
    own_term, near_term = mlp_terms(normed_mlp, near, gathered, jnp.float32)
    far, farthest, near_term = lax.optimization_barrier((far, farthest, near_term))
    near_back = lax.ppermute(near_term, "row", team_pairs(1))
    far_term, farthest_term = mlp_terms(far, farthest, gathered, jnp.bfloat16)
    encoded = after + own_term + near_back.astype(jnp.float32)
    for step, term in ((2, far_term), (3, farthest_term)):
        encoded = encoded + lax.ppermute(term, "row", team_pairs(step)).astype(jnp.float32)
    return encoded.astype(jnp.bfloat16).reshape(1, 1, cols_here, -1, model_width)


def solution(mesh):
    placed = (
        P("section", None, None, "row", "col"),
        P(),
        P(),
        P("col", None),
        P("col", "row", None),
        P(),
        P(None, None, "col"),
        P("col", None),
        P(),
        P(None, "col"),
        P("col", None),
    )
    return jax.shard_map(
        on_device,
        mesh=mesh,
        in_specs=placed,
        out_specs=P("section", "row", "col", None, None),
        check_vma=False,
    )
```

profile of v0, /device:TPU:2, one launch (start us, length us, event | category | flops | bytes accessed | tf_op | source)
XLA Modules:
  0.0 184.6 jit_solution(13878715161289304113)
XLA Ops:
  6.5 1.0 fusion.18
  7.7 0.8 pad_maximum_fusion
  8.7 0.3 copy.23
  9.0 0.2 broadcast_in_dim.47
  9.5 1.0 bitcast_select_fusion
  10.6 7.5 %all-to-all-start = ((bf16[16,96,256]{2,1,0:T(8,128)(2,1)}), bf16[16,96,256]{2,1,0:T(8,128)(2,1)S(1)}, u32[]{:S(2)}, u32[]{:S(2)}) async-start(bf16[16,96,256]{2,1,0:T(8,128)(2,1)} %bitcast_select_fusion), calls=%async_computation | async-start | bytes 1572864 | tf_op jit(solution)/shard_map/all_to_all | solution.py:49
  18.4 0.9 constant_dynamic-slice_fusion.3
  19.3 0.7 pad_maximum_fusion.1
  20.1 11.0 %all-to-all-done = bf16[16,96,256]{2,1,0:T(8,128)(2,1)S(1)} async-done(((bf16[16,96,256]{2,1,0:T(8,128)(2,1)}), bf16[16,96,256]{2,1,0:T(8,128)(2,1)S(1)}, u32[]{:S(2)}, u32[]{:S(2)}) %all-to-all-start) | async-done | bytes 786464 | tf_op jit(solution)/shard_map/all_to_all | solution.py:49
  31.0 0.5 copy.27
  31.6 0.2 fusion.17
  31.8 0.7 copy.32
  32.5 1.3 collective-permute-start
  33.8 0.6 copy.33
  34.4 1.3 collective-permute-start.1
  35.7 1.7 maximum_reduce-precision_fusion.1
  37.5 1.8 maximum_reduce-precision_fusion
  39.7 0.9 fusion.3
  40.5 0.8 fusion.2
  41.4 0.8 fusion.1
  42.2 0.8 fusion
  43.1 1.6 copy-done.1
  44.7 1.3 copy-done.5
  46.0 11.1 %shard_map.109.features_ref = bf16[256,4096]{1,0:T(8,128)(2,1)S(1)} custom-call(f32[2,2048,128]{2,1,0:T(8,128)S(1)} %bitcast.57, f32[2,2048,128]{2,1,0:T(8,128)S(1)} %bitcast.58, f32[2,128,128]{2,1,0:T(8,128)S(1)} %bitcast.62, f32[2,128,128]{2,1,0:T(8,128)S(1)} %bitcast.63, f32[2,128,128]{2,1,0:T(8,128)S(1)} %bitcast.64, f32[2,128,128]{2,1,0:T(8,128)S(1)} %bitcast.65, ...), custom_call_target="tpu_custom_call" | custom-call | flops 4831838208 | bytes 18874368 | tf_op jit(solution)/shard_map/pallas_call | solution.py:182
  57.1 1.4 copy-done.2
  58.5 0.4 all-gather.5.cloned.1.call-done
  58.9 3.4 %shard_map.110 = (bf16[128,512]{1,0:T(8,128)(2,1)S(1)}, bf16[128,512]{1,0:T(8,128)(2,1)S(1)}) custom-call(s32[1]{0:T(128)} %bitcast.2.half_ref, bf16[256,4096]{1,0:T(8,128)(2,1)} %copy-done.2, bf16[16,384,512]{2,1,0:T(8,128)(2,1)} %bitcast.67, bf16[4,32,512]{2,1,0:T(8,128)(2,1)S(1)} %reshape.96.place_ref), custom_call_target="tpu_custom_call" | custom-call | flops 1073741824 | bytes 4194304 | tf_op jit(solution)/shard_map/pallas_call | solution.py:358
  62.3 1.1 collective-permute-start.2
  63.4 4.0 %collective-permute-done.2 = bf16[128,512]{1,0:T(8,128)(2,1)S(1)} collective-permute-done((bf16[128,512]{1,0:T(8,128)(2,1)S(1)}, bf16[128,512]{1,0:T(8,128)(2,1)S(1)}, u32[]{:S(2)}, u32[]{:S(2)}) %collective-permute-start.2) | collective-permute-done | bytes 131104 | tf_op jit(solution)/shard_map/ppermute | solution.py:495
  67.5 0.2 fusion.6
  67.7 0.2 fusion.8.refs_0_
  68.0 5.3 %collective-permute-start.3 = (bf16[128,1024]{1,0:T(8,128)(2,1)S(1)}, bf16[128,1024]{1,0:T(8,128)(2,1)S(1)}, u32[]{:S(2)}, u32[]{:S(2)}) collective-permute-start(bf16[128,1024]{1,0:T(8,128)(2,1)S(1)} %fusion.8.refs_0_), channel_id=1, source_target_pairs={{0,2},{1,3},{2,4},{3,5},{4,6},{5,7},{6,8},{7,9},{8,10},{9,11},{10,... | collective-permute-start | bytes 786440 | tf_op jit(solution)/shard_map/ppermute | solution.py:63
  73.3 3.3 %collective-permute-start.5 = (bf16[128,1024]{1,0:T(8,128)(2,1)S(1)}, bf16[128,1024]{1,0:T(8,128)(2,1)S(1)}, u32[]{:S(2)}, u32[]{:S(2)}) collective-permute-start(bf16[128,1024]{1,0:T(8,128)(2,1)S(1)} %fusion.8.refs_0_), channel_id=1, source_target_pairs={{0,14},{1,15},{2,0},{3,1},{4,2},{5,3},{6,4},{7,5},{8,6},{9,7},{10,... | collective-permute-start | bytes 786440 | tf_op jit(solution)/shard_map/ppermute | solution.py:63
  76.6 4.3 %collective-permute-done.3.refs_4_ = bf16[128,1024]{1,0:T(8,128)(2,1)S(1)} collective-permute-done((bf16[128,1024]{1,0:T(8,128)(2,1)S(1)}, bf16[128,1024]{1,0:T(8,128)(2,1)S(1)}, u32[]{:S(2)}, u32[]{:S(2)}) %collective-permute-start.3) | collective-permute-done | bytes 262176 | tf_op jit(solution)/shard_map/ppermute | solution.py:63
  81.0 3.1 %collective-permute-start.6 = (bf16[128,1024]{1,0:T(8,128)(2,1)S(1)}, bf16[128,1024]{1,0:T(8,128)(2,1)S(1)}, u32[]{:S(2)}, u32[]{:S(2)}) collective-permute-start(bf16[128,1024]{1,0:T(8,128)(2,1)S(1)} %collective-permute-done.5.refs_5_), channel_id=1, source_target_pairs={{0,14},{1,15},{2,0},{3,1},{4,2},{5,3},{6,4},{7,5},{8,6},{9,7},{10,... | collective-permute-start | bytes 786440 | tf_op jit(solution)/shard_map/ppermute | solution.py:63
  84.1 0.5 collective-permute-start.10
  84.6 3.7 %collective-permute-done.4.refs_8_ = bf16[128,1024]{1,0:T(8,128)(2,1)S(1)} collective-permute-done((bf16[128,1024]{1,0:T(8,128)(2,1)S(1)}, bf16[128,1024]{1,0:T(8,128)(2,1)S(1)}, u32[]{:S(2)}, u32[]{:S(2)}) %collective-permute-start.4) | collective-permute-done | bytes 262176 | tf_op jit(solution)/shard_map/ppermute | solution.py:63
  88.4 2.3 %collective-permute-done.6.refs_9_ = bf16[128,1024]{1,0:T(8,128)(2,1)S(1)} collective-permute-done((bf16[128,1024]{1,0:T(8,128)(2,1)S(1)}, bf16[128,1024]{1,0:T(8,128)(2,1)S(1)}, u32[]{:S(2)}, u32[]{:S(2)}) %collective-permute-start.6) | collective-permute-done | bytes 262176 | tf_op jit(solution)/shard_map/ppermute | solution.py:63
  90.7 1.7 collective-permute-start.7
  92.5 1.5 collective-permute-start.8
  94.0 1.7 shard_map.111
  95.7 5.0 %collective-permute-done.7.refs_2_ = bf16[128,1024]{1,0:T(8,128)(2,1)S(1)} collective-permute-done((bf16[128,1024]{1,0:T(8,128)(2,1)S(1)}, bf16[128,1024]{1,0:T(8,128)(2,1)S(1)}, u32[]{:S(2)}, u32[]{:S(2)}) %collective-permute-start.7) | collective-permute-done | bytes 262176 | tf_op jit(solution)/shard_map/ppermute | solution.py:63
  100.6 0.3 collective-permute-done.8.refs_3_
  100.9 1.8 collective-permute-start.16
  102.7 0.5 collective-permute-start.15
  103.2 6.6 %collective-permute-done.16.refs_4_ = bf16[128,1024]{1,0:T(8,128)(2,1)S(1)} collective-permute-done((bf16[128,1024]{1,0:T(8,128)(2,1)S(1)}, bf16[128,1024]{1,0:T(8,128)(2,1)S(1)}, u32[]{:S(2)}, u32[]{:S(2)}) %collective-permute-start.16) | collective-permute-done | bytes 262176 | tf_op jit(solution)/shard_map/ppermute | solution.py:63
  109.8 1.5 collective-permute-done.17.refs_5_
  111.4 11.4 %shard_map.112 = bf16[16,64,128]{2,1,0:T(8,128)(2,1)} custom-call(s32[1]{0:T(128)} %bitcast.place_ref, bf16[3,64,1024]{2,1,0:T(8,128)(2,1)S(1)} %bitcast.61, bf16[1280,128]{1,0:T(8,128)(2,1)S(1)} %get-tuple-element.38.qv_ref, bf16[64,1280]{1,0:T(8,128)(2,1)S(1)} %get-tuple-element.39.early_key_ref, bf16[128,1024]{1,0:T(8,128)(2,1)S(1)} %collective-permute-done.14.refs_0_, ...), custom_call_target="tpu_custom_call" | custom-call | flops 4294967296 | bytes 16777216 | tf_op jit(solution)/shard_map/pallas_call | solution.py:306
  122.8 5.0 %all-to-all-start.1 = ((bf16[16,64,128]{2,1,0:T(8,128)(2,1)}), bf16[16,64,128]{2,1,0:T(8,128)(2,1)S(1)}, u32[]{:S(2)}, u32[]{:S(2)}) async-start(bf16[16,64,128]{2,1,0:T(8,128)(2,1)} %shard_map.112), calls=%async_computation.1 | async-start | bytes 524288 | tf_op jit(solution)/shard_map/all_to_all | solution.py:505
  127.8 13.5 %all-to-all-done.1 = bf16[16,64,128]{2,1,0:T(8,128)(2,1)S(1)} async-done(((bf16[16,64,128]{2,1,0:T(8,128)(2,1)}), bf16[16,64,128]{2,1,0:T(8,128)(2,1)S(1)}, u32[]{:S(2)}, u32[]{:S(2)}) %all-to-all-start.1) | async-done | bytes 262176 | tf_op jit(solution)/shard_map/all_to_all | solution.py:505
  141.3 2.1 %shard_map.113 = (f32[128,1024]{1,0:T(8,128)S(1)}, bf16[128,1024]{1,0:T(8,128)(2,1)S(1)}) custom-call(bf16[1024,128]{1,0:T(8,128)(2,1)S(1)} %bitcast.59, bf16[16,384,512]{2,1,0:T(8,128)(2,1)} %bitcast.68, bf16[128,1024]{1,0:T(8,128)(2,1)S(1)} %pad_maximum_fusion.2.tokens_ref, f32[1,1024]{1,0:T(1,128)S(1)} %bitcast.66), custom_call_target="tpu_custom_call" | custom-call | flops 268435456 | bytes 1048576 | tf_op jit(solution)/shard_map/pallas_call | solution.py:397
  143.4 1.1 collective-permute-start.18
  144.5 0.3 collective-permute-start.19
  144.7 2.2 %collective-permute-start.20 = (bf16[128,1024]{1,0:T(8,128)(2,1)S(1)}, bf16[128,1024]{1,0:T(8,128)(2,1)S(1)}, u32[]{:S(2)}, u32[]{:S(2)}) collective-permute-start(bf16[128,1024]{1,0:T(8,128)(2,1)S(1)} %get-tuple-element.43.first_ref), channel_id=1, source_target_pairs={{0,48},{16,32},{32,16},{48,0},{64,112},{80,96},{96,80},{112,64},{1... | collective-permute-start | bytes 786440 | tf_op jit(solution)/shard_map/ppermute | solution.py:509
  147.0 5.7 %collective-permute-done.18.second_ref = bf16[128,1024]{1,0:T(8,128)(2,1)S(1)} collective-permute-done((bf16[128,1024]{1,0:T(8,128)(2,1)S(1)}, bf16[128,1024]{1,0:T(8,128)(2,1)S(1)}, u32[]{:S(2)}, u32[]{:S(2)}) %collective-permute-start.18) | collective-permute-done | bytes 262176 | tf_op jit(solution)/shard_map/ppermute | solution.py:509
  152.7 3.7 %shard_map.114 = (f32[128,1024]{1,0:T(8,128)S(1)}, bf16[128,1024]{1,0:T(8,128)(2,1)S(1)}) custom-call(bf16[128,1024]{1,0:T(8,128)(2,1)S(1)} %get-tuple-element.43.first_ref, bf16[128,1024]{1,0:T(8,128)(2,1)S(1)} %collective-permute-done.18.second_ref, bf16[16,128,1024]{2,1,0:T(8,128)(2,1)} %bitcast.69), custom_call_target="tpu_custom_call" | custom-call | flops 1073741824 | bytes 4194304 | tf_op jit(solution)/shard_map/pallas_call | solution.py:440
  156.4 2.3 %collective-permute-done.19.first_ref = bf16[128,1024]{1,0:T(8,128)(2,1)S(1)} collective-permute-done((bf16[128,1024]{1,0:T(8,128)(2,1)S(1)}, bf16[128,1024]{1,0:T(8,128)(2,1)S(1)}, u32[]{:S(2)}, u32[]{:S(2)}) %collective-permute-start.19) | collective-permute-done | bytes 262176 | tf_op jit(solution)/shard_map/ppermute | solution.py:509
  158.7 3.7 %shard_map.115 = (bf16[128,1024]{1,0:T(8,128)(2,1)S(1)}, bf16[128,1024]{1,0:T(8,128)(2,1)S(1)}) custom-call(bf16[128,1024]{1,0:T(8,128)(2,1)S(1)} %collective-permute-done.19.first_ref, bf16[128,1024]{1,0:T(8,128)(2,1)S(1)} %collective-permute-done.20.second_ref, bf16[16,128,1024]{2,1,0:T(8,128)(2,1)} %bitcast.70), custom_call_target="tpu_custom_call" | custom-call | flops 1073741824 | bytes 4194304 | tf_op jit(solution)/shard_map/pallas_call | solution.py:440
  162.5 1.3 collective-permute-start.23
  163.7 1.5 collective-permute-start.22
  165.2 0.9 collective-permute-start.21
  166.0 6.6 %collective-permute-done.23 = bf16[128,1024]{1,0:T(8,128)(2,1)S(1)} collective-permute-done((bf16[128,1024]{1,0:T(8,128)(2,1)S(1)}, bf16[128,1024]{1,0:T(8,128)(2,1)S(1)}, u32[]{:S(2)}, u32[]{:S(2)}) %collective-permute-start.23) | collective-permute-done | bytes 262176 | tf_op jit(solution)/shard_map/ppermute | solution.py:516
  172.7 4.2 %collective-permute-done.22 = bf16[128,1024]{1,0:T(8,128)(2,1)S(1)} collective-permute-done((bf16[128,1024]{1,0:T(8,128)(2,1)S(1)}, bf16[128,1024]{1,0:T(8,128)(2,1)S(1)}, u32[]{:S(2)}, u32[]{:S(2)}) %collective-permute-start.22) | collective-permute-done | bytes 262176 | tf_op jit(solution)/shard_map/ppermute | solution.py:516
  176.8 0.9 add_convert_fusion
  (68 shorter events, 1.7 us)
Async XLA Ops:
  6.5 1.1 copy-start
  6.5 2.1 %copy-start.8 = (bf16[1,8,48,16,16]{2,4,3,1,0:T(8,128)(2,1)S(1)}, bf16[1,8,48,16,16]{2,4,3,1,0:T(8,128)(2,1)}, u32[]{:S(2)}) copy-start(bf16[1,8,48,16,16]{2,4,3,1,0:T(8,128)(2,1)} %param.11) | copy-start | bytes 589828
  6.5 52.4 %all-gather.5.cloned.1.call-start = ((), (), s32[]{:S(2)}) async-start(), calls=%async_computation.2 | async-start | bytes 6684672 | tf_op jit(solution)/shard_map/all_gather | solution.py:479
  6.5 2.9 %copy-start.11 = (bf16[4,4,1024]{2,1,0:T(4,128)(2,1)S(1)}, bf16[4,4,1024]{2,1,0:T(4,128)(2,1)}, u32[]{:S(2)}) copy-start(bf16[4,4,1024]{2,1,0:T(4,128)(2,1)} %param.15) | copy-start | bytes 98308
  9.3 8.8 %copy-start.10 = (bf16[1024,256]{1,0:T(8,128)(2,1)S(1)}, bf16[1024,256]{1,0:T(8,128)(2,1)}, u32[]{:S(2)}) copy-start(bf16[1024,256]{1,0:T(8,128)(2,1)} %param.20) | copy-start | bytes 1572868
  10.6 20.5 %all-to-all-start = ((bf16[16,96,256]{2,1,0:T(8,128)(2,1)}), bf16[16,96,256]{2,1,0:T(8,128)(2,1)S(1)}, u32[]{:S(2)}, u32[]{:S(2)}) async-start(bf16[16,96,256]{2,1,0:T(8,128)(2,1)} %bitcast_select_fusion), calls=%async_computation | async-start | bytes 1572864 | tf_op jit(solution)/shard_map/all_to_all | solution.py:49
  18.0 134.6 %all-gather.7.cloned.1.call-start = ((), (), s32[]{:S(2)}) async-start(), calls=%async_computation.3 | async-start | bytes 4456448 | tf_op jit(solution)/shard_map/all_gather | solution.py:503
  31.5 2.9 %copy-start.6 = (bf16[2,8,48,256]{2,3,1,0:T(8,128)(2,1)}, bf16[2,8,48,256]{2,3,1,0:T(8,128)(2,1)S(1)}, u32[]{:S(2)}) copy-start(bf16[2,8,48,256]{2,3,1,0:T(8,128)(2,1)S(1)} %copy.27) | copy-start | bytes 1179652
  31.5 5.9 %copy-start.9 = (bf16[48,256]{1,0:T(8,128)(2,1)S(1)}, bf16[48,256]{1,0:T(8,128)(2,1)}, u32[]{:S(2)}) copy-start(bf16[48,256]{1,0:T(8,128)(2,1)} %param.12) | copy-start | bytes 73732
  32.5 7.1 %collective-permute-start = (bf16[48,256]{0,1:T(8,128)(2,1)}, bf16[48,256]{0,1:T(8,128)(2,1)S(1)}, u32[]{:S(2)}, u32[]{:S(2)}) collective-permute-start(bf16[48,256]{0,1:T(8,128)(2,1)} %bitcast.18), channel_id=1, source_target_pairs={{0,1},{1,2},{2,3},{3,4},{4,5},{5,6},{6,7},{7,8},{8,9},{9,10},{10,1... | collective-permute-start | bytes 73736 | tf_op jit(solution)/shard_map/ppermute | solution.py:166
  34.4 6.9 %collective-permute-start.1 = (bf16[48,256]{0,1:T(8,128)(2,1)}, bf16[48,256]{0,1:T(8,128)(2,1)S(1)}, u32[]{:S(2)}, u32[]{:S(2)}) collective-permute-start(bf16[48,256]{0,1:T(8,128)(2,1)} %bitcast.22), channel_id=1, source_target_pairs={{1,0},{2,1},{3,2},{4,3},{5,4},{6,5},{7,6},{8,7},{9,8},{10,9},{11,1... | collective-permute-start | bytes 73736 | tf_op jit(solution)/shard_map/ppermute | solution.py:167
  35.7 1.8 copy-start.7
  43.1 1.6 copy-start.1
  44.7 1.3 copy-start.5
  57.1 1.4 copy-start.2
  58.9 8.8 %copy-start.12 = (f32[1024]{0:T(1024)S(1)}, f32[1024]{0:T(1024)}, u32[]{:S(2)}) copy-start(f32[1024]{0:T(1024)} %param.16) | copy-start | bytes 12292
  58.9 35.1 %copy-start.3 = (bf16[3,1024,64]{1,2,0:T(8,128)(2,1)S(1)}, bf16[3,1024,64]{1,2,0:T(8,128)(2,1)}, u32[]{:S(2)}) copy-start(bf16[3,1024,64]{1,2,0:T(8,128)(2,1)} %param.17) | copy-start | bytes 1179652
  62.3 5.1 %collective-permute-start.2 = (bf16[128,512]{1,0:T(8,128)(2,1)S(1)}, bf16[128,512]{1,0:T(8,128)(2,1)S(1)}, u32[]{:S(2)}, u32[]{:S(2)}) collective-permute-start(bf16[128,512]{1,0:T(8,128)(2,1)S(1)} %get-tuple-element.31), channel_id=1, source_target_pairs={{0,16},{16,0},{32,48},{48,32},{64,80},{80,64},{96,112},{112,96},{1... | collective-permute-start | bytes 393224 | tf_op jit(solution)/shard_map/ppermute | solution.py:495
  68.0 12.9 %collective-permute-start.3 = (bf16[128,1024]{1,0:T(8,128)(2,1)S(1)}, bf16[128,1024]{1,0:T(8,128)(2,1)S(1)}, u32[]{:S(2)}, u32[]{:S(2)}) collective-permute-start(bf16[128,1024]{1,0:T(8,128)(2,1)S(1)} %fusion.8.refs_0_), channel_id=1, source_target_pairs={{0,2},{1,3},{2,4},{3,5},{4,6},{5,7},{6,8},{7,9},{8,10},{9,11},{10,... | collective-permute-start | bytes 786440 | tf_op jit(solution)/shard_map/ppermute | solution.py:63
  73.3 7.7 %collective-permute-start.5 = (bf16[128,1024]{1,0:T(8,128)(2,1)S(1)}, bf16[128,1024]{1,0:T(8,128)(2,1)S(1)}, u32[]{:S(2)}, u32[]{:S(2)}) collective-permute-start(bf16[128,1024]{1,0:T(8,128)(2,1)S(1)} %fusion.8.refs_0_), channel_id=1, source_target_pairs={{0,14},{1,15},{2,0},{3,1},{4,2},{5,3},{6,4},{7,5},{8,6},{9,7},{10,... | collective-permute-start | bytes 786440 | tf_op jit(solution)/shard_map/ppermute | solution.py:63
  80.8 7.6 %collective-permute-start.4 = (bf16[128,1024]{1,0:T(8,128)(2,1)S(1)}, bf16[128,1024]{1,0:T(8,128)(2,1)S(1)}, u32[]{:S(2)}, u32[]{:S(2)}) collective-permute-start(bf16[128,1024]{1,0:T(8,128)(2,1)S(1)} %collective-permute-done.3.refs_4_), channel_id=1, source_target_pairs={{0,2},{1,3},{2,4},{3,5},{4,6},{5,7},{6,8},{7,9},{8,10},{9,11},{10,... | collective-permute-start | bytes 786440 | tf_op jit(solution)/shard_map/ppermute | solution.py:63
  81.0 9.7 %collective-permute-start.6 = (bf16[128,1024]{1,0:T(8,128)(2,1)S(1)}, bf16[128,1024]{1,0:T(8,128)(2,1)S(1)}, u32[]{:S(2)}, u32[]{:S(2)}) collective-permute-start(bf16[128,1024]{1,0:T(8,128)(2,1)S(1)} %collective-permute-done.5.refs_5_), channel_id=1, source_target_pairs={{0,14},{1,15},{2,0},{3,1},{4,2},{5,3},{6,4},{7,5},{8,6},{9,7},{10,... | collective-permute-start | bytes 786440 | tf_op jit(solution)/shard_map/ppermute | solution.py:63
  84.1 6.6 %collective-permute-start.9 = (bf16[128,1024]{1,0:T(8,128)(2,1)S(1)}, bf16[128,1024]{1,0:T(8,128)(2,1)S(1)}, u32[]{:S(2)}, u32[]{:S(2)}) collective-permute-start(bf16[128,1024]{1,0:T(8,128)(2,1)S(1)} %fusion.8.refs_0_), channel_id=1, source_target_pairs={{0,1},{1,0},{2,3},{3,2},{4,5},{5,4},{6,7},{7,6},{8,9},{9,8},{10,11... | collective-permute-start | bytes 786440 | tf_op jit(solution)/shard_map/ppermute | solution.py:67
  84.1 8.3 %collective-permute-start.10 = (bf16[128,1024]{1,0:T(8,128)(2,1)S(1)}, bf16[128,1024]{1,0:T(8,128)(2,1)S(1)}, u32[]{:S(2)}, u32[]{:S(2)}) collective-permute-start(bf16[128,1024]{1,0:T(8,128)(2,1)S(1)} %collective-permute-done.3.refs_4_), channel_id=1, source_target_pairs={{0,1},{1,0},{2,3},{3,2},{4,5},{5,4},{6,7},{7,6},{8,9},{9,8},{10,11... | collective-permute-start | bytes 786440 | tf_op jit(solution)/shard_map/ppermute | solution.py:67
  84.6 9.3 %collective-permute-start.11 = (bf16[128,1024]{1,0:T(8,128)(2,1)S(1)}, bf16[128,1024]{1,0:T(8,128)(2,1)S(1)}, u32[]{:S(2)}, u32[]{:S(2)}) collective-permute-start(bf16[128,1024]{1,0:T(8,128)(2,1)S(1)} %collective-permute-done.5.refs_5_), channel_id=1, source_target_pairs={{0,1},{1,0},{2,3},{3,2},{4,5},{5,4},{6,7},{7,6},{8,9},{9,8},{10,11... | collective-permute-start | bytes 786440 | tf_op jit(solution)/shard_map/ppermute | solution.py:67
  88.4 5.6 %collective-permute-start.12 = (bf16[128,1024]{1,0:T(8,128)(2,1)S(1)}, bf16[128,1024]{1,0:T(8,128)(2,1)S(1)}, u32[]{:S(2)}, u32[]{:S(2)}) collective-permute-start(bf16[128,1024]{1,0:T(8,128)(2,1)S(1)} %collective-permute-done.4.refs_8_), channel_id=1, source_target_pairs={{0,1},{1,0},{2,3},{3,2},{4,5},{5,4},{6,7},{7,6},{8,9},{9,8},{10,11... | collective-permute-start | bytes 786440 | tf_op jit(solution)/shard_map/ppermute | solution.py:67
  90.7 3.3 %collective-permute-start.13 = (bf16[128,1024]{1,0:T(8,128)(2,1)S(1)}, bf16[128,1024]{1,0:T(8,128)(2,1)S(1)}, u32[]{:S(2)}, u32[]{:S(2)}) collective-permute-start(bf16[128,1024]{1,0:T(8,128)(2,1)S(1)} %collective-permute-done.6.refs_9_), channel_id=1, source_target_pairs={{0,1},{1,0},{2,3},{3,2},{4,5},{5,4},{6,7},{7,6},{8,9},{9,8},{10,11... | collective-permute-start | bytes 786440 | tf_op jit(solution)/shard_map/ppermute | solution.py:67
  90.7 9.9 %collective-permute-start.7 = (bf16[128,1024]{1,0:T(8,128)(2,1)S(1)}, bf16[128,1024]{1,0:T(8,128)(2,1)S(1)}, u32[]{:S(2)}, u32[]{:S(2)}) collective-permute-start(bf16[128,1024]{1,0:T(8,128)(2,1)S(1)} %collective-permute-done.4.refs_8_), channel_id=1, source_target_pairs={{0,2},{1,3},{2,4},{3,5},{4,6},{5,7},{6,8},{7,9},{8,10},{9,11},{10,... | collective-permute-start | bytes 786440 | tf_op jit(solution)/shard_map/ppermute | solution.py:63
  92.5 8.4 %collective-permute-start.8 = (bf16[128,1024]{1,0:T(8,128)(2,1)S(1)}, bf16[128,1024]{1,0:T(8,128)(2,1)S(1)}, u32[]{:S(2)}, u32[]{:S(2)}) collective-permute-start(bf16[128,1024]{1,0:T(8,128)(2,1)S(1)} %collective-permute-done.6.refs_9_), channel_id=1, source_target_pairs={{0,14},{1,15},{2,0},{3,1},{4,2},{5,3},{6,4},{7,5},{8,6},{9,7},{10,... | collective-permute-start | bytes 786440 | tf_op jit(solution)/shard_map/ppermute | solution.py:63
  100.9 8.9 %collective-permute-start.16 = (bf16[128,1024]{1,0:T(8,128)(2,1)S(1)}, bf16[128,1024]{1,0:T(8,128)(2,1)S(1)}, u32[]{:S(2)}, u32[]{:S(2)}) collective-permute-start(bf16[128,1024]{1,0:T(8,128)(2,1)S(1)} %collective-permute-done.7.refs_2_), channel_id=1, source_target_pairs={{0,2},{1,3},{2,4},{3,5},{4,6},{5,7},{6,8},{7,9},{8,10},{9,11},{10,... | collective-permute-start | bytes 786440 | tf_op jit(solution)/shard_map/ppermute | solution.py:63
  102.7 7.1 %collective-permute-start.14 = (bf16[128,1024]{1,0:T(8,128)(2,1)S(1)}, bf16[128,1024]{1,0:T(8,128)(2,1)S(1)}, u32[]{:S(2)}, u32[]{:S(2)}) collective-permute-start(bf16[128,1024]{1,0:T(8,128)(2,1)S(1)} %collective-permute-done.7.refs_2_), channel_id=1, source_target_pairs={{0,1},{1,0},{2,3},{3,2},{4,5},{5,4},{6,7},{7,6},{8,9},{9,8},{10,11... | collective-permute-start | bytes 786440 | tf_op jit(solution)/shard_map/ppermute | solution.py:67
  102.7 7.1 %collective-permute-start.15 = (bf16[128,1024]{1,0:T(8,128)(2,1)S(1)}, bf16[128,1024]{1,0:T(8,128)(2,1)S(1)}, u32[]{:S(2)}, u32[]{:S(2)}) collective-permute-start(bf16[128,1024]{1,0:T(8,128)(2,1)S(1)} %collective-permute-done.8.refs_3_), channel_id=1, source_target_pairs={{0,1},{1,0},{2,3},{3,2},{4,5},{5,4},{6,7},{7,6},{8,9},{9,8},{10,11... | collective-permute-start | bytes 786440 | tf_op jit(solution)/shard_map/ppermute | solution.py:67
  109.8 1.5 collective-permute-start.17
  111.4 29.9 %copy-start.4 = (f32[1024]{0:T(1024)S(1)}, f32[1024]{0:T(1024)}, u32[]{:S(2)}) copy-start(f32[1024]{0:T(1024)} %param.19) | copy-start | bytes 12292
  122.8 18.5 %all-to-all-start.1 = ((bf16[16,64,128]{2,1,0:T(8,128)(2,1)}), bf16[16,64,128]{2,1,0:T(8,128)(2,1)S(1)}, u32[]{:S(2)}, u32[]{:S(2)}) async-start(bf16[16,64,128]{2,1,0:T(8,128)(2,1)} %shard_map.112), calls=%async_computation.1 | async-start | bytes 524288 | tf_op jit(solution)/shard_map/all_to_all | solution.py:505
  143.4 9.3 %collective-permute-start.18 = (bf16[128,1024]{1,0:T(8,128)(2,1)S(1)}, bf16[128,1024]{1,0:T(8,128)(2,1)S(1)}, u32[]{:S(2)}, u32[]{:S(2)}) collective-permute-start(bf16[128,1024]{1,0:T(8,128)(2,1)S(1)} %get-tuple-element.43.first_ref), channel_id=1, source_target_pairs={{0,16},{16,0},{32,48},{48,32},{64,80},{80,64},{96,112},{112,96},{1... | collective-permute-start | bytes 786440 | tf_op jit(solution)/shard_map/ppermute | solution.py:509
  144.5 14.2 %collective-permute-start.19 = (bf16[128,1024]{1,0:T(8,128)(2,1)S(1)}, bf16[128,1024]{1,0:T(8,128)(2,1)S(1)}, u32[]{:S(2)}, u32[]{:S(2)}) collective-permute-start(bf16[128,1024]{1,0:T(8,128)(2,1)S(1)} %get-tuple-element.43.first_ref), channel_id=1, source_target_pairs={{0,32},{16,48},{32,0},{48,16},{64,96},{80,112},{96,64},{112,80},{1... | collective-permute-start | bytes 786440 | tf_op jit(solution)/shard_map/ppermute | solution.py:509
  144.7 14.0 %collective-permute-start.20 = (bf16[128,1024]{1,0:T(8,128)(2,1)S(1)}, bf16[128,1024]{1,0:T(8,128)(2,1)S(1)}, u32[]{:S(2)}, u32[]{:S(2)}) collective-permute-start(bf16[128,1024]{1,0:T(8,128)(2,1)S(1)} %get-tuple-element.43.first_ref), channel_id=1, source_target_pairs={{0,48},{16,32},{32,16},{48,0},{64,112},{80,96},{96,80},{112,64},{1... | collective-permute-start | bytes 786440 | tf_op jit(solution)/shard_map/ppermute | solution.py:509
  162.5 10.2 %collective-permute-start.23 = (bf16[128,1024]{1,0:T(8,128)(2,1)S(1)}, bf16[128,1024]{1,0:T(8,128)(2,1)S(1)}, u32[]{:S(2)}, u32[]{:S(2)}) collective-permute-start(bf16[128,1024]{1,0:T(8,128)(2,1)S(1)} %get-tuple-element.52), channel_id=1, source_target_pairs={{0,48},{16,32},{32,16},{48,0},{64,112},{80,96},{96,80},{112,64},{1... | collective-permute-start | bytes 786440 | tf_op jit(solution)/shard_map/ppermute | solution.py:516
  163.7 13.1 %collective-permute-start.22 = (bf16[128,1024]{1,0:T(8,128)(2,1)S(1)}, bf16[128,1024]{1,0:T(8,128)(2,1)S(1)}, u32[]{:S(2)}, u32[]{:S(2)}) collective-permute-start(bf16[128,1024]{1,0:T(8,128)(2,1)S(1)} %get-tuple-element.51), channel_id=1, source_target_pairs={{0,32},{16,48},{32,0},{48,16},{64,96},{80,112},{96,64},{112,80},{1... | collective-permute-start | bytes 786440 | tf_op jit(solution)/shard_map/ppermute | solution.py:516
  165.2 11.6 %collective-permute-start.21 = (bf16[128,1024]{1,0:T(8,128)(2,1)S(1)}, bf16[128,1024]{1,0:T(8,128)(2,1)S(1)}, u32[]{:S(2)}, u32[]{:S(2)}) collective-permute-start(bf16[128,1024]{1,0:T(8,128)(2,1)S(1)} %get-tuple-element.48), channel_id=1, source_target_pairs={{0,16},{16,0},{32,48},{48,32},{64,80},{80,64},{96,112},{112,96},{1... | collective-permute-start | bytes 786440 | tf_op jit(solution)/shard_map/ppermute | solution.py:512
Sparse Core Ops, SparseCore 0:
  9.2 49.6 all-gather.4
  101.0 44.4 all-gather.6
where the time goes:
time: 187 us; the launch traced here: 185 us
  waiting for transfers between devices  71.4 us (38%)
  starting transfers between devices  41.2 us (22%)
  Pallas kernels  37.2 us (20%)
  between operations  13.9 us (7%)
  local copies, waits for them, and re-layouts  10 us (5%)
  matrix products  6.92 us (4%)
  other arithmetic  4.01 us (2%)
    ppermute x7, waiting for transfers between devices, moved(): lax.ppermute(value, 'col', [(i, (i + step) % count) for i in range(count)])  22.2 us
    ppermute x7, starting transfers between devices, moved(): lax.ppermute(value, 'col', [(i, (i + step) % count) for i in range(count)])  16.9 us
    all_to_all x1, waiting for transfers between devices, on_device(): heads_back = lax.all_to_all(heads, 'col', 0, 0, tiled=True)  13.5 us
    pallas_call x1, Pallas kernels, attended_heads(): heads(lax.axis_index('col').reshape(1), weight, query_value, keys, *(piec...  11.4 us
    pallas_call x1, Pallas kernels, stem_features(): pl.pallas_call(functools.partial(stem_body, len(starts)), out_shape=jax.S...  11.1 us
    all_to_all x1, waiting for transfers between devices, image_strips(): incoming = lax.all_to_all(outgoing, ('section', 'row'), 0, 0, tiled=True)  11 us
    ppermute x2, waiting for transfers between devices, on_device(): lax.ppermute(term, 'row', team_pairs(step)).astype(jnp.float32)  10.8 us
    ppermute x3, waiting for transfers between devices, on_device(): lax.ppermute(normed_mlp, 'row', team_pairs(i))  7.97 us
  transfers between devices with their start and end apart: 28, of which 15 were waited for; matrix products, arithmetic and copies ran while one was open for 7% of the time, Pallas kernels for 16%

commit v1 on v0

--- a/solution.py
+++ b/solution.py
@@ -74,10 +74,11 @@
     below, above = shard, shard
     for step in range(1, steps):
         if step > 2:
-            held = [rows for _, _, rows in pieces[-6:-4]]
-            below, above, held = lax.optimization_barrier((below, above, held))
-            for i, rows in zip((-6, -5), held, strict=True):
-                pieces[i] = (*pieces[i][:2], rows)
+            below, above, first, second = lax.optimization_barrier(
+                (below, above, pieces[-6][2], pieces[-5][2])
+            )
+            pieces[-6] = (*pieces[-6][:2], first)
+            pieces[-5] = (*pieces[-5][:2], second)
         below, above = moved(below, 2), moved(above, -2)
         pieces += [
             (False, chips - step, core_swapped(below)),
@@ -94,9 +95,23 @@
 
 
 def stem_body(parts, *refs):
-    first_refs, low_refs, high_refs = (refs[i * parts : (i + 1) * parts] for i in range(3))
-    weight_ref, out_ref, planes_ref = refs[3 * parts :]
+    first_refs = refs[:parts]
+    low_ref, high_ref, first_weight_ref, conv_ref, out_ref = refs[parts : parts + 5]
+    planes_ref, weight_ref, done_ref, low_refs, high_refs, sems = refs[parts + 5 :]
     images, pixels, lanes = first_refs[0].shape
+    fetch = pltpu.make_async_copy(conv_ref, weight_ref, sems.at[16])
+    fetch.start()
+    low_refs = [low_refs.at[i] for i in range(parts)]
+    high_refs = [high_refs.at[i] for i in range(parts)]
+    for side_ref, side_refs in ((low_ref, low_refs), (high_ref, high_refs)):
+        side = jnp.dot(
+            side_ref[...].astype(jnp.float32).T.astype(jnp.bfloat16),
+            first_weight_ref[...],
+            preferred_element_type=jnp.float32,
+        )
+        side = jnp.maximum(side, 0.0).astype(jnp.bfloat16).astype(jnp.float32)
+        for i, ref in enumerate(side_refs):
+            ref[...] = side[:, i * lanes : (i + 1) * lanes].reshape(images, -1, lanes)
     width = 16
     count = pixels // (4 * width)
     row = lax.broadcasted_iota(jnp.int32, (count, parts * lanes), 0)
@@ -132,6 +147,14 @@
 
     rows = width // 4 * group
     channels = out_ref.shape[1] // 16
+
+    def sent(phase):
+        at = pl.multiple_of(phase * channels, channels)
+        return pltpu.make_async_copy(
+            done_ref.at[phase], out_ref.at[:, pl.ds(at, channels)], sems.at[phase]
+        )
+
+    fetch.wait()
 
     def convolve(phase, carry):
         a, b = phase // 4, phase % 4
@@ -144,11 +167,13 @@
                 summed = summed + jnp.dot(
                     window, weight_ref[tap_a, tap_b], preferred_element_type=jnp.float32
                 )
-        at = pl.multiple_of(phase * channels, channels)
-        out_ref[:, pl.ds(at, channels)] = jnp.maximum(summed, 0.0).astype(jnp.bfloat16)
+        done_ref[phase] = jnp.maximum(summed, 0.0).astype(jnp.bfloat16)
+        sent(phase).start()
         return carry
 
     lax.fori_loop(0, 16, convolve, 0)
+    for phase in range(16):
+        sent(phase).wait()
 
 
 def stem_features(strips, height, width, stem_first, stem_conv):
@@ -177,19 +202,29 @@
         return result.reshape(images, -1, lanes)
 
     firsts = [first_of(strips, "mrkp,kc->mrpc", start) for start in starts]
-    lows, highs = ([first_of(side, "kh,kc->hc", start) for start in starts] for side in (low, high))
     tokens = images * total * width // 16
     return pl.pallas_call(
         functools.partial(stem_body, len(starts)),
-        out_shape=jax.ShapeDtypeStruct((tokens, 16 * channels), jnp.bfloat16),
-        in_specs=[VMEM] * (3 * len(starts) + 1),
-        out_specs=VMEM,
+        out_shape=pltpu.HBM((tokens, 16 * channels), jnp.bfloat16),
+        in_specs=[VMEM] * (len(starts) + 3) + [HBM],
+        out_specs=HBM,
         scratch_shapes=[
-            pltpu.VMEM((6, 4, (width // 4 + 2) * images * total // 4, channels), jnp.bfloat16)
+            pltpu.VMEM((6, 4, (width // 4 + 2) * images * total // 4, channels), jnp.bfloat16),
+            pltpu.VMEM(stem_conv.shape, jnp.bfloat16),
+            pltpu.VMEM((16, tokens, channels), jnp.bfloat16),
+            pltpu.VMEM((len(starts), images, total, lanes), jnp.float32),
+            pltpu.VMEM((len(starts), images, total, lanes), jnp.float32),
+            pltpu.SemaphoreType.DMA((17,)),
         ],
-        compiler_params=pltpu.CompilerParams(vmem_limit_bytes=28 << 20),
+        compiler_params=pltpu.CompilerParams(vmem_limit_bytes=20 << 20),
         cost_estimate=cost(18 * images * total * width * channels**2),
-    )(*firsts, *lows, *highs, stem_conv)
+    )(
+        *firsts,
+        low,
+        high,
+        stem_first,
+        pltpu.with_memory_space_constraint(stem_conv, pltpu.HBM),
+    )
 
 
 def team_pairs(step):
@@ -221,24 +256,33 @@
 
 
 def attention_body(chips, tokens, early, late, place_ref, weight_ref, qv_ref, early_key_ref, *refs):
-    *piece_refs, out_ref, all_ref, key_ref = refs
+    *piece_refs, out_ref, all_ref, key_ref, sems = refs
     place = place_ref[0]
     chip, core = place // 2, place % 2
     key_ref[HD:, :] = jnp.zeros((HD, key_ref.shape[1]), key_ref.dtype)
 
-    def store(same, offset, query_value, keys):
+    def places(same, offset):
         at = 2 * lax.rem(chip + offset, chips) + (core if same else 1 - core)
-        at = pl.multiple_of(at * tokens, tokens)
-        all_ref[pl.ds(at, tokens), :] = query_value
-        key_ref[:HD, pl.ds(at, tokens)] = keys
-
-    start = 0
-    for same, offset in early:
-        part = slice(start, start + tokens)
-        store(same, offset, qv_ref[part, :], early_key_ref[:, part])
-        start += tokens
+        at = pl.ds(pl.multiple_of(at * tokens, tokens), tokens)
+        return all_ref.at[at, :], key_ref.at[pl.ds(0, HD), at]
+
+    copies = []
+    for i, (same, offset) in enumerate(early):
+        part = pl.ds(i * tokens, tokens)
+        query_value, keys = places(same, offset)
+        copies += [
+            pltpu.make_async_copy(qv_ref.at[part, :], query_value, sems.at[0, i]),
+            pltpu.make_async_copy(early_key_ref.at[:, part], keys, sems.at[1, i]),
+        ]
+    for copy in copies:
+        copy.start()
     for (same, offset), piece_ref in zip(late, piece_refs, strict=True):
-        store(same, offset, *project(piece_ref[...], weight_ref))
+        for ref, values in zip(
+            places(same, offset), project(piece_ref[...], weight_ref), strict=True
+        ):
+            ref[...] = values
+    for copy in copies:
+        copy.wait()
 
     block = 2 * tokens
     scale = HD ** (-0.5)
@@ -267,12 +311,12 @@
     return pl.pallas_call(
         project_body,
         out_shape=(
-            jax.ShapeDtypeStruct((rows, 2 * HD), jnp.bfloat16),
-            jax.ShapeDtypeStruct((HD, rows), jnp.bfloat16),
+            pltpu.HBM((rows, 2 * HD), jnp.bfloat16),
+            pltpu.HBM((HD, rows), jnp.bfloat16),
         ),
         in_specs=[VMEM] * (1 + len(pieces)),
         out_specs=(VMEM, VMEM),
-        compiler_params=pltpu.CompilerParams(vmem_limit_bytes=16 << 20),
+        compiler_params=pltpu.CompilerParams(vmem_limit_bytes=8 << 20),
         cost_estimate=cost(6 * rows * HD * weight.shape[2]),
     )(weight, *(piece for _, _, piece in pieces))
 
@@ -294,17 +338,22 @@
     heads = pl.pallas_call(
         body,
         out_shape=jax.ShapeDtypeStruct((cols, HD, tokens), jnp.bfloat16),
-        in_specs=[pl.BlockSpec(memory_space=pltpu.SMEM)] + [VMEM] * (3 + len(late)),
+        in_specs=[pl.BlockSpec(memory_space=pltpu.SMEM), VMEM, HBM, HBM] + [VMEM] * len(late),
         out_specs=VMEM,
         scratch_shapes=[
             pltpu.VMEM((cols * tokens, 2 * HD), jnp.bfloat16),
             pltpu.VMEM((2 * HD, cols * tokens), jnp.bfloat16),
+            pltpu.SemaphoreType.DMA((2, len(early))),
         ],
-        compiler_params=pltpu.CompilerParams(vmem_limit_bytes=24 << 20),
+        compiler_params=pltpu.CompilerParams(vmem_limit_bytes=14 << 20),
         cost_estimate=cost(16 * HD * (cols * tokens) ** 2),
     )
     return heads(
-        lax.axis_index("col").reshape(1), weight, query_value, keys, *(piece for _, _, piece in late)
+        lax.axis_index("col").reshape(1),
+        weight,
+        pltpu.with_memory_space_constraint(query_value, pltpu.HBM),
+        pltpu.with_memory_space_constraint(keys, pltpu.HBM),
+        *(piece for _, _, piece in late)
     ), mark
 
 
@@ -370,29 +419,24 @@
     )(half.reshape(1), features, gathered, place)
 
 
-def out_body(heads_ref, gathered_ref, tokens_ref, gain_ref, after_ref, normed_ref, weight_ref, sems):
-    first = gathered_ref.shape[1] - PAIR * HD
-    copies = [
-        pltpu.make_async_copy(
-            gathered_ref.at[:, pl.ds(first + i * HD, HD), :], weight_ref.at[i], sems.at[i]
-        )
-        for i in range(PAIR)
-    ]
-    for copy in copies:
-        copy.start()
-    heads = heads_ref[...].astype(jnp.float32).T.astype(jnp.bfloat16)
-    sides = []
-    for i, copy in enumerate(copies):
-        copy.wait()
-        weight = weight_ref[i].reshape(heads.shape[1], weight_ref.shape[-1])
-        sides.append(jnp.dot(heads, weight, preferred_element_type=jnp.float32))
+def out_body(member_ref, heads_ref, *refs):
+    *weight_refs, tokens_ref, gain_ref, after_ref, normed_ref = refs
+    cols, rows, half_width = weight_refs[0].shape
+    rows = rows // PAIR
+    sides = [0.0] * PAIR
+    for step, weight_ref in enumerate(weight_refs):
+        at = pl.multiple_of(jnp.bitwise_xor(member_ref[0], step) * rows, rows)
+        heads = heads_ref[:, pl.ds(at, rows), :].reshape(cols * rows, -1)
+        heads = heads.astype(jnp.float32).T.astype(jnp.bfloat16)
+        for i in range(PAIR):
+            weight = weight_ref[:, i * rows : (i + 1) * rows, :].reshape(cols * rows, half_width)
+            sides[i] = sides[i] + jnp.dot(heads, weight, preferred_element_type=jnp.float32)
     after = tokens_ref[...].astype(jnp.float32) + jnp.concatenate(sides, axis=1)
     after_ref[...] = after
     normed_ref[...] = layer_norm(after, gain_ref[...]).astype(jnp.bfloat16)
 
 
-def out_projection(heads, gathered, tokens_in, gain):
-    cols, _, half_width = gathered.shape
+def out_projection(member, heads, quarters, tokens_in, gain):
     width = tokens_in.shape[1]
     return pl.pallas_call(
         out_body,
@@ -400,15 +444,11 @@
             jax.ShapeDtypeStruct(tokens_in.shape, jnp.float32),
             jax.ShapeDtypeStruct(tokens_in.shape, jnp.bfloat16),
         ),
-        in_specs=[VMEM, HBM, VMEM, VMEM],
+        in_specs=[pl.BlockSpec(memory_space=pltpu.SMEM)] + [VMEM] * (3 + len(quarters)),
         out_specs=(VMEM, VMEM),
-        scratch_shapes=[
-            pltpu.VMEM((PAIR, cols, HD, half_width), jnp.bfloat16),
-            pltpu.SemaphoreType.DMA((PAIR,)),
-        ],
-        compiler_params=pltpu.CompilerParams(vmem_limit_bytes=16 << 20),
+        compiler_params=pltpu.CompilerParams(vmem_limit_bytes=10 << 20),
         cost_estimate=cost(2 * tokens_in.shape[0] * width * width),
-    )(heads, gathered, tokens_in, gain.reshape(1, width))
+    )(member.reshape(1), heads, *quarters, tokens_in, gain.reshape(1, width))
 
 
 def mlp_body(first_ref, second_ref, gathered_ref, out_first_ref, out_second_ref, weight_ref, sems):
@@ -473,11 +513,12 @@
     half = lax.axis_index("row") % PAIR
     half_width = model_width // PAIR
     half_patch = lax.dynamic_slice_in_dim(patch_weight, half * half_width, half_width, 1)
+    out_here = w_out.shape[0] // TEAM
+    out_quarter = lax.dynamic_slice_in_dim(w_out, member * out_here, out_here, 0)
     first_shard = jnp.concatenate(
-        [half_patch, w_out[:, :half_width], w_out[:, half_width:]], axis=0
+        [half_patch, out_quarter[:, :half_width], out_quarter[:, half_width:]], axis=0
     )
     first_weights = lax.all_gather(first_shard, "col", axis=0, tiled=False)
-    first_weights = pltpu.with_memory_space_constraint(first_weights, pltpu.HBM)
     strips, place = image_strips(images, position)
     packed = jnp.concatenate(
         [
@@ -489,14 +530,22 @@
     packed, strips = lax.optimization_barrier((packed, strips))
     cols_here = position.shape[0]
     features = stem_features(strips, images.shape[3], images.shape[4], stem_first, stem_conv)
-    features = pltpu.with_memory_space_constraint(features, pltpu.HBM)
     even = half == 0
-    own, others = embed(half, features, first_weights, place)
+    own, others = embed(
+        half,
+        pltpu.with_memory_space_constraint(features, pltpu.HBM),
+        pltpu.with_memory_space_constraint(first_weights, pltpu.HBM),
+        place,
+    )
     others = lax.ppermute(others, "row", team_pairs(1))
     tokens_in = jnp.concatenate(
         [jnp.where(even, own, others), jnp.where(even, others, own)], axis=1
     )
-    token_rows = tokens_in.shape[0]
+    quarter = first_weights[:, half_patch.shape[0] :]
+    quarter, tokens_in = lax.optimization_barrier((quarter, tokens_in))
+    quarters = [quarter]
+    for step in range(1, TEAM):
+        quarters.append(lax.ppermute(quarter, "row", team_pairs(step)))
     normed = layer_norm(tokens_in.astype(jnp.float32), gain_attn).astype(jnp.bfloat16)
     heads, mark = attended_heads(normed, w_qkv)
     packed, mark = lax.optimization_barrier((packed, mark))
@@ -504,7 +553,7 @@
     gathered = pltpu.with_memory_space_constraint(gathered, pltpu.HBM)
     heads_back = lax.all_to_all(heads, "col", 0, 0, tiled=True)
     after, normed_mlp = out_projection(
-        heads_back.reshape(-1, token_rows), first_weights, tokens_in, gain_mlp
+        member, heads_back, quarters, tokens_in, gain_mlp
     )
     near, far, farthest = (lax.ppermute(normed_mlp, "row", team_pairs(i)) for i in (1, 2, 3))
     own_term, near_term = mlp_terms(normed_mlp, near, gathered, jnp.float32)

time: 187 us -> 186 us (level); the launches traced: 185 us -> 186 us
  waiting for transfers between devices: 71.4 us -> 63.1 us
  local copies, waits for them, and re-layouts: 10 us -> 16 us
  starting transfers between devices: 41.2 us -> 46.6 us
  matrix products: 6.92 us -> 3.45 us
    all_to_all x1, waiting for transfers between devices: 13.5 us -> 8.69 us  [on_device(): heads_back = lax.all_to_all(heads, 'col', 0, 0, tiled=True)]
    unnamed x30 -> x40, local copies, waits for them, and re-layouts: 6.29 us -> 10.3 us
    ppermute x0 -> x3, starting transfers between devices: none -> 3.49 us  [on_device(): quarters.append(lax.ppermute(quarter, 'row', team_pairs(step)))]
    dot_general x6 -> x2, matrix products: 6.92 us -> 3.45 us  [first_of(): jnp.einsum(spec, values, stem_first[:, start:start + lanes], preferred_el...]
    pallas_call x3, Pallas kernels: 24.2 us -> 26.9 us  [the longest x1 12.3 us: attended_heads(): heads(lax.axis_index('col').reshape(1), weight, pltpu.with_memory_space_c...]
    ppermute x0 -> x3, waiting for transfers between devices: none -> 2.32 us  [on_device(): quarters.append(lax.ppermute(quarter, 'row', team_pairs(step)))]
  transfers between devices with their start and end apart: 28 -> 31, of which waited for: 15 -> 14; matrix products, arithmetic and copies ran while one was open for 7% -> 6% of each run, Pallas kernels for 16% -> 17%
where the time goes in v1:
time: 186 us
  waiting for transfers between devices  63.1 us (34%)
  starting transfers between devices  46.6 us (25%)
  Pallas kernels  38.4 us (21%)
  local copies, waits for them, and re-layouts  16 us (9%)
  between operations  13.9 us (7%)
  other arithmetic  4.04 us (2%)
  matrix products  3.45 us (2%)
    ppermute x7, waiting for transfers between devices, moved(): lax.ppermute(value, 'col', [(i, (i + step) % count) for i in range(count)])  20.5 us
    ppermute x7, starting transfers between devices, moved(): lax.ppermute(value, 'col', [(i, (i + step) % count) for i in range(count)])  17.9 us
    pallas_call x1, Pallas kernels, attended_heads(): heads(lax.axis_index('col').reshape(1), weight, pltpu.with_memory_space_c...  12.3 us
    pallas_call x1, Pallas kernels, stem_features(): pl.pallas_call(functools.partial(stem_body, len(starts)), out_shape=pltpu...  12.2 us
    all_to_all x1, waiting for transfers between devices, image_strips(): incoming = lax.all_to_all(outgoing, ('section', 'row'), 0, 0, tiled=True)  10.9 us
    unnamed x40, local copies, waits for them, and re-layouts  10.3 us
    ppermute x2, waiting for transfers between devices, on_device(): lax.ppermute(term, 'row', team_pairs(step)).astype(jnp.float32)  9.44 us
    all_to_all x1, waiting for transfers between devices, on_device(): heads_back = lax.all_to_all(heads, 'col', 0, 0, tiled=True)  8.69 us
  transfers between devices with their start and end apart: 31, of which 14 were waited for; matrix products, arithmetic and copies ran while one was open for 6% of the time, Pallas kernels for 17%

profile of v1, /device:TPU:2, one launch (start us, length us, event | category | flops | bytes accessed | tf_op | source)
XLA Modules:
  0.0 185.6 jit_solution(5226072110607126767)
XLA Ops:
  6.5 1.0 copy-done
  7.6 0.7 constant_dynamic-slice_fusion
  8.3 0.8 pad_maximum_fusion
  9.3 1.4 copy.27
  10.7 0.2 broadcast_in_dim.47
  11.2 1.0 bitcast_select_fusion
  12.3 7.5 %all-to-all-start = ((bf16[16,96,256]{2,1,0:T(8,128)(2,1)}), bf16[16,96,256]{2,1,0:T(8,128)(2,1)S(1)}, u32[]{:S(2)}, u32[]{:S(2)}) async-start(bf16[16,96,256]{2,1,0:T(8,128)(2,1)} %bitcast_select_fusion), calls=%async_computation | async-start | bytes 1572864 | tf_op jit(solution)/shard_map/all_to_all | solution.py:49
  20.1 0.9 constant_dynamic-slice_fusion.3
  21.1 0.7 pad_maximum_fusion.1
  21.8 10.9 %all-to-all-done = bf16[16,96,256]{2,1,0:T(8,128)(2,1)S(1)} async-done(((bf16[16,96,256]{2,1,0:T(8,128)(2,1)}), bf16[16,96,256]{2,1,0:T(8,128)(2,1)S(1)}, u32[]{:S(2)}, u32[]{:S(2)}) %all-to-all-start) | async-done | bytes 786464 | tf_op jit(solution)/shard_map/all_to_all | solution.py:49
  32.8 0.9 copy-done.14
  33.7 0.5 copy.31
  34.5 1.3 collective-permute-start
  35.9 1.3 collective-permute-start.1
  37.2 1.7 maximum_reduce-precision_fusion.1
  38.9 1.7 maximum_reduce-precision_fusion
  40.7 1.0 constant_dynamic-slice_fusion.1
  42.0 1.6 copy-done.1
  43.6 12.2 %shard_map.109.features_ref = bf16[256,4096]{1,0:T(8,128)(2,1)} custom-call(f32[2,2048,128]{2,1,0:T(8,128)S(1)} %bitcast.49, f32[2,2048,128]{2,1,0:T(8,128)S(1)} %bitcast.50, bf16[48,256]{1,0:T(8,128)(2,1)S(1)} %collective-permute-done.refs_2_, bf16[48,256]{1,0:T(8,128)(2,1)S(1)} %collective-permute-done.1.refs_3_, bf16[48,256]{1,0:T(8,128)(2,1)S(1)} %copy-done.6, ...), custom_call_target="tpu_custom_call" | custom-call | flops 4831838208 | bytes 18874368 | tf_op jit(solution)/shard_map/pallas_call | solution.py:206
  55.8 3.3 %shard_map.110 = (bf16[128,512]{1,0:T(8,128)(2,1)S(1)}, bf16[128,512]{1,0:T(8,128)(2,1)S(1)}) custom-call(s32[1]{0:T(128)} %bitcast.4.half_ref, bf16[256,4096]{1,0:T(8,128)(2,1)} %shard_map.109.features_ref, bf16[16,288,512]{2,1,0:T(8,128)(2,1)} %bitcast.57, bf16[4,32,512]{2,1,0:T(8,128)(2,1)S(1)} %reshape.81.place_ref), custom_call_target="tpu_custom_call" | custom-call | flops 1073741824 | bytes 4194304 | tf_op jit(solution)/shard_map/pallas_call | solution.py:407
  59.2 1.6 collective-permute-start.2
  60.8 1.1 slice.28.refs_0_
  61.9 2.4 %collective-permute-done.2 = bf16[128,512]{1,0:T(8,128)(2,1)S(1)} collective-permute-done((bf16[128,512]{1,0:T(8,128)(2,1)S(1)}, bf16[128,512]{1,0:T(8,128)(2,1)S(1)}, u32[]{:S(2)}, u32[]{:S(2)}) %collective-permute-start.2) | collective-permute-done | bytes 131104 | tf_op jit(solution)/shard_map/ppermute | solution.py:540
  64.7 0.2 fusion.4.refs_0_
  64.9 5.7 %collective-permute-start.3 = (bf16[128,1024]{1,0:T(8,128)(2,1)S(1)}, bf16[128,1024]{1,0:T(8,128)(2,1)S(1)}, u32[]{:S(2)}, u32[]{:S(2)}) collective-permute-start(bf16[128,1024]{1,0:T(8,128)(2,1)S(1)} %fusion.4.refs_0_), channel_id=1, source_target_pairs={{0,2},{1,3},{2,4},{3,5},{4,6},{5,7},{6,8},{7,9},{8,10},{9,11},{10,... | collective-permute-start | bytes 786440 | tf_op jit(solution)/shard_map/ppermute | solution.py:63
  70.7 3.3 %collective-permute-start.5 = (bf16[128,1024]{1,0:T(8,128)(2,1)S(1)}, bf16[128,1024]{1,0:T(8,128)(2,1)S(1)}, u32[]{:S(2)}, u32[]{:S(2)}) collective-permute-start(bf16[128,1024]{1,0:T(8,128)(2,1)S(1)} %fusion.4.refs_0_), channel_id=1, source_target_pairs={{0,14},{1,15},{2,0},{3,1},{4,2},{5,3},{6,4},{7,5},{8,6},{9,7},{10,... | collective-permute-start | bytes 786440 | tf_op jit(solution)/shard_map/ppermute | solution.py:63
  73.9 4.3 %collective-permute-done.3.refs_4_ = bf16[128,1024]{1,0:T(8,128)(2,1)S(1)} collective-permute-done((bf16[128,1024]{1,0:T(8,128)(2,1)S(1)}, bf16[128,1024]{1,0:T(8,128)(2,1)S(1)}, u32[]{:S(2)}, u32[]{:S(2)}) %collective-permute-start.3) | collective-permute-done | bytes 262176 | tf_op jit(solution)/shard_map/ppermute | solution.py:63
  78.3 3.2 %collective-permute-start.6 = (bf16[128,1024]{1,0:T(8,128)(2,1)S(1)}, bf16[128,1024]{1,0:T(8,128)(2,1)S(1)}, u32[]{:S(2)}, u32[]{:S(2)}) collective-permute-start(bf16[128,1024]{1,0:T(8,128)(2,1)S(1)} %collective-permute-done.5.refs_5_), channel_id=1, source_target_pairs={{0,14},{1,15},{2,0},{3,1},{4,2},{5,3},{6,4},{7,5},{8,6},{9,7},{10,... | collective-permute-start | bytes 786440 | tf_op jit(solution)/shard_map/ppermute | solution.py:63
  81.5 0.5 collective-permute-start.10
  82.0 3.7 %collective-permute-done.4.refs_8_ = bf16[128,1024]{1,0:T(8,128)(2,1)S(1)} collective-permute-done((bf16[128,1024]{1,0:T(8,128)(2,1)S(1)}, bf16[128,1024]{1,0:T(8,128)(2,1)S(1)}, u32[]{:S(2)}, u32[]{:S(2)}) %collective-permute-start.4) | collective-permute-done | bytes 262176 | tf_op jit(solution)/shard_map/ppermute | solution.py:63
  85.8 1.4 collective-permute-done.6.refs_9_
  87.2 2.1 %collective-permute-start.7 = (bf16[128,1024]{1,0:T(8,128)(2,1)S(1)}, bf16[128,1024]{1,0:T(8,128)(2,1)S(1)}, u32[]{:S(2)}, u32[]{:S(2)}) collective-permute-start(bf16[128,1024]{1,0:T(8,128)(2,1)S(1)} %collective-permute-done.4.refs_8_), channel_id=1, source_target_pairs={{0,2},{1,3},{2,4},{3,5},{4,6},{5,7},{6,8},{7,9},{8,10},{9,11},{10,... | collective-permute-start | bytes 786440 | tf_op jit(solution)/shard_map/ppermute | solution.py:63
  89.3 1.1 collective-permute-start.8
  90.4 2.5 %shard_map.111 = (bf16[1280,128]{1,0:T(8,128)(2,1)}, bf16[64,1280]{1,0:T(8,128)(2,1)}) custom-call(bf16[3,64,1024]{2,1,0:T(8,128)(2,1)S(1)} %bitcast.51, bf16[128,1024]{1,0:T(8,128)(2,1)S(1)} %fusion.4.refs_0_, bf16[128,1024]{1,0:T(8,128)(2,1)S(1)} %collective-permute-done.9.refs_1_, bf16[128,1024]{1,0:T(8,128)(2,1)S(1)} %collective-permute-done.10.refs_2_, ...), custom_call_target="tpu_custom_call" | custom-call | flops 503316480 | bytes 1966080 | tf_op jit(solution)/shard_map/pallas_call | solution.py:311
  92.9 4.2 %collective-permute-done.7.refs_2_ = bf16[128,1024]{1,0:T(8,128)(2,1)S(1)} collective-permute-done((bf16[128,1024]{1,0:T(8,128)(2,1)S(1)}, bf16[128,1024]{1,0:T(8,128)(2,1)S(1)}, u32[]{:S(2)}, u32[]{:S(2)}) %collective-permute-start.7) | collective-permute-done | bytes 262176 | tf_op jit(solution)/shard_map/ppermute | solution.py:63
  97.1 0.7 collective-permute-done.8.refs_3_
  97.8 2.3 %collective-permute-start.16 = (bf16[128,1024]{1,0:T(8,128)(2,1)S(1)}, bf16[128,1024]{1,0:T(8,128)(2,1)}, u32[]{:S(2)}, u32[]{:S(2)}) collective-permute-start(bf16[128,1024]{1,0:T(8,128)(2,1)S(1)} %collective-permute-done.7.refs_2_), channel_id=1, source_target_pairs={{0,2},{1,3},{2,4},{3,5},{4,6},{5,7},{6,8},{7,9},{8,10},{9,11},{10,... | collective-permute-start | bytes 786440 | tf_op jit(solution)/shard_map/ppermute | solution.py:63
  100.2 0.5 collective-permute-start.15
  100.7 6.1 %collective-permute-done.16.refs_4_ = bf16[128,1024]{1,0:T(8,128)(2,1)} collective-permute-done((bf16[128,1024]{1,0:T(8,128)(2,1)S(1)}, bf16[128,1024]{1,0:T(8,128)(2,1)}, u32[]{:S(2)}, u32[]{:S(2)}) %collective-permute-start.16) | collective-permute-done | bytes 262176 | tf_op jit(solution)/shard_map/ppermute | solution.py:63
  106.8 1.5 collective-permute-start.18
  108.4 0.7 copy-done.10
  109.1 1.9 %collective-permute-start.20 = (bf16[16,32,512]{2,1,0:T(8,128)(2,1)S(1)}, bf16[16,32,512]{2,1,0:T(8,128)(2,1)S(1)}, u32[]{:S(2)}, u32[]{:S(2)}) collective-permute-start(bf16[16,32,512]{2,1,0:T(8,128)(2,1)S(1)} %slice.28.refs_0_), channel_id=1, source_target_pairs={{0,48},{16,32},{32,16},{48,0},{64,112},{80,96},{96,80},{112,64},{1... | collective-permute-start | bytes 1572872 | tf_op jit(solution)/shard_map/ppermute | solution.py:548
  111.0 0.9 copy-done.9
  112.0 0.9 copy-done.11
  112.9 12.3 %shard_map.112 = bf16[16,64,128]{2,1,0:T(8,128)(2,1)S(1)} custom-call(s32[1]{0:T(128)} %bitcast.1.place_ref, bf16[3,64,1024]{2,1,0:T(8,128)(2,1)S(1)} %bitcast.52, bf16[1280,128]{1,0:T(8,128)(2,1)} %get-tuple-element.41.qv_ref, bf16[64,1280]{1,0:T(8,128)(2,1)} %get-tuple-element.42.early_key_ref, bf16[128,1024]{1,0:T(8,128)(2,1)S(1)} %copy-done.11, ...), custom_call_target="tpu_custom_call" | custom-call | flops 4294967296 | bytes 16777216 | tf_op jit(solution)/shard_map/pallas_call | solution.py:351
  125.2 0.7 copy-done.5
  125.9 5.4 %all-to-all-start.1 = ((bf16[16,64,128]{2,1,0:T(8,128)(2,1)}), bf16[16,64,128]{2,1,0:T(8,128)(2,1)S(1)}, u32[]{:S(2)}, u32[]{:S(2)}) async-start(bf16[16,64,128]{2,1,0:T(8,128)(2,1)} %copy-done.5), calls=%async_computation.1 | async-start | bytes 524288 | tf_op jit(solution)/shard_map/all_to_all | solution.py:554
  131.3 2.3 %collective-permute-done.19.refs_2_ = bf16[16,32,512]{2,1,0:T(8,128)(2,1)S(1)} collective-permute-done((bf16[16,32,512]{2,1,0:T(8,128)(2,1)S(1)}, bf16[16,32,512]{2,1,0:T(8,128)(2,1)S(1)}, u32[]{:S(2)}, u32[]{:S(2)}) %collective-permute-start.19) | collective-permute-done | bytes 524320 | tf_op jit(solution)/shard_map/ppermute | solution.py:548
  133.7 0.8 copy-done.2
  134.5 8.7 %all-to-all-done.1.heads_ref = bf16[16,64,128]{2,1,0:T(8,128)(2,1)S(1)} async-done(((bf16[16,64,128]{2,1,0:T(8,128)(2,1)}), bf16[16,64,128]{2,1,0:T(8,128)(2,1)S(1)}, u32[]{:S(2)}, u32[]{:S(2)}) %all-to-all-start.1) | async-done | bytes 262176 | tf_op jit(solution)/shard_map/all_to_all | solution.py:554
  143.2 1.0 copy-done.3
  144.2 0.7 shard_map.113
  144.9 1.1 collective-permute-start.21
  146.0 2.4 %collective-permute-start.23 = (bf16[128,1024]{1,0:T(8,128)(2,1)S(1)}, bf16[128,1024]{1,0:T(8,128)(2,1)S(1)}, u32[]{:S(2)}, u32[]{:S(2)}) collective-permute-start(bf16[128,1024]{1,0:T(8,128)(2,1)S(1)} %get-tuple-element.47.first_ref), channel_id=1, source_target_pairs={{0,48},{16,32},{32,16},{48,0},{64,112},{80,96},{96,80},{112,64},{1... | collective-permute-start | bytes 786440 | tf_op jit(solution)/shard_map/ppermute | solution.py:558
  148.5 5.7 %collective-permute-done.21.second_ref = bf16[128,1024]{1,0:T(8,128)(2,1)S(1)} collective-permute-done((bf16[128,1024]{1,0:T(8,128)(2,1)S(1)}, bf16[128,1024]{1,0:T(8,128)(2,1)S(1)}, u32[]{:S(2)}, u32[]{:S(2)}) %collective-permute-start.21) | collective-permute-done | bytes 262176 | tf_op jit(solution)/shard_map/ppermute | solution.py:558
  154.2 3.7 %shard_map.114 = (f32[128,1024]{1,0:T(8,128)S(1)}, bf16[128,1024]{1,0:T(8,128)(2,1)S(1)}) custom-call(bf16[128,1024]{1,0:T(8,128)(2,1)S(1)} %get-tuple-element.47.first_ref, bf16[128,1024]{1,0:T(8,128)(2,1)S(1)} %collective-permute-done.21.second_ref, bf16[16,128,1024]{2,1,0:T(8,128)(2,1)} %bitcast.54), custom_call_target="tpu_custom_call" | custom-call | flops 1073741824 | bytes 4194304 | tf_op jit(solution)/shard_map/pallas_call | solution.py:480
  157.9 1.9 %collective-permute-done.22.first_ref = bf16[128,1024]{1,0:T(8,128)(2,1)S(1)} collective-permute-done((bf16[128,1024]{1,0:T(8,128)(2,1)S(1)}, bf16[128,1024]{1,0:T(8,128)(2,1)S(1)}, u32[]{:S(2)}, u32[]{:S(2)}) %collective-permute-start.22) | collective-permute-done | bytes 262176 | tf_op jit(solution)/shard_map/ppermute | solution.py:558
  159.8 3.8 %shard_map.115 = (bf16[128,1024]{1,0:T(8,128)(2,1)S(1)}, bf16[128,1024]{1,0:T(8,128)(2,1)S(1)}) custom-call(bf16[128,1024]{1,0:T(8,128)(2,1)S(1)} %collective-permute-done.22.first_ref, bf16[128,1024]{1,0:T(8,128)(2,1)S(1)} %collective-permute-done.23.second_ref, bf16[16,128,1024]{2,1,0:T(8,128)(2,1)} %bitcast.55), custom_call_target="tpu_custom_call" | custom-call | flops 1073741824 | bytes 4194304 | tf_op jit(solution)/shard_map/pallas_call | solution.py:480
  163.6 0.7 collective-permute-start.25
  164.3 1.8 collective-permute-start.26
  166.1 1.1 collective-permute-start.24
  167.2 9.4 %collective-permute-done.25 = bf16[128,1024]{1,0:T(8,128)(2,1)S(1)} collective-permute-done((bf16[128,1024]{1,0:T(8,128)(2,1)S(1)}, bf16[128,1024]{1,0:T(8,128)(2,1)S(1)}, u32[]{:S(2)}, u32[]{:S(2)}) %collective-permute-start.25) | collective-permute-done | bytes 262176 | tf_op jit(solution)/shard_map/ppermute | solution.py:565
  176.6 1.2 collective-permute-done.24
  177.8 0.9 add_convert_fusion
  (83 shorter events, 2.2 us)
Async XLA Ops:
  6.5 1.0 copy-start
  6.5 4.6 %copy-start.16 = (bf16[4,4,1024]{2,1,0:T(4,128)(2,1)S(1)}, bf16[4,4,1024]{2,1,0:T(4,128)(2,1)}, u32[]{:S(2)}) copy-start(bf16[4,4,1024]{2,1,0:T(4,128)(2,1)} %param.15) | copy-start | bytes 98308
  6.5 49.3 %all-gather.5.cloned.1.call-start = ((), (), s32[]{:S(2)}) async-start(), calls=%async_computation.2 | async-start | bytes 5013504 | tf_op jit(solution)/shard_map/all_gather | solution.py:521
  11.0 8.9 %copy-start.15 = (bf16[1024,256]{1,0:T(8,128)(2,1)S(1)}, bf16[1024,256]{1,0:T(8,128)(2,1)}, u32[]{:S(2)}) copy-start(bf16[1024,256]{1,0:T(8,128)(2,1)} %param.20) | copy-start | bytes 1572868
  12.3 20.5 %all-to-all-start = ((bf16[16,96,256]{2,1,0:T(8,128)(2,1)}), bf16[16,96,256]{2,1,0:T(8,128)(2,1)S(1)}, u32[]{:S(2)}, u32[]{:S(2)}) async-start(bf16[16,96,256]{2,1,0:T(8,128)(2,1)} %bitcast_select_fusion), calls=%async_computation | async-start | bytes 1572864 | tf_op jit(solution)/shard_map/all_to_all | solution.py:49
  19.7 134.4 %all-gather.7.cloned.1.call-start = ((), (), s32[]{:S(2)}) async-start(), calls=%async_computation.3 | async-start | bytes 4456448 | tf_op jit(solution)/shard_map/all_gather | solution.py:552
  20.1 17.1 %copy-start.6 = (bf16[48,256]{1,0:T(8,128)(2,1)S(1)}, bf16[48,256]{1,0:T(8,128)(2,1)}, u32[]{:S(2)}) copy-start(bf16[48,256]{1,0:T(8,128)(2,1)} %refs_4_.1) | copy-start | bytes 73732
  32.7 0.9 copy-start.14
  34.1 1.8 copy-start.12
  34.5 7.5 %collective-permute-start = (bf16[48,256]{1,0:T(8,128)(2,1)S(1)}, bf16[48,256]{1,0:T(8,128)(2,1)S(1)}, u32[]{:S(2)}, u32[]{:S(2)}) collective-permute-start(bf16[48,256]{1,0:T(8,128)(2,1)S(1)} %copy.32), channel_id=1, source_target_pairs={{0,1},{1,2},{2,3},{3,4},{4,5},{5,6},{6,7},{7,8},{8,9},{9,10},{10,1... | collective-permute-start | bytes 73736 | tf_op jit(solution)/shard_map/ppermute | solution.py:191
  35.9 6.1 %collective-permute-start.1 = (bf16[48,256]{1,0:T(8,128)(2,1)S(1)}, bf16[48,256]{1,0:T(8,128)(2,1)S(1)}, u32[]{:S(2)}, u32[]{:S(2)}) collective-permute-start(bf16[48,256]{1,0:T(8,128)(2,1)S(1)} %copy.33), channel_id=1, source_target_pairs={{1,0},{2,1},{3,2},{4,3},{5,4},{6,5},{7,6},{8,7},{9,8},{10,9},{11,1... | collective-permute-start | bytes 73736 | tf_op jit(solution)/shard_map/ppermute | solution.py:192
  37.2 1.7 copy-start.13
  42.0 1.6 copy-start.1
  59.2 5.5 %copy-start.17 = (f32[1024]{0:T(1024)S(1)}, f32[1024]{0:T(1024)}, u32[]{:S(2)}) copy-start(f32[1024]{0:T(1024)} %param.16) | copy-start | bytes 12292
  59.2 31.2 %copy-start.4 = (bf16[3,1024,64]{1,2,0:T(8,128)(2,1)S(1)}, bf16[3,1024,64]{1,2,0:T(8,128)(2,1)}, u32[]{:S(2)}) copy-start(bf16[3,1024,64]{1,2,0:T(8,128)(2,1)} %param.17) | copy-start | bytes 1179652
  59.2 5.1 %collective-permute-start.2 = (bf16[128,512]{1,0:T(8,128)(2,1)S(1)}, bf16[128,512]{1,0:T(8,128)(2,1)S(1)}, u32[]{:S(2)}, u32[]{:S(2)}) collective-permute-start(bf16[128,512]{1,0:T(8,128)(2,1)S(1)} %get-tuple-element.33), channel_id=1, source_target_pairs={{0,16},{16,0},{32,48},{48,32},{64,80},{80,64},{96,112},{112,96},{1... | collective-permute-start | bytes 393224 | tf_op jit(solution)/shard_map/ppermute | solution.py:540
  64.9 13.3 %collective-permute-start.3 = (bf16[128,1024]{1,0:T(8,128)(2,1)S(1)}, bf16[128,1024]{1,0:T(8,128)(2,1)S(1)}, u32[]{:S(2)}, u32[]{:S(2)}) collective-permute-start(bf16[128,1024]{1,0:T(8,128)(2,1)S(1)} %fusion.4.refs_0_), channel_id=1, source_target_pairs={{0,2},{1,3},{2,4},{3,5},{4,6},{5,7},{6,8},{7,9},{8,10},{9,11},{10,... | collective-permute-start | bytes 786440 | tf_op jit(solution)/shard_map/ppermute | solution.py:63
  70.7 7.7 %collective-permute-start.5 = (bf16[128,1024]{1,0:T(8,128)(2,1)S(1)}, bf16[128,1024]{1,0:T(8,128)(2,1)S(1)}, u32[]{:S(2)}, u32[]{:S(2)}) collective-permute-start(bf16[128,1024]{1,0:T(8,128)(2,1)S(1)} %fusion.4.refs_0_), channel_id=1, source_target_pairs={{0,14},{1,15},{2,0},{3,1},{4,2},{5,3},{6,4},{7,5},{8,6},{9,7},{10,... | collective-permute-start | bytes 786440 | tf_op jit(solution)/shard_map/ppermute | solution.py:63
  78.2 7.6 %collective-permute-start.4 = (bf16[128,1024]{1,0:T(8,128)(2,1)S(1)}, bf16[128,1024]{1,0:T(8,128)(2,1)S(1)}, u32[]{:S(2)}, u32[]{:S(2)}) collective-permute-start(bf16[128,1024]{1,0:T(8,128)(2,1)S(1)} %collective-permute-done.3.refs_4_), channel_id=1, source_target_pairs={{0,2},{1,3},{2,4},{3,5},{4,6},{5,7},{6,8},{7,9},{8,10},{9,11},{10,... | collective-permute-start | bytes 786440 | tf_op jit(solution)/shard_map/ppermute | solution.py:63
  78.3 8.8 %collective-permute-start.6 = (bf16[128,1024]{1,0:T(8,128)(2,1)S(1)}, bf16[128,1024]{1,0:T(8,128)(2,1)S(1)}, u32[]{:S(2)}, u32[]{:S(2)}) collective-permute-start(bf16[128,1024]{1,0:T(8,128)(2,1)S(1)} %collective-permute-done.5.refs_5_), channel_id=1, source_target_pairs={{0,14},{1,15},{2,0},{3,1},{4,2},{5,3},{6,4},{7,5},{8,6},{9,7},{10,... | collective-permute-start | bytes 786440 | tf_op jit(solution)/shard_map/ppermute | solution.py:63
  81.5 5.7 %collective-permute-start.9 = (bf16[128,1024]{1,0:T(8,128)(2,1)S(1)}, bf16[128,1024]{1,0:T(8,128)(2,1)S(1)}, u32[]{:S(2)}, u32[]{:S(2)}) collective-permute-start(bf16[128,1024]{1,0:T(8,128)(2,1)S(1)} %fusion.4.refs_0_), channel_id=1, source_target_pairs={{0,1},{1,0},{2,3},{3,2},{4,5},{5,4},{6,7},{7,6},{8,9},{9,8},{10,11... | collective-permute-start | bytes 786440 | tf_op jit(solution)/shard_map/ppermute | solution.py:67
  81.5 7.8 %collective-permute-start.10 = (bf16[128,1024]{1,0:T(8,128)(2,1)S(1)}, bf16[128,1024]{1,0:T(8,128)(2,1)S(1)}, u32[]{:S(2)}, u32[]{:S(2)}) collective-permute-start(bf16[128,1024]{1,0:T(8,128)(2,1)S(1)} %collective-permute-done.3.refs_4_), channel_id=1, source_target_pairs={{0,1},{1,0},{2,3},{3,2},{4,5},{5,4},{6,7},{7,6},{8,9},{9,8},{10,11... | collective-permute-start | bytes 786440 | tf_op jit(solution)/shard_map/ppermute | solution.py:67
  82.0 8.4 %collective-permute-start.11 = (bf16[128,1024]{1,0:T(8,128)(2,1)S(1)}, bf16[128,1024]{1,0:T(8,128)(2,1)S(1)}, u32[]{:S(2)}, u32[]{:S(2)}) collective-permute-start(bf16[128,1024]{1,0:T(8,128)(2,1)S(1)} %collective-permute-done.5.refs_5_), channel_id=1, source_target_pairs={{0,1},{1,0},{2,3},{3,2},{4,5},{5,4},{6,7},{7,6},{8,9},{9,8},{10,11... | collective-permute-start | bytes 786440 | tf_op jit(solution)/shard_map/ppermute | solution.py:67
  85.8 4.7 %collective-permute-start.12 = (bf16[128,1024]{1,0:T(8,128)(2,1)S(1)}, bf16[128,1024]{1,0:T(8,128)(2,1)S(1)}, u32[]{:S(2)}, u32[]{:S(2)}) collective-permute-start(bf16[128,1024]{1,0:T(8,128)(2,1)S(1)} %collective-permute-done.4.refs_8_), channel_id=1, source_target_pairs={{0,1},{1,0},{2,3},{3,2},{4,5},{5,4},{6,7},{7,6},{8,9},{9,8},{10,11... | collective-permute-start | bytes 786440 | tf_op jit(solution)/shard_map/ppermute | solution.py:67
  87.2 3.3 %collective-permute-start.13 = (bf16[128,1024]{1,0:T(8,128)(2,1)S(1)}, bf16[128,1024]{1,0:T(8,128)(2,1)S(1)}, u32[]{:S(2)}, u32[]{:S(2)}) collective-permute-start(bf16[128,1024]{1,0:T(8,128)(2,1)S(1)} %collective-permute-done.6.refs_9_), channel_id=1, source_target_pairs={{0,1},{1,0},{2,3},{3,2},{4,5},{5,4},{6,7},{7,6},{8,9},{9,8},{10,11... | collective-permute-start | bytes 786440 | tf_op jit(solution)/shard_map/ppermute | solution.py:67
  87.2 9.9 %collective-permute-start.7 = (bf16[128,1024]{1,0:T(8,128)(2,1)S(1)}, bf16[128,1024]{1,0:T(8,128)(2,1)S(1)}, u32[]{:S(2)}, u32[]{:S(2)}) collective-permute-start(bf16[128,1024]{1,0:T(8,128)(2,1)S(1)} %collective-permute-done.4.refs_8_), channel_id=1, source_target_pairs={{0,2},{1,3},{2,4},{3,5},{4,6},{5,7},{6,8},{7,9},{8,10},{9,11},{10,... | collective-permute-start | bytes 786440 | tf_op jit(solution)/shard_map/ppermute | solution.py:63
  89.3 8.5 %collective-permute-start.8 = (bf16[128,1024]{1,0:T(8,128)(2,1)S(1)}, bf16[128,1024]{1,0:T(8,128)(2,1)}, u32[]{:S(2)}, u32[]{:S(2)}) collective-permute-start(bf16[128,1024]{1,0:T(8,128)(2,1)S(1)} %collective-permute-done.6.refs_9_), channel_id=1, source_target_pairs={{0,14},{1,15},{2,0},{3,1},{4,2},{5,3},{6,4},{7,5},{8,6},{9,7},{10,... | collective-permute-start | bytes 786440 | tf_op jit(solution)/shard_map/ppermute | solution.py:63
  97.1 13.9 %copy-start.8 = (bf16[128,1024]{1,0:T(8,128)(2,1)}, bf16[128,1024]{1,0:T(8,128)(2,1)S(1)}, u32[]{:S(2)}) copy-start(bf16[128,1024]{1,0:T(8,128)(2,1)S(1)} %collective-permute-done.7.refs_2_) | copy-start | bytes 786436
  97.8 9.0 %collective-permute-start.16 = (bf16[128,1024]{1,0:T(8,128)(2,1)S(1)}, bf16[128,1024]{1,0:T(8,128)(2,1)}, u32[]{:S(2)}, u32[]{:S(2)}) collective-permute-start(bf16[128,1024]{1,0:T(8,128)(2,1)S(1)} %collective-permute-done.7.refs_2_), channel_id=1, source_target_pairs={{0,2},{1,3},{2,4},{3,5},{4,6},{5,7},{6,8},{7,9},{8,10},{9,11},{10,... | collective-permute-start | bytes 786440 | tf_op jit(solution)/shard_map/ppermute | solution.py:63
  100.2 8.2 %collective-permute-start.14 = (bf16[128,1024]{1,0:T(8,128)(2,1)S(1)}, bf16[128,1024]{1,0:T(8,128)(2,1)S(1)}, u32[]{:S(2)}, u32[]{:S(2)}) collective-permute-start(bf16[128,1024]{1,0:T(8,128)(2,1)S(1)} %collective-permute-done.7.refs_2_), channel_id=1, source_target_pairs={{0,1},{1,0},{2,3},{3,2},{4,5},{5,4},{6,7},{7,6},{8,9},{9,8},{10,11... | collective-permute-start | bytes 786440 | tf_op jit(solution)/shard_map/ppermute | solution.py:67
  100.2 10.8 %collective-permute-start.15 = (bf16[128,1024]{1,0:T(8,128)(2,1)}, bf16[128,1024]{1,0:T(8,128)(2,1)}, u32[]{:S(2)}, u32[]{:S(2)}) collective-permute-start(bf16[128,1024]{1,0:T(8,128)(2,1)} %collective-permute-done.8.refs_3_), channel_id=1, source_target_pairs={{0,1},{1,0},{2,3},{3,2},{4,5},{5,4},{6,7},{7,6},{8,9},{9,8},{10,11... | collective-permute-start | bytes 786440 | tf_op jit(solution)/shard_map/ppermute | solution.py:67
  106.8 4.2 %collective-permute-start.17 = (bf16[128,1024]{1,0:T(8,128)(2,1)}, bf16[128,1024]{1,0:T(8,128)(2,1)}, u32[]{:S(2)}, u32[]{:S(2)}) collective-permute-start(bf16[128,1024]{1,0:T(8,128)(2,1)} %collective-permute-done.16.refs_4_), channel_id=1, source_target_pairs={{0,1},{1,0},{2,3},{3,2},{4,5},{5,4},{6,7},{7,6},{8,9},{9,8},{10,11... | collective-permute-start | bytes 786440 | tf_op jit(solution)/shard_map/ppermute | solution.py:67
  106.8 24.5 %collective-permute-start.18 = (bf16[16,32,512]{2,1,0:T(8,128)(2,1)S(1)}, bf16[16,32,512]{2,1,0:T(8,128)(2,1)S(1)}, u32[]{:S(2)}, u32[]{:S(2)}) collective-permute-start(bf16[16,32,512]{2,1,0:T(8,128)(2,1)S(1)} %slice.28.refs_0_), channel_id=1, source_target_pairs={{0,16},{16,0},{32,48},{48,32},{64,80},{80,64},{96,112},{112,96},{1... | collective-permute-start | bytes 1572872 | tf_op jit(solution)/shard_map/ppermute | solution.py:548
  108.4 25.3 %collective-permute-start.19 = (bf16[16,32,512]{2,1,0:T(8,128)(2,1)S(1)}, bf16[16,32,512]{2,1,0:T(8,128)(2,1)S(1)}, u32[]{:S(2)}, u32[]{:S(2)}) collective-permute-start(bf16[16,32,512]{2,1,0:T(8,128)(2,1)S(1)} %slice.28.refs_0_), channel_id=1, source_target_pairs={{0,32},{16,48},{32,0},{48,16},{64,96},{80,112},{96,64},{112,80},{1... | collective-permute-start | bytes 1572872 | tf_op jit(solution)/shard_map/ppermute | solution.py:548
  108.4 0.7 copy-start.10
  109.1 24.6 %collective-permute-start.20 = (bf16[16,32,512]{2,1,0:T(8,128)(2,1)S(1)}, bf16[16,32,512]{2,1,0:T(8,128)(2,1)S(1)}, u32[]{:S(2)}, u32[]{:S(2)}) collective-permute-start(bf16[16,32,512]{2,1,0:T(8,128)(2,1)S(1)} %slice.28.refs_0_), channel_id=1, source_target_pairs={{0,48},{16,32},{32,16},{48,0},{64,112},{80,96},{96,80},{112,64},{1... | collective-permute-start | bytes 1572872 | tf_op jit(solution)/shard_map/ppermute | solution.py:548
  111.0 1.0 copy-start.9
  112.0 0.9 copy-start.11
  112.9 30.2 %copy-start.7 = (f32[1024]{0:T(1024)S(1)}, f32[1024]{0:T(1024)}, u32[]{:S(2)}) copy-start(f32[1024]{0:T(1024)} %param.19) | copy-start | bytes 12292
  125.2 0.7 copy-start.5
  125.9 17.2 %all-to-all-start.1 = ((bf16[16,64,128]{2,1,0:T(8,128)(2,1)}), bf16[16,64,128]{2,1,0:T(8,128)(2,1)S(1)}, u32[]{:S(2)}, u32[]{:S(2)}) async-start(bf16[16,64,128]{2,1,0:T(8,128)(2,1)} %copy-done.5), calls=%async_computation.1 | async-start | bytes 524288 | tf_op jit(solution)/shard_map/all_to_all | solution.py:554
  133.7 0.8 copy-start.2
  143.2 1.0 copy-start.3
  144.9 9.3 %collective-permute-start.21 = (bf16[128,1024]{1,0:T(8,128)(2,1)S(1)}, bf16[128,1024]{1,0:T(8,128)(2,1)S(1)}, u32[]{:S(2)}, u32[]{:S(2)}) collective-permute-start(bf16[128,1024]{1,0:T(8,128)(2,1)S(1)} %get-tuple-element.47.first_ref), channel_id=1, source_target_pairs={{0,16},{16,0},{32,48},{48,32},{64,80},{80,64},{96,112},{112,96},{1... | collective-permute-start | bytes 786440 | tf_op jit(solution)/shard_map/ppermute | solution.py:558
  146.0 13.8 %collective-permute-start.22 = (bf16[128,1024]{1,0:T(8,128)(2,1)S(1)}, bf16[128,1024]{1,0:T(8,128)(2,1)S(1)}, u32[]{:S(2)}, u32[]{:S(2)}) collective-permute-start(bf16[128,1024]{1,0:T(8,128)(2,1)S(1)} %get-tuple-element.47.first_ref), channel_id=1, source_target_pairs={{0,32},{16,48},{32,0},{48,16},{64,96},{80,112},{96,64},{112,80},{1... | collective-permute-start | bytes 786440 | tf_op jit(solution)/shard_map/ppermute | solution.py:558
  146.0 13.8 %collective-permute-start.23 = (bf16[128,1024]{1,0:T(8,128)(2,1)S(1)}, bf16[128,1024]{1,0:T(8,128)(2,1)S(1)}, u32[]{:S(2)}, u32[]{:S(2)}) collective-permute-start(bf16[128,1024]{1,0:T(8,128)(2,1)S(1)} %get-tuple-element.47.first_ref), channel_id=1, source_target_pairs={{0,48},{16,32},{32,16},{48,0},{64,112},{80,96},{96,80},{112,64},{1... | collective-permute-start | bytes 786440 | tf_op jit(solution)/shard_map/ppermute | solution.py:558
  163.6 13.0 %collective-permute-start.25 = (bf16[128,1024]{1,0:T(8,128)(2,1)S(1)}, bf16[128,1024]{1,0:T(8,128)(2,1)S(1)}, u32[]{:S(2)}, u32[]{:S(2)}) collective-permute-start(bf16[128,1024]{1,0:T(8,128)(2,1)S(1)} %get-tuple-element.55), channel_id=1, source_target_pairs={{0,32},{16,48},{32,0},{48,16},{64,96},{80,112},{96,64},{112,80},{1... | collective-permute-start | bytes 786440 | tf_op jit(solution)/shard_map/ppermute | solution.py:565
  164.3 12.3 %collective-permute-start.26 = (bf16[128,1024]{1,0:T(8,128)(2,1)S(1)}, bf16[128,1024]{1,0:T(8,128)(2,1)S(1)}, u32[]{:S(2)}, u32[]{:S(2)}) collective-permute-start(bf16[128,1024]{1,0:T(8,128)(2,1)S(1)} %get-tuple-element.56), channel_id=1, source_target_pairs={{0,48},{16,32},{32,16},{48,0},{64,112},{80,96},{96,80},{112,64},{1... | collective-permute-start | bytes 786440 | tf_op jit(solution)/shard_map/ppermute | solution.py:565
  166.1 11.8 %collective-permute-start.24 = (bf16[128,1024]{1,0:T(8,128)(2,1)S(1)}, bf16[128,1024]{1,0:T(8,128)(2,1)S(1)}, u32[]{:S(2)}, u32[]{:S(2)}) collective-permute-start(bf16[128,1024]{1,0:T(8,128)(2,1)S(1)} %get-tuple-element.52), channel_id=1, source_target_pairs={{0,16},{16,0},{32,48},{48,32},{64,80},{80,64},{96,112},{112,96},{1... | collective-permute-start | bytes 786440 | tf_op jit(solution)/shard_map/ppermute | solution.py:561
Sparse Core Ops, SparseCore 0:
  9.3 45.3 all-gather.4
  98.0 42.9 all-gather.6

commit v2 on v1

--- a/solution.py
+++ b/solution.py
@@ -1,4 +1,5 @@
 import functools
+import math
 
 import jax
 import jax.numpy as jnp
@@ -89,7 +90,12 @@
     done = early_work(pieces[:-4])
     below, above, done = lax.optimization_barrier((below, above, done))
     pieces[-1] = (True, steps - 1, above)
-    last = moved(below, 2)
+    count = lax.axis_size("col")
+    last = lax.ppermute(
+        jnp.where(lax.axis_index("col") % 2 == 0, below, above),
+        "col",
+        [(i, (i + (2 if i % 2 == 0 else -2)) % count) for i in range(count)],
+    )
     pieces += [(True, steps, last), (False, steps, core_swapped(last))]
     return pieces, done, above
 
@@ -285,7 +291,7 @@
         copy.wait()
 
     block = 2 * tokens
-    scale = HD ** (-0.5)
+    scale = HD ** (-0.5) * math.log2(math.e)
 
     def attend(step, carry):
         for i in range(2):
@@ -294,7 +300,7 @@
                 all_ref[pl.ds(at, block), :], key_ref[...], preferred_element_type=jnp.float32
             )
             peak = jnp.max(scores, axis=-1, keepdims=True)
-            expo = jnp.exp((scores - peak) * scale)
+            expo = jnp.exp2((scores - peak) * scale)
             total = jnp.sum(expo, axis=-1, keepdims=True)
             probs = (expo * (1.0 / total)).astype(jnp.bfloat16)
             mixed = jnp.dot(probs, all_ref[...], preferred_element_type=jnp.float32)

time: 186 us -> 185 us (level)
    ppermute x7 -> x6, waiting for transfers between devices: 20.5 us -> 14.3 us  [moved(): lax.ppermute(value, 'col', [(i, (i + step) % count) for i in range(count)])]
    ppermute x0 -> x1, waiting for transfers between devices: none -> 4.82 us  [ring(): lax.ppermute(jnp.where(lax.axis_index('col') % 2 == 0, below, above), 'co...]
    ppermute x3, waiting for transfers between devices: 2.32 us -> 4.77 us  [on_device(): quarters.append(lax.ppermute(quarter, 'row', team_pairs(step)))]
    ppermute x0 -> x1, starting transfers between devices: none -> 2.33 us  [ring(): lax.ppermute(jnp.where(lax.axis_index('col') % 2 == 0, below, above), 'co...]
    ppermute x7 -> x6, starting transfers between devices: 17.9 us -> 15.6 us  [moved(): lax.ppermute(value, 'col', [(i, (i + step) % count) for i in range(count)])]
    all_to_all x1, waiting for transfers between devices: 8.69 us -> 6.77 us  [on_device(): heads_back = lax.all_to_all(heads, 'col', 0, 0, tiled=True)]
    unnamed x40 -> x36, local copies, waits for them, and re-layouts: 10.3 us -> 8.6 us
where the time goes in v2:
time: 185 us; the launch traced here: 184 us
  waiting for transfers between devices  64.2 us (35%)
  starting transfers between devices  46.6 us (25%)
  Pallas kernels  37.7 us (20%)
  local copies, waits for them, and re-layouts  14.3 us (8%)
  between operations  13.9 us (8%)
  other arithmetic  4.07 us (2%)
  matrix products  3.46 us (2%)
    ppermute x6, starting transfers between devices, moved(): lax.ppermute(value, 'col', [(i, (i + step) % count) for i in range(count)])  15.6 us
    ppermute x6, waiting for transfers between devices, moved(): lax.ppermute(value, 'col', [(i, (i + step) % count) for i in range(count)])  14.3 us
    pallas_call x1, Pallas kernels, stem_features(): pl.pallas_call(functools.partial(stem_body, len(starts)), out_shape=pltpu...  12.2 us
    pallas_call x1, Pallas kernels, attended_heads(): heads(lax.axis_index('col').reshape(1), weight, pltpu.with_memory_space_c...  11.5 us
    all_to_all x1, waiting for transfers between devices, image_strips(): incoming = lax.all_to_all(outgoing, ('section', 'row'), 0, 0, tiled=True)  10.9 us
    ppermute x2, waiting for transfers between devices, on_device(): lax.ppermute(term, 'row', team_pairs(step)).astype(jnp.float32)  10.2 us
    ppermute x3, waiting for transfers between devices, on_device(): lax.ppermute(normed_mlp, 'row', team_pairs(i))  8.62 us
    unnamed x36, local copies, waits for them, and re-layouts  8.6 us
  transfers between devices with their start and end apart: 31, of which 14 were waited for; matrix products, arithmetic and copies ran while one was open for 6% of the time, Pallas kernels for 17%

profile of v2, /device:TPU:2, one launch (start us, length us, event | category | flops | bytes accessed | tf_op | source)
XLA Modules:
  0.0 184.2 jit_solution(16631029765565886935)
XLA Ops:
  6.5 1.0 copy-done
  7.6 0.7 constant_dynamic-slice_fusion
  8.3 0.8 pad_maximum_fusion
  9.3 1.4 copy.27
  10.7 0.2 broadcast_in_dim.47
  11.2 1.0 bitcast_select_fusion
  12.3 7.5 %all-to-all-start = ((bf16[16,96,256]{2,1,0:T(8,128)(2,1)}), bf16[16,96,256]{2,1,0:T(8,128)(2,1)S(1)}, u32[]{:S(2)}, u32[]{:S(2)}) async-start(bf16[16,96,256]{2,1,0:T(8,128)(2,1)} %bitcast_select_fusion), calls=%async_computation | async-start | bytes 1572864 | tf_op jit(solution)/shard_map/all_to_all | solution.py:50
  20.1 0.9 constant_dynamic-slice_fusion.3
  21.1 0.7 pad_maximum_fusion.1
  21.8 10.9 %all-to-all-done = bf16[16,96,256]{2,1,0:T(8,128)(2,1)S(1)} async-done(((bf16[16,96,256]{2,1,0:T(8,128)(2,1)}), bf16[16,96,256]{2,1,0:T(8,128)(2,1)S(1)}, u32[]{:S(2)}, u32[]{:S(2)}) %all-to-all-start) | async-done | bytes 786464 | tf_op jit(solution)/shard_map/all_to_all | solution.py:50
  32.8 0.9 copy-done.12
  33.7 0.5 copy.31
  34.5 1.3 collective-permute-start
  35.9 1.3 collective-permute-start.1
  37.2 1.7 maximum_reduce-precision_fusion.1
  38.9 1.8 maximum_reduce-precision_fusion
  40.7 1.0 constant_dynamic-slice_fusion.1
  42.0 1.6 copy-done.1
  43.6 12.2 %shard_map.109.features_ref = bf16[256,4096]{1,0:T(8,128)(2,1)} custom-call(f32[2,2048,128]{2,1,0:T(8,128)S(1)} %bitcast.49, f32[2,2048,128]{2,1,0:T(8,128)S(1)} %bitcast.50, bf16[48,256]{1,0:T(8,128)(2,1)S(1)} %collective-permute-done.refs_2_, bf16[48,256]{1,0:T(8,128)(2,1)S(1)} %collective-permute-done.1.refs_3_, bf16[48,256]{1,0:T(8,128)(2,1)S(1)} %copy-done.8, ...), custom_call_target="tpu_custom_call" | custom-call | flops 4831838208 | bytes 18874368 | tf_op jit(solution)/shard_map/pallas_call | solution.py:212
  55.8 3.3 %shard_map.110 = (bf16[128,512]{1,0:T(8,128)(2,1)S(1)}, bf16[128,512]{1,0:T(8,128)(2,1)S(1)}) custom-call(s32[1]{0:T(128)} %bitcast.4.half_ref, bf16[256,4096]{1,0:T(8,128)(2,1)} %shard_map.109.features_ref, bf16[16,288,512]{2,1,0:T(8,128)(2,1)} %bitcast.57, bf16[4,32,512]{2,1,0:T(8,128)(2,1)S(1)} %reshape.81.place_ref), custom_call_target="tpu_custom_call" | custom-call | flops 1073741824 | bytes 4194304 | tf_op jit(solution)/shard_map/pallas_call | solution.py:413
  59.2 1.6 collective-permute-start.2
  60.8 1.1 slice.28.refs_0_
  61.9 2.4 %collective-permute-done.2 = bf16[128,512]{1,0:T(8,128)(2,1)S(1)} collective-permute-done((bf16[128,512]{1,0:T(8,128)(2,1)S(1)}, bf16[128,512]{1,0:T(8,128)(2,1)S(1)}, u32[]{:S(2)}, u32[]{:S(2)}) %collective-permute-start.2) | collective-permute-done | bytes 131104 | tf_op jit(solution)/shard_map/ppermute | solution.py:546
  64.4 0.2 fusion.2
  64.7 0.2 fusion.4.refs_0_
  64.9 5.8 %collective-permute-start.3 = (bf16[128,1024]{1,0:T(8,128)(2,1)S(1)}, bf16[128,1024]{1,0:T(8,128)(2,1)S(1)}, u32[]{:S(2)}, u32[]{:S(2)}) collective-permute-start(bf16[128,1024]{1,0:T(8,128)(2,1)S(1)} %fusion.4.refs_0_), channel_id=1, source_target_pairs={{0,2},{1,3},{2,4},{3,5},{4,6},{5,7},{6,8},{7,9},{8,10},{9,11},{10,... | collective-permute-start | bytes 786440 | tf_op jit(solution)/shard_map/ppermute | solution.py:64
  70.7 3.3 %collective-permute-start.5 = (bf16[128,1024]{1,0:T(8,128)(2,1)S(1)}, bf16[128,1024]{1,0:T(8,128)(2,1)S(1)}, u32[]{:S(2)}, u32[]{:S(2)}) collective-permute-start(bf16[128,1024]{1,0:T(8,128)(2,1)S(1)} %fusion.4.refs_0_), channel_id=1, source_target_pairs={{0,14},{1,15},{2,0},{3,1},{4,2},{5,3},{6,4},{7,5},{8,6},{9,7},{10,... | collective-permute-start | bytes 786440 | tf_op jit(solution)/shard_map/ppermute | solution.py:64
  73.9 4.3 %collective-permute-done.3.refs_4_ = bf16[128,1024]{1,0:T(8,128)(2,1)S(1)} collective-permute-done((bf16[128,1024]{1,0:T(8,128)(2,1)S(1)}, bf16[128,1024]{1,0:T(8,128)(2,1)S(1)}, u32[]{:S(2)}, u32[]{:S(2)}) %collective-permute-start.3) | collective-permute-done | bytes 262176 | tf_op jit(solution)/shard_map/ppermute | solution.py:64
  78.4 3.2 %collective-permute-start.6 = (bf16[128,1024]{1,0:T(8,128)(2,1)S(1)}, bf16[128,1024]{1,0:T(8,128)(2,1)S(1)}, u32[]{:S(2)}, u32[]{:S(2)}) collective-permute-start(bf16[128,1024]{1,0:T(8,128)(2,1)S(1)} %collective-permute-done.5.refs_5_), channel_id=1, source_target_pairs={{0,14},{1,15},{2,0},{3,1},{4,2},{5,3},{6,4},{7,5},{8,6},{9,7},{10,... | collective-permute-start | bytes 786440 | tf_op jit(solution)/shard_map/ppermute | solution.py:64
  81.5 0.5 collective-permute-start.10
  82.0 3.7 %collective-permute-done.4.refs_8_ = bf16[128,1024]{1,0:T(8,128)(2,1)S(1)} collective-permute-done((bf16[128,1024]{1,0:T(8,128)(2,1)S(1)}, bf16[128,1024]{1,0:T(8,128)(2,1)S(1)}, u32[]{:S(2)}, u32[]{:S(2)}) %collective-permute-start.4) | collective-permute-done | bytes 262176 | tf_op jit(solution)/shard_map/ppermute | solution.py:64
  85.8 1.4 collective-permute-done.6.refs_9_
  87.2 2.1 %collective-permute-start.7 = (bf16[128,1024]{1,0:T(8,128)(2,1)S(1)}, bf16[128,1024]{1,0:T(8,128)(2,1)S(1)}, u32[]{:S(2)}, u32[]{:S(2)}) collective-permute-start(bf16[128,1024]{1,0:T(8,128)(2,1)S(1)} %collective-permute-done.4.refs_8_), channel_id=1, source_target_pairs={{0,2},{1,3},{2,4},{3,5},{4,6},{5,7},{6,8},{7,9},{8,10},{9,11},{10,... | collective-permute-start | bytes 786440 | tf_op jit(solution)/shard_map/ppermute | solution.py:64
  89.3 1.1 collective-permute-start.8
  90.4 2.4 %shard_map.111 = (bf16[1280,128]{1,0:T(8,128)(2,1)}, bf16[64,1280]{1,0:T(8,128)(2,1)}) custom-call(bf16[3,64,1024]{2,1,0:T(8,128)(2,1)S(1)} %bitcast.51, bf16[128,1024]{1,0:T(8,128)(2,1)S(1)} %fusion.4.refs_0_, bf16[128,1024]{1,0:T(8,128)(2,1)S(1)} %collective-permute-done.9.refs_1_, bf16[128,1024]{1,0:T(8,128)(2,1)S(1)} %collective-permute-done.10.refs_2_, ...), custom_call_target="tpu_custom_call" | custom-call | flops 503316480 | bytes 1966080 | tf_op jit(solution)/shard_map/pallas_call | solution.py:317
  92.9 4.2 %collective-permute-done.7.refs_2_ = bf16[128,1024]{1,0:T(8,128)(2,1)S(1)} collective-permute-done((bf16[128,1024]{1,0:T(8,128)(2,1)S(1)}, bf16[128,1024]{1,0:T(8,128)(2,1)S(1)}, u32[]{:S(2)}, u32[]{:S(2)}) %collective-permute-start.7) | collective-permute-done | bytes 262176 | tf_op jit(solution)/shard_map/ppermute | solution.py:64
  97.1 0.7 collective-permute-done.8.refs_3_
  97.9 2.3 %collective-permute-start.16 = (bf16[128,1024]{1,0:T(8,128)(2,1)S(1)}, bf16[128,1024]{1,0:T(8,128)(2,1)S(1)}, u32[]{:S(2)}, u32[]{:S(2)}) collective-permute-start(bf16[128,1024]{1,0:T(8,128)(2,1)S(1)} %broadcast_select_fusion), channel_id=1, source_target_pairs={{0,2},{1,15},{2,4},{3,1},{4,6},{5,3},{6,8},{7,5},{8,10},{9,7},{10,... | collective-permute-start | bytes 786440 | tf_op jit(solution)/shard_map/ppermute | solution.py:94
  100.4 0.4 collective-permute-start.15
  100.7 4.8 %collective-permute-done.16.refs_4_ = bf16[128,1024]{1,0:T(8,128)(2,1)S(1)} collective-permute-done((bf16[128,1024]{1,0:T(8,128)(2,1)S(1)}, bf16[128,1024]{1,0:T(8,128)(2,1)S(1)}, u32[]{:S(2)}, u32[]{:S(2)}) %collective-permute-start.16) | collective-permute-done | bytes 262176 | tf_op jit(solution)/shard_map/ppermute | solution.py:94
  105.6 1.5 collective-permute-start.18
  107.1 1.9 %collective-permute-start.20 = (bf16[16,32,512]{2,1,0:T(8,128)(2,1)S(1)}, bf16[16,32,512]{2,1,0:T(8,128)(2,1)S(1)}, u32[]{:S(2)}, u32[]{:S(2)}) collective-permute-start(bf16[16,32,512]{2,1,0:T(8,128)(2,1)S(1)} %slice.28.refs_0_), channel_id=1, source_target_pairs={{0,48},{16,32},{32,16},{48,0},{64,112},{80,96},{96,80},{112,64},{1... | collective-permute-start | bytes 1572872 | tf_op jit(solution)/shard_map/ppermute | solution.py:554
  109.1 0.9 copy-done.7
  110.0 11.5 %shard_map.112 = bf16[16,64,128]{2,1,0:T(8,128)(2,1)S(1)} custom-call(s32[1]{0:T(128)} %bitcast.1.place_ref, bf16[3,64,1024]{2,1,0:T(8,128)(2,1)S(1)} %bitcast.52, bf16[1280,128]{1,0:T(8,128)(2,1)} %get-tuple-element.41.qv_ref, bf16[64,1280]{1,0:T(8,128)(2,1)} %get-tuple-element.42.early_key_ref, bf16[128,1024]{1,0:T(8,128)(2,1)S(1)} %collective-permute-done.14.refs_0_, ...), custom_call_target="tpu_custom_call" | custom-call | flops 4294967296 | bytes 16777216 | tf_op jit(solution)/shard_map/pallas_call | solution.py:357
  121.6 0.7 copy-done.5
  122.3 5.4 %all-to-all-start.1 = ((bf16[16,64,128]{2,1,0:T(8,128)(2,1)}), bf16[16,64,128]{2,1,0:T(8,128)(2,1)S(1)}, u32[]{:S(2)}, u32[]{:S(2)}) async-start(bf16[16,64,128]{2,1,0:T(8,128)(2,1)} %copy-done.5), calls=%async_computation.1 | async-start | bytes 524288 | tf_op jit(solution)/shard_map/all_to_all | solution.py:560
  127.6 4.8 %collective-permute-done.19.refs_2_ = bf16[16,32,512]{2,1,0:T(8,128)(2,1)S(1)} collective-permute-done((bf16[16,32,512]{2,1,0:T(8,128)(2,1)S(1)}, bf16[16,32,512]{2,1,0:T(8,128)(2,1)S(1)}, u32[]{:S(2)}, u32[]{:S(2)}) %collective-permute-start.19) | collective-permute-done | bytes 524320 | tf_op jit(solution)/shard_map/ppermute | solution.py:554
  132.4 0.8 copy-done.2
  133.2 6.8 %all-to-all-done.1.heads_ref = bf16[16,64,128]{2,1,0:T(8,128)(2,1)S(1)} async-done(((bf16[16,64,128]{2,1,0:T(8,128)(2,1)}), bf16[16,64,128]{2,1,0:T(8,128)(2,1)S(1)}, u32[]{:S(2)}, u32[]{:S(2)}) %all-to-all-start.1) | async-done | bytes 262176 | tf_op jit(solution)/shard_map/all_to_all | solution.py:560
  140.0 1.0 copy-done.3
  141.0 0.7 shard_map.113
  141.7 1.4 collective-permute-start.21
  143.1 0.4 collective-permute-start.22
  143.5 1.8 collective-permute-start.23
  145.3 5.7 %collective-permute-done.21.second_ref = bf16[128,1024]{1,0:T(8,128)(2,1)S(1)} collective-permute-done((bf16[128,1024]{1,0:T(8,128)(2,1)S(1)}, bf16[128,1024]{1,0:T(8,128)(2,1)S(1)}, u32[]{:S(2)}, u32[]{:S(2)}) %collective-permute-start.21) | collective-permute-done | bytes 262176 | tf_op jit(solution)/shard_map/ppermute | solution.py:564
  151.0 3.7 %shard_map.114 = (f32[128,1024]{1,0:T(8,128)S(1)}, bf16[128,1024]{1,0:T(8,128)(2,1)S(1)}) custom-call(bf16[128,1024]{1,0:T(8,128)(2,1)S(1)} %get-tuple-element.47.first_ref, bf16[128,1024]{1,0:T(8,128)(2,1)S(1)} %collective-permute-done.21.second_ref, bf16[16,128,1024]{2,1,0:T(8,128)(2,1)} %bitcast.54), custom_call_target="tpu_custom_call" | custom-call | flops 1073741824 | bytes 4194304 | tf_op jit(solution)/shard_map/pallas_call | solution.py:486
  154.7 2.9 %collective-permute-done.22.first_ref = bf16[128,1024]{1,0:T(8,128)(2,1)S(1)} collective-permute-done((bf16[128,1024]{1,0:T(8,128)(2,1)S(1)}, bf16[128,1024]{1,0:T(8,128)(2,1)S(1)}, u32[]{:S(2)}, u32[]{:S(2)}) %collective-permute-start.22) | collective-permute-done | bytes 262176 | tf_op jit(solution)/shard_map/ppermute | solution.py:564
  157.7 3.7 %shard_map.115 = (bf16[128,1024]{1,0:T(8,128)(2,1)S(1)}, bf16[128,1024]{1,0:T(8,128)(2,1)S(1)}) custom-call(bf16[128,1024]{1,0:T(8,128)(2,1)S(1)} %collective-permute-done.22.first_ref, bf16[128,1024]{1,0:T(8,128)(2,1)S(1)} %collective-permute-done.23.second_ref, bf16[16,128,1024]{2,1,0:T(8,128)(2,1)} %bitcast.55), custom_call_target="tpu_custom_call" | custom-call | flops 1073741824 | bytes 4194304 | tf_op jit(solution)/shard_map/pallas_call | solution.py:486
  161.4 0.5 collective-permute-start.25
  161.9 1.7 collective-permute-start.26
  163.6 1.4 collective-permute-start.24
  165.0 10.2 %collective-permute-done.25 = bf16[128,1024]{1,0:T(8,128)(2,1)S(1)} collective-permute-done((bf16[128,1024]{1,0:T(8,128)(2,1)S(1)}, bf16[128,1024]{1,0:T(8,128)(2,1)S(1)}, u32[]{:S(2)}, u32[]{:S(2)}) %collective-permute-start.25) | collective-permute-done | bytes 262176 | tf_op jit(solution)/shard_map/ppermute | solution.py:571
  175.2 1.2 collective-permute-done.24
  176.5 0.9 add_convert_fusion
  (80 shorter events, 2.1 us)
Async XLA Ops:
  6.5 1.0 copy-start
  6.5 4.6 %copy-start.14 = (bf16[4,4,1024]{2,1,0:T(4,128)(2,1)S(1)}, bf16[4,4,1024]{2,1,0:T(4,128)(2,1)}, u32[]{:S(2)}) copy-start(bf16[4,4,1024]{2,1,0:T(4,128)(2,1)} %param.15) | copy-start | bytes 98308
  6.5 49.3 %all-gather.5.cloned.1.call-start = ((), (), s32[]{:S(2)}) async-start(), calls=%async_computation.2 | async-start | bytes 5013504 | tf_op jit(solution)/shard_map/all_gather | solution.py:527
  11.0 8.9 %copy-start.13 = (bf16[1024,256]{1,0:T(8,128)(2,1)S(1)}, bf16[1024,256]{1,0:T(8,128)(2,1)}, u32[]{:S(2)}) copy-start(bf16[1024,256]{1,0:T(8,128)(2,1)} %param.20) | copy-start | bytes 1572868
  12.3 20.5 %all-to-all-start = ((bf16[16,96,256]{2,1,0:T(8,128)(2,1)}), bf16[16,96,256]{2,1,0:T(8,128)(2,1)S(1)}, u32[]{:S(2)}, u32[]{:S(2)}) async-start(bf16[16,96,256]{2,1,0:T(8,128)(2,1)} %bitcast_select_fusion), calls=%async_computation | async-start | bytes 1572864 | tf_op jit(solution)/shard_map/all_to_all | solution.py:50
  19.7 131.2 %all-gather.7.cloned.1.call-start = ((), (), s32[]{:S(2)}) async-start(), calls=%async_computation.3 | async-start | bytes 4456448 | tf_op jit(solution)/shard_map/all_gather | solution.py:558
  20.1 17.1 %copy-start.8 = (bf16[48,256]{1,0:T(8,128)(2,1)S(1)}, bf16[48,256]{1,0:T(8,128)(2,1)}, u32[]{:S(2)}) copy-start(bf16[48,256]{1,0:T(8,128)(2,1)} %refs_4_.1) | copy-start | bytes 73732
  32.7 0.9 copy-start.12
  34.1 1.8 copy-start.10
  34.5 7.5 %collective-permute-start = (bf16[48,256]{1,0:T(8,128)(2,1)S(1)}, bf16[48,256]{1,0:T(8,128)(2,1)S(1)}, u32[]{:S(2)}, u32[]{:S(2)}) collective-permute-start(bf16[48,256]{1,0:T(8,128)(2,1)S(1)} %copy.32), channel_id=1, source_target_pairs={{0,1},{1,2},{2,3},{3,4},{4,5},{5,6},{6,7},{7,8},{8,9},{9,10},{10,1... | collective-permute-start | bytes 73736 | tf_op jit(solution)/shard_map/ppermute | solution.py:197
  35.9 6.1 %collective-permute-start.1 = (bf16[48,256]{1,0:T(8,128)(2,1)S(1)}, bf16[48,256]{1,0:T(8,128)(2,1)S(1)}, u32[]{:S(2)}, u32[]{:S(2)}) collective-permute-start(bf16[48,256]{1,0:T(8,128)(2,1)S(1)} %copy.33), channel_id=1, source_target_pairs={{1,0},{2,1},{3,2},{4,3},{5,4},{6,5},{7,6},{8,7},{9,8},{10,9},{11,1... | collective-permute-start | bytes 73736 | tf_op jit(solution)/shard_map/ppermute | solution.py:198
  37.2 1.7 copy-start.11
  42.0 1.6 copy-start.1
  59.2 5.5 %copy-start.15 = (f32[1024]{0:T(1024)S(1)}, f32[1024]{0:T(1024)}, u32[]{:S(2)}) copy-start(f32[1024]{0:T(1024)} %param.16) | copy-start | bytes 12292
  59.2 31.2 %copy-start.4 = (bf16[3,1024,64]{1,2,0:T(8,128)(2,1)S(1)}, bf16[3,1024,64]{1,2,0:T(8,128)(2,1)}, u32[]{:S(2)}) copy-start(bf16[3,1024,64]{1,2,0:T(8,128)(2,1)} %param.17) | copy-start | bytes 1179652
  59.2 5.1 %collective-permute-start.2 = (bf16[128,512]{1,0:T(8,128)(2,1)S(1)}, bf16[128,512]{1,0:T(8,128)(2,1)S(1)}, u32[]{:S(2)}, u32[]{:S(2)}) collective-permute-start(bf16[128,512]{1,0:T(8,128)(2,1)S(1)} %get-tuple-element.33), channel_id=1, source_target_pairs={{0,16},{16,0},{32,48},{48,32},{64,80},{80,64},{96,112},{112,96},{1... | collective-permute-start | bytes 393224 | tf_op jit(solution)/shard_map/ppermute | solution.py:546
  64.9 13.3 %collective-permute-start.3 = (bf16[128,1024]{1,0:T(8,128)(2,1)S(1)}, bf16[128,1024]{1,0:T(8,128)(2,1)S(1)}, u32[]{:S(2)}, u32[]{:S(2)}) collective-permute-start(bf16[128,1024]{1,0:T(8,128)(2,1)S(1)} %fusion.4.refs_0_), channel_id=1, source_target_pairs={{0,2},{1,3},{2,4},{3,5},{4,6},{5,7},{6,8},{7,9},{8,10},{9,11},{10,... | collective-permute-start | bytes 786440 | tf_op jit(solution)/shard_map/ppermute | solution.py:64
  70.7 7.7 %collective-permute-start.5 = (bf16[128,1024]{1,0:T(8,128)(2,1)S(1)}, bf16[128,1024]{1,0:T(8,128)(2,1)S(1)}, u32[]{:S(2)}, u32[]{:S(2)}) collective-permute-start(bf16[128,1024]{1,0:T(8,128)(2,1)S(1)} %fusion.4.refs_0_), channel_id=1, source_target_pairs={{0,14},{1,15},{2,0},{3,1},{4,2},{5,3},{6,4},{7,5},{8,6},{9,7},{10,... | collective-permute-start | bytes 786440 | tf_op jit(solution)/shard_map/ppermute | solution.py:64
  78.2 7.6 %collective-permute-start.4 = (bf16[128,1024]{1,0:T(8,128)(2,1)S(1)}, bf16[128,1024]{1,0:T(8,128)(2,1)S(1)}, u32[]{:S(2)}, u32[]{:S(2)}) collective-permute-start(bf16[128,1024]{1,0:T(8,128)(2,1)S(1)} %collective-permute-done.3.refs_4_), channel_id=1, source_target_pairs={{0,2},{1,3},{2,4},{3,5},{4,6},{5,7},{6,8},{7,9},{8,10},{9,11},{10,... | collective-permute-start | bytes 786440 | tf_op jit(solution)/shard_map/ppermute | solution.py:64
  78.4 8.8 %collective-permute-start.6 = (bf16[128,1024]{1,0:T(8,128)(2,1)S(1)}, bf16[128,1024]{1,0:T(8,128)(2,1)S(1)}, u32[]{:S(2)}, u32[]{:S(2)}) collective-permute-start(bf16[128,1024]{1,0:T(8,128)(2,1)S(1)} %collective-permute-done.5.refs_5_), channel_id=1, source_target_pairs={{0,14},{1,15},{2,0},{3,1},{4,2},{5,3},{6,4},{7,5},{8,6},{9,7},{10,... | collective-permute-start | bytes 786440 | tf_op jit(solution)/shard_map/ppermute | solution.py:64
  81.5 5.7 %collective-permute-start.9 = (bf16[128,1024]{1,0:T(8,128)(2,1)S(1)}, bf16[128,1024]{1,0:T(8,128)(2,1)S(1)}, u32[]{:S(2)}, u32[]{:S(2)}) collective-permute-start(bf16[128,1024]{1,0:T(8,128)(2,1)S(1)} %fusion.4.refs_0_), channel_id=1, source_target_pairs={{0,1},{1,0},{2,3},{3,2},{4,5},{5,4},{6,7},{7,6},{8,9},{9,8},{10,11... | collective-permute-start | bytes 786440 | tf_op jit(solution)/shard_map/ppermute | solution.py:68
  81.5 7.8 %collective-permute-start.10 = (bf16[128,1024]{1,0:T(8,128)(2,1)S(1)}, bf16[128,1024]{1,0:T(8,128)(2,1)S(1)}, u32[]{:S(2)}, u32[]{:S(2)}) collective-permute-start(bf16[128,1024]{1,0:T(8,128)(2,1)S(1)} %collective-permute-done.3.refs_4_), channel_id=1, source_target_pairs={{0,1},{1,0},{2,3},{3,2},{4,5},{5,4},{6,7},{7,6},{8,9},{9,8},{10,11... | collective-permute-start | bytes 786440 | tf_op jit(solution)/shard_map/ppermute | solution.py:68
  82.0 8.4 %collective-permute-start.11 = (bf16[128,1024]{1,0:T(8,128)(2,1)S(1)}, bf16[128,1024]{1,0:T(8,128)(2,1)S(1)}, u32[]{:S(2)}, u32[]{:S(2)}) collective-permute-start(bf16[128,1024]{1,0:T(8,128)(2,1)S(1)} %collective-permute-done.5.refs_5_), channel_id=1, source_target_pairs={{0,1},{1,0},{2,3},{3,2},{4,5},{5,4},{6,7},{7,6},{8,9},{9,8},{10,11... | collective-permute-start | bytes 786440 | tf_op jit(solution)/shard_map/ppermute | solution.py:68
  85.8 4.6 %collective-permute-start.12 = (bf16[128,1024]{1,0:T(8,128)(2,1)S(1)}, bf16[128,1024]{1,0:T(8,128)(2,1)S(1)}, u32[]{:S(2)}, u32[]{:S(2)}) collective-permute-start(bf16[128,1024]{1,0:T(8,128)(2,1)S(1)} %collective-permute-done.4.refs_8_), channel_id=1, source_target_pairs={{0,1},{1,0},{2,3},{3,2},{4,5},{5,4},{6,7},{7,6},{8,9},{9,8},{10,11... | collective-permute-start | bytes 786440 | tf_op jit(solution)/shard_map/ppermute | solution.py:68
  87.2 3.3 %collective-permute-start.13 = (bf16[128,1024]{1,0:T(8,128)(2,1)S(1)}, bf16[128,1024]{1,0:T(8,128)(2,1)S(1)}, u32[]{:S(2)}, u32[]{:S(2)}) collective-permute-start(bf16[128,1024]{1,0:T(8,128)(2,1)S(1)} %collective-permute-done.6.refs_9_), channel_id=1, source_target_pairs={{0,1},{1,0},{2,3},{3,2},{4,5},{5,4},{6,7},{7,6},{8,9},{9,8},{10,11... | collective-permute-start | bytes 786440 | tf_op jit(solution)/shard_map/ppermute | solution.py:68
  87.2 9.9 %collective-permute-start.7 = (bf16[128,1024]{1,0:T(8,128)(2,1)S(1)}, bf16[128,1024]{1,0:T(8,128)(2,1)S(1)}, u32[]{:S(2)}, u32[]{:S(2)}) collective-permute-start(bf16[128,1024]{1,0:T(8,128)(2,1)S(1)} %collective-permute-done.4.refs_8_), channel_id=1, source_target_pairs={{0,2},{1,3},{2,4},{3,5},{4,6},{5,7},{6,8},{7,9},{8,10},{9,11},{10,... | collective-permute-start | bytes 786440 | tf_op jit(solution)/shard_map/ppermute | solution.py:64
  89.3 8.5 %collective-permute-start.8 = (bf16[128,1024]{1,0:T(8,128)(2,1)S(1)}, bf16[128,1024]{1,0:T(8,128)(2,1)}, u32[]{:S(2)}, u32[]{:S(2)}) collective-permute-start(bf16[128,1024]{1,0:T(8,128)(2,1)S(1)} %collective-permute-done.6.refs_9_), channel_id=1, source_target_pairs={{0,14},{1,15},{2,0},{3,1},{4,2},{5,3},{6,4},{7,5},{8,6},{9,7},{10,... | collective-permute-start | bytes 786440 | tf_op jit(solution)/shard_map/ppermute | solution.py:64
  97.1 12.0 %copy-start.6 = (bf16[128,1024]{1,0:T(8,128)(2,1)}, bf16[128,1024]{1,0:T(8,128)(2,1)S(1)}, u32[]{:S(2)}) copy-start(bf16[128,1024]{1,0:T(8,128)(2,1)S(1)} %collective-permute-done.7.refs_2_) | copy-start | bytes 786436
  97.9 7.7 %collective-permute-start.16 = (bf16[128,1024]{1,0:T(8,128)(2,1)S(1)}, bf16[128,1024]{1,0:T(8,128)(2,1)S(1)}, u32[]{:S(2)}, u32[]{:S(2)}) collective-permute-start(bf16[128,1024]{1,0:T(8,128)(2,1)S(1)} %broadcast_select_fusion), channel_id=1, source_target_pairs={{0,2},{1,15},{2,4},{3,1},{4,6},{5,3},{6,8},{7,5},{8,10},{9,7},{10,... | collective-permute-start | bytes 786440 | tf_op jit(solution)/shard_map/ppermute | solution.py:94
  100.2 6.9 %collective-permute-start.14 = (bf16[128,1024]{1,0:T(8,128)(2,1)S(1)}, bf16[128,1024]{1,0:T(8,128)(2,1)S(1)}, u32[]{:S(2)}, u32[]{:S(2)}) collective-permute-start(bf16[128,1024]{1,0:T(8,128)(2,1)S(1)} %collective-permute-done.7.refs_2_), channel_id=1, source_target_pairs={{0,1},{1,0},{2,3},{3,2},{4,5},{5,4},{6,7},{7,6},{8,9},{9,8},{10,11... | collective-permute-start | bytes 786440 | tf_op jit(solution)/shard_map/ppermute | solution.py:68
  100.4 8.7 %collective-permute-start.15 = (bf16[128,1024]{1,0:T(8,128)(2,1)}, bf16[128,1024]{1,0:T(8,128)(2,1)S(1)}, u32[]{:S(2)}, u32[]{:S(2)}) collective-permute-start(bf16[128,1024]{1,0:T(8,128)(2,1)} %collective-permute-done.8.refs_3_), channel_id=1, source_target_pairs={{0,1},{1,0},{2,3},{3,2},{4,5},{5,4},{6,7},{7,6},{8,9},{9,8},{10,11... | collective-permute-start | bytes 786440 | tf_op jit(solution)/shard_map/ppermute | solution.py:68
  105.6 3.5 %collective-permute-start.17 = (bf16[128,1024]{1,0:T(8,128)(2,1)S(1)}, bf16[128,1024]{1,0:T(8,128)(2,1)S(1)}, u32[]{:S(2)}, u32[]{:S(2)}) collective-permute-start(bf16[128,1024]{1,0:T(8,128)(2,1)S(1)} %collective-permute-done.16.refs_4_), channel_id=1, source_target_pairs={{0,1},{1,0},{2,3},{3,2},{4,5},{5,4},{6,7},{7,6},{8,9},{9,8},{10,11... | collective-permute-start | bytes 786440 | tf_op jit(solution)/shard_map/ppermute | solution.py:68
  105.6 22.1 %collective-permute-start.18 = (bf16[16,32,512]{2,1,0:T(8,128)(2,1)S(1)}, bf16[16,32,512]{2,1,0:T(8,128)(2,1)S(1)}, u32[]{:S(2)}, u32[]{:S(2)}) collective-permute-start(bf16[16,32,512]{2,1,0:T(8,128)(2,1)S(1)} %slice.28.refs_0_), channel_id=1, source_target_pairs={{0,16},{16,0},{32,48},{48,32},{64,80},{80,64},{96,112},{112,96},{1... | collective-permute-start | bytes 1572872 | tf_op jit(solution)/shard_map/ppermute | solution.py:554
  107.1 25.3 %collective-permute-start.19 = (bf16[16,32,512]{2,1,0:T(8,128)(2,1)S(1)}, bf16[16,32,512]{2,1,0:T(8,128)(2,1)S(1)}, u32[]{:S(2)}, u32[]{:S(2)}) collective-permute-start(bf16[16,32,512]{2,1,0:T(8,128)(2,1)S(1)} %slice.28.refs_0_), channel_id=1, source_target_pairs={{0,32},{16,48},{32,0},{48,16},{64,96},{80,112},{96,64},{112,80},{1... | collective-permute-start | bytes 1572872 | tf_op jit(solution)/shard_map/ppermute | solution.py:554
  107.1 25.3 %collective-permute-start.20 = (bf16[16,32,512]{2,1,0:T(8,128)(2,1)S(1)}, bf16[16,32,512]{2,1,0:T(8,128)(2,1)S(1)}, u32[]{:S(2)}, u32[]{:S(2)}) collective-permute-start(bf16[16,32,512]{2,1,0:T(8,128)(2,1)S(1)} %slice.28.refs_0_), channel_id=1, source_target_pairs={{0,48},{16,32},{32,16},{48,0},{64,112},{80,96},{96,80},{112,64},{1... | collective-permute-start | bytes 1572872 | tf_op jit(solution)/shard_map/ppermute | solution.py:554
  109.1 1.0 copy-start.7
  110.0 29.9 %copy-start.9 = (f32[1024]{0:T(1024)S(1)}, f32[1024]{0:T(1024)}, u32[]{:S(2)}) copy-start(f32[1024]{0:T(1024)} %param.19) | copy-start | bytes 12292
  121.6 0.7 copy-start.5
  122.3 17.7 %all-to-all-start.1 = ((bf16[16,64,128]{2,1,0:T(8,128)(2,1)}), bf16[16,64,128]{2,1,0:T(8,128)(2,1)S(1)}, u32[]{:S(2)}, u32[]{:S(2)}) async-start(bf16[16,64,128]{2,1,0:T(8,128)(2,1)} %copy-done.5), calls=%async_computation.1 | async-start | bytes 524288 | tf_op jit(solution)/shard_map/all_to_all | solution.py:560
  132.4 0.8 copy-start.2
  140.0 1.0 copy-start.3
  141.7 9.3 %collective-permute-start.21 = (bf16[128,1024]{1,0:T(8,128)(2,1)S(1)}, bf16[128,1024]{1,0:T(8,128)(2,1)S(1)}, u32[]{:S(2)}, u32[]{:S(2)}) collective-permute-start(bf16[128,1024]{1,0:T(8,128)(2,1)S(1)} %get-tuple-element.47.first_ref), channel_id=1, source_target_pairs={{0,16},{16,0},{32,48},{48,32},{64,80},{80,64},{96,112},{112,96},{1... | collective-permute-start | bytes 786440 | tf_op jit(solution)/shard_map/ppermute | solution.py:564
  143.1 14.6 %collective-permute-start.22 = (bf16[128,1024]{1,0:T(8,128)(2,1)S(1)}, bf16[128,1024]{1,0:T(8,128)(2,1)S(1)}, u32[]{:S(2)}, u32[]{:S(2)}) collective-permute-start(bf16[128,1024]{1,0:T(8,128)(2,1)S(1)} %get-tuple-element.47.first_ref), channel_id=1, source_target_pairs={{0,32},{16,48},{32,0},{48,16},{64,96},{80,112},{96,64},{112,80},{1... | collective-permute-start | bytes 786440 | tf_op jit(solution)/shard_map/ppermute | solution.py:564
  143.5 14.1 %collective-permute-start.23 = (bf16[128,1024]{1,0:T(8,128)(2,1)S(1)}, bf16[128,1024]{1,0:T(8,128)(2,1)S(1)}, u32[]{:S(2)}, u32[]{:S(2)}) collective-permute-start(bf16[128,1024]{1,0:T(8,128)(2,1)S(1)} %get-tuple-element.47.first_ref), channel_id=1, source_target_pairs={{0,48},{16,32},{32,16},{48,0},{64,112},{80,96},{96,80},{112,64},{1... | collective-permute-start | bytes 786440 | tf_op jit(solution)/shard_map/ppermute | solution.py:564
  161.4 13.8 %collective-permute-start.25 = (bf16[128,1024]{1,0:T(8,128)(2,1)S(1)}, bf16[128,1024]{1,0:T(8,128)(2,1)S(1)}, u32[]{:S(2)}, u32[]{:S(2)}) collective-permute-start(bf16[128,1024]{1,0:T(8,128)(2,1)S(1)} %get-tuple-element.55), channel_id=1, source_target_pairs={{0,32},{16,48},{32,0},{48,16},{64,96},{80,112},{96,64},{112,80},{1... | collective-permute-start | bytes 786440 | tf_op jit(solution)/shard_map/ppermute | solution.py:571
  161.9 13.3 %collective-permute-start.26 = (bf16[128,1024]{1,0:T(8,128)(2,1)S(1)}, bf16[128,1024]{1,0:T(8,128)(2,1)S(1)}, u32[]{:S(2)}, u32[]{:S(2)}) collective-permute-start(bf16[128,1024]{1,0:T(8,128)(2,1)S(1)} %get-tuple-element.56), channel_id=1, source_target_pairs={{0,48},{16,32},{32,16},{48,0},{64,112},{80,96},{96,80},{112,64},{1... | collective-permute-start | bytes 786440 | tf_op jit(solution)/shard_map/ppermute | solution.py:571
  163.6 12.8 %collective-permute-start.24 = (bf16[128,1024]{1,0:T(8,128)(2,1)S(1)}, bf16[128,1024]{1,0:T(8,128)(2,1)S(1)}, u32[]{:S(2)}, u32[]{:S(2)}) collective-permute-start(bf16[128,1024]{1,0:T(8,128)(2,1)S(1)} %get-tuple-element.52), channel_id=1, source_target_pairs={{0,16},{16,0},{32,48},{48,32},{64,80},{80,64},{96,112},{112,96},{1... | collective-permute-start | bytes 786440 | tf_op jit(solution)/shard_map/ppermute | solution.py:567
Sparse Core Ops, SparseCore 0:
  9.3 45.3 all-gather.4
  98.0 43.6 all-gather.6

commit v3 on v2

--- a/solution.py
+++ b/solution.py
@@ -262,7 +262,7 @@
 
 
 def attention_body(chips, tokens, early, late, place_ref, weight_ref, qv_ref, early_key_ref, *refs):
-    *piece_refs, out_ref, all_ref, key_ref, sems = refs
+    *piece_refs, out_ref, all_ref, key_ref, done_ref, sems, out_sems = refs
     place = place_ref[0]
     chip, core = place // 2, place % 2
     key_ref[HD:, :] = jnp.zeros((HD, key_ref.shape[1]), key_ref.dtype)
@@ -293,6 +293,9 @@
     block = 2 * tokens
     scale = HD ** (-0.5) * math.log2(math.e)
 
+    def sent(target):
+        return pltpu.make_async_copy(done_ref.at[target], out_ref.at[target], out_sems.at[target])
+
     def attend(step, carry):
         for i in range(2):
             at = pl.multiple_of((2 * step + i) * block, block)
@@ -306,10 +309,14 @@
             mixed = jnp.dot(probs, all_ref[...], preferred_element_type=jnp.float32)
             for j in range(2):
                 out = mixed[j * tokens : (j + 1) * tokens, :].T[HD:, :]
-                out_ref[2 * (2 * step + i) + j] = out.astype(jnp.bfloat16)
+                target = 2 * (2 * step + i) + j
+                done_ref[target] = out.astype(jnp.bfloat16)
+                sent(target).start()
         return carry
 
     lax.fori_loop(0, all_ref.shape[0] // (2 * block), attend, 0)
+    for target in range(out_ref.shape[0]):
+        sent(target).wait()
 
 
 def early_projection(weight, pieces):
@@ -343,13 +350,15 @@
     )
     heads = pl.pallas_call(
         body,
-        out_shape=jax.ShapeDtypeStruct((cols, HD, tokens), jnp.bfloat16),
+        out_shape=pltpu.HBM((cols, HD, tokens), jnp.bfloat16),
         in_specs=[pl.BlockSpec(memory_space=pltpu.SMEM), VMEM, HBM, HBM] + [VMEM] * len(late),
-        out_specs=VMEM,
+        out_specs=HBM,
         scratch_shapes=[
             pltpu.VMEM((cols * tokens, 2 * HD), jnp.bfloat16),
             pltpu.VMEM((2 * HD, cols * tokens), jnp.bfloat16),
+            pltpu.VMEM((cols, HD, tokens), jnp.bfloat16),
             pltpu.SemaphoreType.DMA((2, len(early))),
+            pltpu.SemaphoreType.DMA((cols,)),
         ],
         compiler_params=pltpu.CompilerParams(vmem_limit_bytes=14 << 20),
         cost_estimate=cost(16 * HD * (cols * tokens) ** 2),
@@ -447,7 +456,7 @@
     return pl.pallas_call(
         out_body,
         out_shape=(
-            jax.ShapeDtypeStruct(tokens_in.shape, jnp.float32),
+            pltpu.HBM(tokens_in.shape, jnp.float32),
             jax.ShapeDtypeStruct(tokens_in.shape, jnp.bfloat16),
         ),
         in_specs=[pl.BlockSpec(memory_space=pltpu.SMEM)] + [VMEM] * (3 + len(quarters)),

time: 185 us -> 183 us (0.989)
  local copies, waits for them, and re-layouts: 14.3 us -> 9.79 us
  Pallas kernels: 37.7 us -> 39.7 us
    unnamed x36 -> x26, local copies, waits for them, and re-layouts: 8.6 us -> 5.03 us
  transfers between devices with their start and end apart: 31 -> 31, of which waited for: 14 -> 16; matrix products, arithmetic and copies ran while one was open for 6% -> 6% of each run, Pallas kernels for 17% -> 18%
where the time goes in v3:
time: 183 us; the launch traced here: 182 us
  waiting for transfers between devices  65.1 us (36%)
  starting transfers between devices  46 us (25%)
  Pallas kernels  39.7 us (22%)
  between operations  13.9 us (8%)
  local copies, waits for them, and re-layouts  9.79 us (5%)
  other arithmetic  4.06 us (2%)
  matrix products  3.39 us (2%)
    ppermute x6, starting transfers between devices, moved(): lax.ppermute(value, 'col', [(i, (i + step) % count) for i in range(count)])  15.2 us
    ppermute x6, waiting for transfers between devices, moved(): lax.ppermute(value, 'col', [(i, (i + step) % count) for i in range(count)])  14.7 us
    pallas_call x1, Pallas kernels, stem_features(): pl.pallas_call(functools.partial(stem_body, len(starts)), out_shape=pltpu...  12.7 us
    pallas_call x1, Pallas kernels, attended_heads(): heads(lax.axis_index('col').reshape(1), weight, pltpu.with_memory_space_c...  12.3 us
    all_to_all x1, waiting for transfers between devices, image_strips(): incoming = lax.all_to_all(outgoing, ('section', 'row'), 0, 0, tiled=True)  10.9 us
    ppermute x2, waiting for transfers between devices, on_device(): lax.ppermute(term, 'row', team_pairs(step)).astype(jnp.float32)  9.92 us
    ppermute x3, waiting for transfers between devices, on_device(): lax.ppermute(normed_mlp, 'row', team_pairs(i))  8.11 us
    pallas_call x2, Pallas kernels, mlp_terms(): pl.pallas_call(mlp_body, out_shape=(jax.ShapeDtypeStruct(first.shape, fir...  7.56 us
  transfers between devices with their start and end apart: 31, of which 16 were waited for; matrix products, arithmetic and copies ran while one was open for 6% of the time, Pallas kernels for 18%

profile of v3, /device:TPU:2, one launch (start us, length us, event | category | flops | bytes accessed | tf_op | source)
XLA Modules:
  0.0 182.0 jit_solution(8406799612093766274)
XLA Ops:
  6.5 1.0 copy-done
  7.6 0.7 constant_dynamic-slice_fusion
  8.3 0.7 pad_maximum_fusion
  9.3 1.4 copy.27
  10.7 0.2 broadcast_in_dim.47
  10.9 0.2 copy.28
  11.2 1.1 bitcast_select_fusion
  12.3 7.5 %all-to-all-start = ((bf16[16,96,256]{2,1,0:T(8,128)(2,1)}), bf16[16,96,256]{2,1,0:T(8,128)(2,1)S(1)}, u32[]{:S(2)}, u32[]{:S(2)}) async-start(bf16[16,96,256]{2,1,0:T(8,128)(2,1)} %bitcast_select_fusion), calls=%async_computation | async-start | bytes 1572864 | tf_op jit(solution)/shard_map/all_to_all | solution.py:50
  19.8 0.1 constant_dynamic-slice_fusion.4
  20.1 0.9 constant_dynamic-slice_fusion.3
  21.1 0.7 pad_maximum_fusion.1
  21.8 10.9 %all-to-all-done = bf16[16,96,256]{2,1,0:T(8,128)(2,1)S(1)} async-done(((bf16[16,96,256]{2,1,0:T(8,128)(2,1)}), bf16[16,96,256]{2,1,0:T(8,128)(2,1)S(1)}, u32[]{:S(2)}, u32[]{:S(2)}) %all-to-all-start) | async-done | bytes 786464 | tf_op jit(solution)/shard_map/all_to_all | solution.py:50
  32.8 0.5 copy.31
  33.2 0.2 fusion.9
  33.5 0.8 copy-done.5
  34.3 1.3 collective-permute-start
  35.8 1.4 collective-permute-start.1
  37.2 1.6 maximum_reduce-precision_fusion.1
  38.9 1.8 maximum_reduce-precision_fusion
  41.1 1.6 copy-done.1
  42.8 12.7 %shard_map.109.features_ref = bf16[256,4096]{1,0:T(8,128)(2,1)} custom-call(f32[2,2048,128]{2,1,0:T(8,128)S(1)} %bitcast.49, f32[2,2048,128]{2,1,0:T(8,128)S(1)} %bitcast.50, bf16[48,256]{1,0:T(8,128)(2,1)S(1)} %collective-permute-done.refs_2_, bf16[48,256]{1,0:T(8,128)(2,1)S(1)} %collective-permute-done.1.refs_3_, bf16[48,256]{1,0:T(8,128)(2,1)S(1)} %copy-done.3, ...), custom_call_target="tpu_custom_call" | custom-call | flops 4831838208 | bytes 18874368 | tf_op jit(solution)/shard_map/pallas_call | solution.py:212
  55.5 3.3 %shard_map.110 = (bf16[128,512]{1,0:T(8,128)(2,1)S(1)}, bf16[128,512]{1,0:T(8,128)(2,1)S(1)}) custom-call(s32[1]{0:T(128)} %bitcast.4.half_ref, bf16[256,4096]{1,0:T(8,128)(2,1)} %shard_map.109.features_ref, bf16[16,288,512]{2,1,0:T(8,128)(2,1)} %bitcast.57, bf16[4,32,512]{2,1,0:T(8,128)(2,1)S(1)} %reshape.81.place_ref), custom_call_target="tpu_custom_call" | custom-call | flops 1073741824 | bytes 4194304 | tf_op jit(solution)/shard_map/pallas_call | solution.py:422
  58.9 1.5 collective-permute-start.2
  60.5 1.1 slice.28.refs_0_
  61.5 2.4 %collective-permute-done.2 = bf16[128,512]{1,0:T(8,128)(2,1)S(1)} collective-permute-done((bf16[128,512]{1,0:T(8,128)(2,1)S(1)}, bf16[128,512]{1,0:T(8,128)(2,1)S(1)}, u32[]{:S(2)}, u32[]{:S(2)}) %collective-permute-start.2) | collective-permute-done | bytes 131104 | tf_op jit(solution)/shard_map/ppermute | solution.py:555
  64.1 0.2 fusion.2
  64.4 0.2 fusion.4.refs_0_
  64.6 5.7 %collective-permute-start.3 = (bf16[128,1024]{1,0:T(8,128)(2,1)S(1)}, bf16[128,1024]{1,0:T(8,128)(2,1)S(1)}, u32[]{:S(2)}, u32[]{:S(2)}) collective-permute-start(bf16[128,1024]{1,0:T(8,128)(2,1)S(1)} %fusion.4.refs_0_), channel_id=1, source_target_pairs={{0,2},{1,3},{2,4},{3,5},{4,6},{5,7},{6,8},{7,9},{8,10},{9,11},{10,... | collective-permute-start | bytes 786440 | tf_op jit(solution)/shard_map/ppermute | solution.py:64
  70.3 3.2 %collective-permute-start.5 = (bf16[128,1024]{1,0:T(8,128)(2,1)S(1)}, bf16[128,1024]{1,0:T(8,128)(2,1)S(1)}, u32[]{:S(2)}, u32[]{:S(2)}) collective-permute-start(bf16[128,1024]{1,0:T(8,128)(2,1)S(1)} %fusion.4.refs_0_), channel_id=1, source_target_pairs={{0,14},{1,15},{2,0},{3,1},{4,2},{5,3},{6,4},{7,5},{8,6},{9,7},{10,... | collective-permute-start | bytes 786440 | tf_op jit(solution)/shard_map/ppermute | solution.py:64
  73.5 4.3 %collective-permute-done.3.refs_4_ = bf16[128,1024]{1,0:T(8,128)(2,1)S(1)} collective-permute-done((bf16[128,1024]{1,0:T(8,128)(2,1)S(1)}, bf16[128,1024]{1,0:T(8,128)(2,1)S(1)}, u32[]{:S(2)}, u32[]{:S(2)}) %collective-permute-start.3) | collective-permute-done | bytes 262176 | tf_op jit(solution)/shard_map/ppermute | solution.py:64
  77.8 0.3 collective-permute-start.4
  78.0 0.3 collective-permute-done.5.refs_5_
  78.3 2.8 %collective-permute-start.6 = (bf16[128,1024]{1,0:T(8,128)(2,1)S(1)}, bf16[128,1024]{1,0:T(8,128)(2,1)S(1)}, u32[]{:S(2)}, u32[]{:S(2)}) collective-permute-start(bf16[128,1024]{1,0:T(8,128)(2,1)S(1)} %collective-permute-done.5.refs_5_), channel_id=1, source_target_pairs={{0,14},{1,15},{2,0},{3,1},{4,2},{5,3},{6,4},{7,5},{8,6},{9,7},{10,... | collective-permute-start | bytes 786440 | tf_op jit(solution)/shard_map/ppermute | solution.py:64
  81.1 0.5 collective-permute-start.10
  81.6 3.7 %collective-permute-done.4.refs_8_ = bf16[128,1024]{1,0:T(8,128)(2,1)S(1)} collective-permute-done((bf16[128,1024]{1,0:T(8,128)(2,1)S(1)}, bf16[128,1024]{1,0:T(8,128)(2,1)S(1)}, u32[]{:S(2)}, u32[]{:S(2)}) %collective-permute-start.4) | collective-permute-done | bytes 262176 | tf_op jit(solution)/shard_map/ppermute | solution.py:64
  85.4 1.9 %collective-permute-done.6.refs_9_ = bf16[128,1024]{1,0:T(8,128)(2,1)S(1)} collective-permute-done((bf16[128,1024]{1,0:T(8,128)(2,1)S(1)}, bf16[128,1024]{1,0:T(8,128)(2,1)S(1)}, u32[]{:S(2)}, u32[]{:S(2)}) %collective-permute-start.6) | collective-permute-done | bytes 262176 | tf_op jit(solution)/shard_map/ppermute | solution.py:64
  87.3 1.7 collective-permute-start.7
  89.0 1.5 collective-permute-start.8
  90.5 2.5 %shard_map.111 = (bf16[1280,128]{1,0:T(8,128)(2,1)}, bf16[64,1280]{1,0:T(8,128)(2,1)}) custom-call(bf16[3,64,1024]{2,1,0:T(8,128)(2,1)S(1)} %bitcast.51, bf16[128,1024]{1,0:T(8,128)(2,1)S(1)} %fusion.4.refs_0_, bf16[128,1024]{1,0:T(8,128)(2,1)S(1)} %collective-permute-done.9.refs_1_, bf16[128,1024]{1,0:T(8,128)(2,1)S(1)} %collective-permute-done.10.refs_2_, ...), custom_call_target="tpu_custom_call" | custom-call | flops 503316480 | bytes 1966080 | tf_op jit(solution)/shard_map/pallas_call | solution.py:324
  93.0 4.2 %collective-permute-done.7.refs_2_ = bf16[128,1024]{1,0:T(8,128)(2,1)S(1)} collective-permute-done((bf16[128,1024]{1,0:T(8,128)(2,1)S(1)}, bf16[128,1024]{1,0:T(8,128)(2,1)S(1)}, u32[]{:S(2)}, u32[]{:S(2)}) %collective-permute-start.7) | collective-permute-done | bytes 262176 | tf_op jit(solution)/shard_map/ppermute | solution.py:64
  97.2 0.4 collective-permute-done.8.refs_3_
  97.7 2.2 %collective-permute-start.16 = (bf16[128,1024]{1,0:T(8,128)(2,1)S(1)}, bf16[128,1024]{1,0:T(8,128)(2,1)S(1)}, u32[]{:S(2)}, u32[]{:S(2)}) collective-permute-start(bf16[128,1024]{1,0:T(8,128)(2,1)S(1)} %broadcast_select_fusion), channel_id=1, source_target_pairs={{0,2},{1,15},{2,4},{3,1},{4,6},{5,3},{6,8},{7,5},{8,10},{9,7},{10,... | collective-permute-start | bytes 786440 | tf_op jit(solution)/shard_map/ppermute | solution.py:94
  99.8 0.7 collective-permute-start.14
  100.5 4.8 %collective-permute-done.16.refs_4_ = bf16[128,1024]{1,0:T(8,128)(2,1)S(1)} collective-permute-done((bf16[128,1024]{1,0:T(8,128)(2,1)S(1)}, bf16[128,1024]{1,0:T(8,128)(2,1)S(1)}, u32[]{:S(2)}, u32[]{:S(2)}) %collective-permute-start.16) | collective-permute-done | bytes 262176 | tf_op jit(solution)/shard_map/ppermute | solution.py:94
  105.3 1.7 collective-permute-start.18
  107.1 1.8 collective-permute-start.20
  108.8 12.3 %shard_map.112 = bf16[16,64,128]{2,1,0:T(8,128)(2,1)} custom-call(s32[1]{0:T(128)} %bitcast.1.place_ref, bf16[3,64,1024]{2,1,0:T(8,128)(2,1)S(1)} %bitcast.52, bf16[1280,128]{1,0:T(8,128)(2,1)} %get-tuple-element.41.qv_ref, bf16[64,1280]{1,0:T(8,128)(2,1)} %get-tuple-element.42.early_key_ref, bf16[128,1024]{1,0:T(8,128)(2,1)S(1)} %collective-permute-done.14.refs_0_, ...), custom_call_target="tpu_custom_call" | custom-call | flops 4294967296 | bytes 16777216 | tf_op jit(solution)/shard_map/pallas_call | solution.py:366
  121.1 5.2 %all-to-all-start.1 = ((bf16[16,64,128]{2,1,0:T(8,128)(2,1)}), bf16[16,64,128]{2,1,0:T(8,128)(2,1)S(1)}, u32[]{:S(2)}, u32[]{:S(2)}) async-start(bf16[16,64,128]{2,1,0:T(8,128)(2,1)} %shard_map.112), calls=%async_computation.1 | async-start | bytes 524288 | tf_op jit(solution)/shard_map/all_to_all | solution.py:569
  126.3 6.0 %collective-permute-done.19.refs_2_ = bf16[16,32,512]{2,1,0:T(8,128)(2,1)S(1)} collective-permute-done((bf16[16,32,512]{2,1,0:T(8,128)(2,1)S(1)}, bf16[16,32,512]{2,1,0:T(8,128)(2,1)S(1)}, u32[]{:S(2)}, u32[]{:S(2)}) %collective-permute-start.19) | collective-permute-done | bytes 524320 | tf_op jit(solution)/shard_map/ppermute | solution.py:563
  132.3 6.7 %all-to-all-done.1.heads_ref = bf16[16,64,128]{2,1,0:T(8,128)(2,1)S(1)} async-done(((bf16[16,64,128]{2,1,0:T(8,128)(2,1)}), bf16[16,64,128]{2,1,0:T(8,128)(2,1)S(1)}, u32[]{:S(2)}, u32[]{:S(2)}) %all-to-all-start.1) | async-done | bytes 262176 | tf_op jit(solution)/shard_map/all_to_all | solution.py:569
  139.0 1.3 shard_map.113
  140.3 1.4 collective-permute-start.21
  141.8 0.6 collective-permute-start.22
  142.4 1.5 collective-permute-start.23
  143.8 5.7 %collective-permute-done.21.second_ref = bf16[128,1024]{1,0:T(8,128)(2,1)S(1)} collective-permute-done((bf16[128,1024]{1,0:T(8,128)(2,1)S(1)}, bf16[128,1024]{1,0:T(8,128)(2,1)S(1)}, u32[]{:S(2)}, u32[]{:S(2)}) %collective-permute-start.21) | collective-permute-done | bytes 262176 | tf_op jit(solution)/shard_map/ppermute | solution.py:573
  149.5 3.8 %shard_map.114 = (f32[128,1024]{1,0:T(8,128)S(1)}, bf16[128,1024]{1,0:T(8,128)(2,1)S(1)}) custom-call(bf16[128,1024]{1,0:T(8,128)(2,1)S(1)} %get-tuple-element.47.first_ref, bf16[128,1024]{1,0:T(8,128)(2,1)S(1)} %collective-permute-done.21.second_ref, bf16[16,128,1024]{2,1,0:T(8,128)(2,1)} %bitcast.54), custom_call_target="tpu_custom_call" | custom-call | flops 1073741824 | bytes 4194304 | tf_op jit(solution)/shard_map/pallas_call | solution.py:495
  153.3 2.4 %collective-permute-done.22.first_ref = bf16[128,1024]{1,0:T(8,128)(2,1)S(1)} collective-permute-done((bf16[128,1024]{1,0:T(8,128)(2,1)S(1)}, bf16[128,1024]{1,0:T(8,128)(2,1)S(1)}, u32[]{:S(2)}, u32[]{:S(2)}) %collective-permute-start.22) | collective-permute-done | bytes 262176 | tf_op jit(solution)/shard_map/ppermute | solution.py:573
  155.7 3.8 %shard_map.115 = (bf16[128,1024]{1,0:T(8,128)(2,1)S(1)}, bf16[128,1024]{1,0:T(8,128)(2,1)S(1)}) custom-call(bf16[128,1024]{1,0:T(8,128)(2,1)S(1)} %collective-permute-done.22.first_ref, bf16[128,1024]{1,0:T(8,128)(2,1)S(1)} %collective-permute-done.23.second_ref, bf16[16,128,1024]{2,1,0:T(8,128)(2,1)} %bitcast.55), custom_call_target="tpu_custom_call" | custom-call | flops 1073741824 | bytes 4194304 | tf_op jit(solution)/shard_map/pallas_call | solution.py:495
  159.5 0.4 collective-permute-start.25
  159.9 1.7 collective-permute-start.26
  161.6 1.5 collective-permute-start.24
  163.1 9.9 %collective-permute-done.25 = bf16[128,1024]{1,0:T(8,128)(2,1)S(1)} collective-permute-done((bf16[128,1024]{1,0:T(8,128)(2,1)S(1)}, bf16[128,1024]{1,0:T(8,128)(2,1)S(1)}, u32[]{:S(2)}, u32[]{:S(2)}) %collective-permute-start.25) | collective-permute-done | bytes 262176 | tf_op jit(solution)/shard_map/ppermute | solution.py:580
  173.0 1.2 collective-permute-done.24
  174.2 0.9 add_convert_fusion
  (70 shorter events, 1.5 us)
Async XLA Ops:
  6.5 1.0 copy-start
  6.5 4.6 %copy-start.9 = (bf16[4,4,1024]{2,1,0:T(4,128)(2,1)S(1)}, bf16[4,4,1024]{2,1,0:T(4,128)(2,1)}, u32[]{:S(2)}) copy-start(bf16[4,4,1024]{2,1,0:T(4,128)(2,1)} %param.15) | copy-start | bytes 98308
  6.5 49.0 %all-gather.5.cloned.1.call-start = ((), (), s32[]{:S(2)}) async-start(), calls=%async_computation.2 | async-start | bytes 5013504 | tf_op jit(solution)/shard_map/all_gather | solution.py:536
  10.9 8.9 %copy-start.8 = (bf16[1024,256]{1,0:T(8,128)(2,1)S(1)}, bf16[1024,256]{1,0:T(8,128)(2,1)}, u32[]{:S(2)}) copy-start(bf16[1024,256]{1,0:T(8,128)(2,1)} %param.20) | copy-start | bytes 1572868
  12.3 20.5 %all-to-all-start = ((bf16[16,96,256]{2,1,0:T(8,128)(2,1)}), bf16[16,96,256]{2,1,0:T(8,128)(2,1)S(1)}, u32[]{:S(2)}, u32[]{:S(2)}) async-start(bf16[16,96,256]{2,1,0:T(8,128)(2,1)} %bitcast_select_fusion), calls=%async_computation | async-start | bytes 1572864 | tf_op jit(solution)/shard_map/all_to_all | solution.py:50
  19.7 129.8 %all-gather.7.cloned.1.call-start = ((), (), s32[]{:S(2)}) async-start(), calls=%async_computation.3 | async-start | bytes 4456448 | tf_op jit(solution)/shard_map/all_gather | solution.py:567
  20.1 17.1 %copy-start.3 = (bf16[48,256]{1,0:T(8,128)(2,1)S(1)}, bf16[48,256]{1,0:T(8,128)(2,1)}, u32[]{:S(2)}) copy-start(bf16[48,256]{1,0:T(8,128)(2,1)} %refs_4_.1) | copy-start | bytes 73732
  33.2 1.0 copy-start.5
  34.3 6.6 %collective-permute-start = (bf16[48,256]{1,0:T(8,128)(2,1)S(1)}, bf16[48,256]{1,0:T(8,128)(2,1)S(1)}, u32[]{:S(2)}, u32[]{:S(2)}) collective-permute-start(bf16[48,256]{1,0:T(8,128)(2,1)S(1)} %copy.32), channel_id=1, source_target_pairs={{0,1},{1,2},{2,3},{3,4},{4,5},{5,6},{6,7},{7,8},{8,9},{9,10},{10,1... | collective-permute-start | bytes 73736 | tf_op jit(solution)/shard_map/ppermute | solution.py:197
  35.8 3.1 %copy-start.6 = (bf16[2,8,48,256]{2,3,1,0:T(8,128)(2,1)S(1)}, bf16[2,8,48,256]{2,3,1,0:T(8,128)(2,1)}, u32[]{:S(2)}) copy-start(bf16[2,8,48,256]{2,3,1,0:T(8,128)(2,1)} %copy-done.5) | copy-start | bytes 1179652
  35.8 5.4 %collective-permute-start.1 = (bf16[48,256]{1,0:T(8,128)(2,1)S(1)}, bf16[48,256]{1,0:T(8,128)(2,1)S(1)}, u32[]{:S(2)}, u32[]{:S(2)}) collective-permute-start(bf16[48,256]{1,0:T(8,128)(2,1)S(1)} %copy.33), channel_id=1, source_target_pairs={{1,0},{2,1},{3,2},{4,3},{5,4},{6,5},{7,6},{8,7},{9,8},{10,9},{11,1... | collective-permute-start | bytes 73736 | tf_op jit(solution)/shard_map/ppermute | solution.py:198
  41.1 1.6 copy-start.1
  58.9 5.5 %copy-start.10 = (f32[1024]{0:T(1024)S(1)}, f32[1024]{0:T(1024)}, u32[]{:S(2)}) copy-start(f32[1024]{0:T(1024)} %param.16) | copy-start | bytes 12292
  58.9 31.6 %copy-start.2 = (bf16[3,1024,64]{1,2,0:T(8,128)(2,1)S(1)}, bf16[3,1024,64]{1,2,0:T(8,128)(2,1)}, u32[]{:S(2)}) copy-start(bf16[3,1024,64]{1,2,0:T(8,128)(2,1)} %param.17) | copy-start | bytes 1179652
  58.9 5.1 %collective-permute-start.2 = (bf16[128,512]{1,0:T(8,128)(2,1)S(1)}, bf16[128,512]{1,0:T(8,128)(2,1)S(1)}, u32[]{:S(2)}, u32[]{:S(2)}) collective-permute-start(bf16[128,512]{1,0:T(8,128)(2,1)S(1)} %get-tuple-element.33), channel_id=1, source_target_pairs={{0,16},{16,0},{32,48},{48,32},{64,80},{80,64},{96,112},{112,96},{1... | collective-permute-start | bytes 393224 | tf_op jit(solution)/shard_map/ppermute | solution.py:555
  64.6 13.1 %collective-permute-start.3 = (bf16[128,1024]{1,0:T(8,128)(2,1)S(1)}, bf16[128,1024]{1,0:T(8,128)(2,1)S(1)}, u32[]{:S(2)}, u32[]{:S(2)}) collective-permute-start(bf16[128,1024]{1,0:T(8,128)(2,1)S(1)} %fusion.4.refs_0_), channel_id=1, source_target_pairs={{0,2},{1,3},{2,4},{3,5},{4,6},{5,7},{6,8},{7,9},{8,10},{9,11},{10,... | collective-permute-start | bytes 786440 | tf_op jit(solution)/shard_map/ppermute | solution.py:64
  70.3 8.0 %collective-permute-start.5 = (bf16[128,1024]{1,0:T(8,128)(2,1)S(1)}, bf16[128,1024]{1,0:T(8,128)(2,1)S(1)}, u32[]{:S(2)}, u32[]{:S(2)}) collective-permute-start(bf16[128,1024]{1,0:T(8,128)(2,1)S(1)} %fusion.4.refs_0_), channel_id=1, source_target_pairs={{0,14},{1,15},{2,0},{3,1},{4,2},{5,3},{6,4},{7,5},{8,6},{9,7},{10,... | collective-permute-start | bytes 786440 | tf_op jit(solution)/shard_map/ppermute | solution.py:64
  77.8 7.6 %collective-permute-start.4 = (bf16[128,1024]{1,0:T(8,128)(2,1)S(1)}, bf16[128,1024]{1,0:T(8,128)(2,1)S(1)}, u32[]{:S(2)}, u32[]{:S(2)}) collective-permute-start(bf16[128,1024]{1,0:T(8,128)(2,1)S(1)} %collective-permute-done.3.refs_4_), channel_id=1, source_target_pairs={{0,2},{1,3},{2,4},{3,5},{4,6},{5,7},{6,8},{7,9},{8,10},{9,11},{10,... | collective-permute-start | bytes 786440 | tf_op jit(solution)/shard_map/ppermute | solution.py:64
  78.3 9.0 %collective-permute-start.6 = (bf16[128,1024]{1,0:T(8,128)(2,1)S(1)}, bf16[128,1024]{1,0:T(8,128)(2,1)S(1)}, u32[]{:S(2)}, u32[]{:S(2)}) collective-permute-start(bf16[128,1024]{1,0:T(8,128)(2,1)S(1)} %collective-permute-done.5.refs_5_), channel_id=1, source_target_pairs={{0,14},{1,15},{2,0},{3,1},{4,2},{5,3},{6,4},{7,5},{8,6},{9,7},{10,... | collective-permute-start | bytes 786440 | tf_op jit(solution)/shard_map/ppermute | solution.py:64
  81.1 6.2 %collective-permute-start.9 = (bf16[128,1024]{1,0:T(8,128)(2,1)S(1)}, bf16[128,1024]{1,0:T(8,128)(2,1)S(1)}, u32[]{:S(2)}, u32[]{:S(2)}) collective-permute-start(bf16[128,1024]{1,0:T(8,128)(2,1)S(1)} %fusion.4.refs_0_), channel_id=1, source_target_pairs={{0,1},{1,0},{2,3},{3,2},{4,5},{5,4},{6,7},{7,6},{8,9},{9,8},{10,11... | collective-permute-start | bytes 786440 | tf_op jit(solution)/shard_map/ppermute | solution.py:68
  81.1 7.9 %collective-permute-start.10 = (bf16[128,1024]{1,0:T(8,128)(2,1)S(1)}, bf16[128,1024]{1,0:T(8,128)(2,1)S(1)}, u32[]{:S(2)}, u32[]{:S(2)}) collective-permute-start(bf16[128,1024]{1,0:T(8,128)(2,1)S(1)} %collective-permute-done.3.refs_4_), channel_id=1, source_target_pairs={{0,1},{1,0},{2,3},{3,2},{4,5},{5,4},{6,7},{7,6},{8,9},{9,8},{10,11... | collective-permute-start | bytes 786440 | tf_op jit(solution)/shard_map/ppermute | solution.py:68
  81.6 8.9 %collective-permute-start.11 = (bf16[128,1024]{1,0:T(8,128)(2,1)S(1)}, bf16[128,1024]{1,0:T(8,128)(2,1)S(1)}, u32[]{:S(2)}, u32[]{:S(2)}) collective-permute-start(bf16[128,1024]{1,0:T(8,128)(2,1)S(1)} %collective-permute-done.5.refs_5_), channel_id=1, source_target_pairs={{0,1},{1,0},{2,3},{3,2},{4,5},{5,4},{6,7},{7,6},{8,9},{9,8},{10,11... | collective-permute-start | bytes 786440 | tf_op jit(solution)/shard_map/ppermute | solution.py:68
  85.4 5.2 %collective-permute-start.12 = (bf16[128,1024]{1,0:T(8,128)(2,1)S(1)}, bf16[128,1024]{1,0:T(8,128)(2,1)S(1)}, u32[]{:S(2)}, u32[]{:S(2)}) collective-permute-start(bf16[128,1024]{1,0:T(8,128)(2,1)S(1)} %collective-permute-done.4.refs_8_), channel_id=1, source_target_pairs={{0,1},{1,0},{2,3},{3,2},{4,5},{5,4},{6,7},{7,6},{8,9},{9,8},{10,11... | collective-permute-start | bytes 786440 | tf_op jit(solution)/shard_map/ppermute | solution.py:68
  87.3 3.3 %collective-permute-start.13 = (bf16[128,1024]{1,0:T(8,128)(2,1)S(1)}, bf16[128,1024]{1,0:T(8,128)(2,1)S(1)}, u32[]{:S(2)}, u32[]{:S(2)}) collective-permute-start(bf16[128,1024]{1,0:T(8,128)(2,1)S(1)} %collective-permute-done.6.refs_9_), channel_id=1, source_target_pairs={{0,1},{1,0},{2,3},{3,2},{4,5},{5,4},{6,7},{7,6},{8,9},{9,8},{10,11... | collective-permute-start | bytes 786440 | tf_op jit(solution)/shard_map/ppermute | solution.py:68
  87.3 9.9 %collective-permute-start.7 = (bf16[128,1024]{1,0:T(8,128)(2,1)S(1)}, bf16[128,1024]{1,0:T(8,128)(2,1)S(1)}, u32[]{:S(2)}, u32[]{:S(2)}) collective-permute-start(bf16[128,1024]{1,0:T(8,128)(2,1)S(1)} %collective-permute-done.4.refs_8_), channel_id=1, source_target_pairs={{0,2},{1,3},{2,4},{3,5},{4,6},{5,7},{6,8},{7,9},{8,10},{9,11},{10,... | collective-permute-start | bytes 786440 | tf_op jit(solution)/shard_map/ppermute | solution.py:64
  89.0 8.5 %collective-permute-start.8 = (bf16[128,1024]{1,0:T(8,128)(2,1)S(1)}, bf16[128,1024]{1,0:T(8,128)(2,1)}, u32[]{:S(2)}, u32[]{:S(2)}) collective-permute-start(bf16[128,1024]{1,0:T(8,128)(2,1)S(1)} %collective-permute-done.6.refs_9_), channel_id=1, source_target_pairs={{0,14},{1,15},{2,0},{3,1},{4,2},{5,3},{6,4},{7,5},{8,6},{9,7},{10,... | collective-permute-start | bytes 786440 | tf_op jit(solution)/shard_map/ppermute | solution.py:64
  97.7 7.7 %collective-permute-start.16 = (bf16[128,1024]{1,0:T(8,128)(2,1)S(1)}, bf16[128,1024]{1,0:T(8,128)(2,1)S(1)}, u32[]{:S(2)}, u32[]{:S(2)}) collective-permute-start(bf16[128,1024]{1,0:T(8,128)(2,1)S(1)} %broadcast_select_fusion), channel_id=1, source_target_pairs={{0,2},{1,15},{2,4},{3,1},{4,6},{5,3},{6,8},{7,5},{8,10},{9,7},{10,... | collective-permute-start | bytes 786440 | tf_op jit(solution)/shard_map/ppermute | solution.py:94
  99.8 7.2 %collective-permute-start.14 = (bf16[128,1024]{1,0:T(8,128)(2,1)S(1)}, bf16[128,1024]{1,0:T(8,128)(2,1)S(1)}, u32[]{:S(2)}, u32[]{:S(2)}) collective-permute-start(bf16[128,1024]{1,0:T(8,128)(2,1)S(1)} %collective-permute-done.7.refs_2_), channel_id=1, source_target_pairs={{0,1},{1,0},{2,3},{3,2},{4,5},{5,4},{6,7},{7,6},{8,9},{9,8},{10,11... | collective-permute-start | bytes 786440 | tf_op jit(solution)/shard_map/ppermute | solution.py:68
  100.5 8.3 %collective-permute-start.15 = (bf16[128,1024]{1,0:T(8,128)(2,1)}, bf16[128,1024]{1,0:T(8,128)(2,1)S(1)}, u32[]{:S(2)}, u32[]{:S(2)}) collective-permute-start(bf16[128,1024]{1,0:T(8,128)(2,1)} %collective-permute-done.8.refs_3_), channel_id=1, source_target_pairs={{0,1},{1,0},{2,3},{3,2},{4,5},{5,4},{6,7},{7,6},{8,9},{9,8},{10,11... | collective-permute-start | bytes 786440 | tf_op jit(solution)/shard_map/ppermute | solution.py:68
  105.3 3.5 %collective-permute-start.17 = (bf16[128,1024]{1,0:T(8,128)(2,1)S(1)}, bf16[128,1024]{1,0:T(8,128)(2,1)S(1)}, u32[]{:S(2)}, u32[]{:S(2)}) collective-permute-start(bf16[128,1024]{1,0:T(8,128)(2,1)S(1)} %collective-permute-done.16.refs_4_), channel_id=1, source_target_pairs={{0,1},{1,0},{2,3},{3,2},{4,5},{5,4},{6,7},{7,6},{8,9},{9,8},{10,11... | collective-permute-start | bytes 786440 | tf_op jit(solution)/shard_map/ppermute | solution.py:68
  105.3 21.0 %collective-permute-start.18 = (bf16[16,32,512]{2,1,0:T(8,128)(2,1)S(1)}, bf16[16,32,512]{2,1,0:T(8,128)(2,1)S(1)}, u32[]{:S(2)}, u32[]{:S(2)}) collective-permute-start(bf16[16,32,512]{2,1,0:T(8,128)(2,1)S(1)} %slice.28.refs_0_), channel_id=1, source_target_pairs={{0,16},{16,0},{32,48},{48,32},{64,80},{80,64},{96,112},{112,96},{1... | collective-permute-start | bytes 1572872 | tf_op jit(solution)/shard_map/ppermute | solution.py:563
  107.0 25.3 %collective-permute-start.19 = (bf16[16,32,512]{2,1,0:T(8,128)(2,1)S(1)}, bf16[16,32,512]{2,1,0:T(8,128)(2,1)S(1)}, u32[]{:S(2)}, u32[]{:S(2)}) collective-permute-start(bf16[16,32,512]{2,1,0:T(8,128)(2,1)S(1)} %slice.28.refs_0_), channel_id=1, source_target_pairs={{0,32},{16,48},{32,0},{48,16},{64,96},{80,112},{96,64},{112,80},{1... | collective-permute-start | bytes 1572872 | tf_op jit(solution)/shard_map/ppermute | solution.py:563
  107.1 25.3 %collective-permute-start.20 = (bf16[16,32,512]{2,1,0:T(8,128)(2,1)S(1)}, bf16[16,32,512]{2,1,0:T(8,128)(2,1)S(1)}, u32[]{:S(2)}, u32[]{:S(2)}) collective-permute-start(bf16[16,32,512]{2,1,0:T(8,128)(2,1)S(1)} %slice.28.refs_0_), channel_id=1, source_target_pairs={{0,48},{16,32},{32,16},{48,0},{64,112},{80,96},{96,80},{112,64},{1... | collective-permute-start | bytes 1572872 | tf_op jit(solution)/shard_map/ppermute | solution.py:563
  108.8 30.2 %copy-start.4 = (f32[1024]{0:T(1024)S(1)}, f32[1024]{0:T(1024)}, u32[]{:S(2)}) copy-start(f32[1024]{0:T(1024)} %param.19) | copy-start | bytes 12292
  121.1 17.9 %all-to-all-start.1 = ((bf16[16,64,128]{2,1,0:T(8,128)(2,1)}), bf16[16,64,128]{2,1,0:T(8,128)(2,1)S(1)}, u32[]{:S(2)}, u32[]{:S(2)}) async-start(bf16[16,64,128]{2,1,0:T(8,128)(2,1)} %shard_map.112), calls=%async_computation.1 | async-start | bytes 524288 | tf_op jit(solution)/shard_map/all_to_all | solution.py:569
  140.3 9.2 %collective-permute-start.21 = (bf16[128,1024]{1,0:T(8,128)(2,1)S(1)}, bf16[128,1024]{1,0:T(8,128)(2,1)S(1)}, u32[]{:S(2)}, u32[]{:S(2)}) collective-permute-start(bf16[128,1024]{1,0:T(8,128)(2,1)S(1)} %get-tuple-element.47.first_ref), channel_id=1, source_target_pairs={{0,16},{16,0},{32,48},{48,32},{64,80},{80,64},{96,112},{112,96},{1... | collective-permute-start | bytes 786440 | tf_op jit(solution)/shard_map/ppermute | solution.py:573
  141.8 13.9 %collective-permute-start.22 = (bf16[128,1024]{1,0:T(8,128)(2,1)S(1)}, bf16[128,1024]{1,0:T(8,128)(2,1)S(1)}, u32[]{:S(2)}, u32[]{:S(2)}) collective-permute-start(bf16[128,1024]{1,0:T(8,128)(2,1)S(1)} %get-tuple-element.47.first_ref), channel_id=1, source_target_pairs={{0,32},{16,48},{32,0},{48,16},{64,96},{80,112},{96,64},{112,80},{1... | collective-permute-start | bytes 786440 | tf_op jit(solution)/shard_map/ppermute | solution.py:573
  142.4 13.3 %collective-permute-start.23 = (bf16[128,1024]{1,0:T(8,128)(2,1)S(1)}, bf16[128,1024]{1,0:T(8,128)(2,1)S(1)}, u32[]{:S(2)}, u32[]{:S(2)}) collective-permute-start(bf16[128,1024]{1,0:T(8,128)(2,1)S(1)} %get-tuple-element.47.first_ref), channel_id=1, source_target_pairs={{0,48},{16,32},{32,16},{48,0},{64,112},{80,96},{96,80},{112,64},{1... | collective-permute-start | bytes 786440 | tf_op jit(solution)/shard_map/ppermute | solution.py:573
  155.7 18.5 %copy-start.7 = (f32[128,1024]{1,0:T(8,128)S(1)}, f32[128,1024]{1,0:T(8,128)}, u32[]{:S(2)}) copy-start(f32[128,1024]{1,0:T(8,128)} %get-tuple-element.46) | copy-start | bytes 1572868
  159.5 13.5 %collective-permute-start.25 = (bf16[128,1024]{1,0:T(8,128)(2,1)S(1)}, bf16[128,1024]{1,0:T(8,128)(2,1)S(1)}, u32[]{:S(2)}, u32[]{:S(2)}) collective-permute-start(bf16[128,1024]{1,0:T(8,128)(2,1)S(1)} %get-tuple-element.55), channel_id=1, source_target_pairs={{0,32},{16,48},{32,0},{48,16},{64,96},{80,112},{96,64},{112,80},{1... | collective-permute-start | bytes 786440 | tf_op jit(solution)/shard_map/ppermute | solution.py:580
  159.9 13.1 %collective-permute-start.26 = (bf16[128,1024]{1,0:T(8,128)(2,1)S(1)}, bf16[128,1024]{1,0:T(8,128)(2,1)S(1)}, u32[]{:S(2)}, u32[]{:S(2)}) collective-permute-start(bf16[128,1024]{1,0:T(8,128)(2,1)S(1)} %get-tuple-element.56), channel_id=1, source_target_pairs={{0,48},{16,32},{32,16},{48,0},{64,112},{80,96},{96,80},{112,64},{1... | collective-permute-start | bytes 786440 | tf_op jit(solution)/shard_map/ppermute | solution.py:580
  161.6 12.7 %collective-permute-start.24 = (bf16[128,1024]{1,0:T(8,128)(2,1)S(1)}, bf16[128,1024]{1,0:T(8,128)(2,1)S(1)}, u32[]{:S(2)}, u32[]{:S(2)}) collective-permute-start(bf16[128,1024]{1,0:T(8,128)(2,1)S(1)} %get-tuple-element.52), channel_id=1, source_target_pairs={{0,16},{16,0},{32,48},{48,32},{64,80},{80,64},{96,112},{112,96},{1... | collective-permute-start | bytes 786440 | tf_op jit(solution)/shard_map/ppermute | solution.py:576
Sparse Core Ops, SparseCore 0:
  9.2 45.4 all-gather.4
  97.7 44.5 all-gather.6
